TPU v7x, 768 devices: a whole 4x8x12 slice. The times are simulated.
768 devices in a mesh: gx: 48 (over z_hi, y, core), gy: 4 (over x), gz: 4 (over z_lo).
Axes of the slice: x: 4, y: 8, z: 12 (z_hi: 3, z_lo: 4; z = z_hi * 4 + z_lo), core: 2. Of those that a mesh axis runs over, the one named last changes fastest.
Arguments:
- thermal_state: float32 [384, 32, 512], P('gx', 'gy', 'gz'), may hold values from 0.5 to 1.5
- diffusivity: float32 [384, 32, 512], P('gx', 'gy', 'gz'), may hold values from 1.1 to 13.2
- staggered_flux_density: float32 [3, 384, 32, 512], P(None, 'gx', 'gy', 'gz'), may hold values from -6 to 6
- bulk_motion: float32 [3, 384, 32, 512], P(None, 'gx', 'gy', 'gz'), may hold values from -3 to 3
- mass_per_volume: float32 [384, 32, 512], P('gx', 'gy', 'gz'), may hold values from 0.5 to 2
Outputs:
- temperature_out: float32 [384, 32, 512], P('gx', 'gy', 'gz')
- face_field_out: float32 [3, 384, 32, 512], P(None, 'gx', 'gy', 'gz')
All inputs are finite; a program needn't handle non-finite values.
Results may differ from a plain program's by a relative error of at most 0.00002.
Values sent between devices are 32-bit elements; how exact they have to be, the bound alone decides.
No kernel may reach another device: no remote copies, remote signals or barrier semaphores. Data moves between devices by JAX's collectives and lax.ppermute only.
A program may use at most 128 MiB of HBM per device.

v0:
```python
import jax
import jax.numpy as jnp
from jax import lax
from jax.sharding import Mesh
from jax.sharding import PartitionSpec as P

SECTIONS = 8
GX_GY_GZ = ("gx_0", "gx_1", "gx_2", "gy", "gz")
GX = ("gx_0", "gx_1", "gx_2")


GAMMA = 5.0 / 3.0
FACE_FLOOR = 0.25
REFERENCE_SPOT = (0, 0, 0)


def extended(block, sides, width):
    for axis, dim in sides:
        count = lax.axis_size(axis)
        forward = [(i, i + 1) for i in range(count - 1)]
        forward.append((count - 1, 0))
        backward = [(target, source) for source, target in forward]
        low = lax.ppermute(
            lax.slice_in_dim(block, block.shape[dim] - width, None, axis=dim), axis, forward
        )
        high = lax.ppermute(lax.slice_in_dim(block, 0, width, axis=dim), axis, backward)
        block = jnp.concatenate([low, block, high], axis=dim)
    return block


def by_axis(x, axes):
    for axis in axes:
        x = lax.pmin(x, axis)
    return x


def unit_step(direction, amount):
    return tuple((amount if candidate == direction else 0 for candidate in range(3)))


def combine_steps(left_step, right_step):
    return tuple(
        map(lambda first_part, second_part: first_part + second_part, left_step, right_step)
    )


def even_reach(amount):
    return (amount, amount, amount)


def sites_placed(source, ghost_layer_sites, offset, low_side, high_side):
    extents = source.shape[-3:]
    selector = [slice(None)] * (source.ndim - 3)
    for direction in range(3):
        interior = extents[direction] - 2 * ghost_layer_sites
        begin_at = ghost_layer_sites - low_side[direction] + offset[direction]
        selector.append(
            slice(begin_at, begin_at + interior + low_side[direction] + high_side[direction])
        )
    return source[tuple(selector)]


def trim_extent(source, ghost_layer_sites, amount):
    return sites_placed(
        source, ghost_layer_sites, REFERENCE_SPOT, even_reach(amount), even_reach(amount)
    )


def face_coefficients(diffusion_coefficient, interface_quantities, ghost_layer_sites, reach):
    interior_block = even_reach(reach)
    lookup_arrays = []
    for normal in range(3):
        backward = unit_step(normal, -1)
        kappa_face = 0.5 * (
            sites_placed(
                diffusion_coefficient,
                ghost_layer_sites,
                REFERENCE_SPOT,
                interior_block,
                interior_block,
            )
            + sites_placed(
                diffusion_coefficient, ghost_layer_sites, backward, interior_block, interior_block
            )
        )
        normal_part = sites_placed(
            interface_quantities[normal],
            ghost_layer_sites,
            REFERENCE_SPOT,
            interior_block,
            interior_block,
        )
        across = []
        for rotation in (1, 2):
            other_axis = (normal + rotation) % 3
            forward = unit_step(other_axis, 1)
            across.append(
                0.25
                * (
                    sites_placed(
                        interface_quantities[other_axis],
                        ghost_layer_sites,
                        REFERENCE_SPOT,
                        interior_block,
                        interior_block,
                    )
                    + sites_placed(
                        interface_quantities[other_axis],
                        ghost_layer_sites,
                        forward,
                        interior_block,
                        interior_block,
                    )
                    + sites_placed(
                        interface_quantities[other_axis],
                        ghost_layer_sites,
                        backward,
                        interior_block,
                        interior_block,
                    )
                    + sites_placed(
                        interface_quantities[other_axis],
                        ghost_layer_sites,
                        combine_steps(backward, forward),
                        interior_block,
                        interior_block,
                    )
                )
            )
        squared = normal_part * normal_part + across[0] * across[0] + across[1] * across[1]
        scaling = kappa_face / jnp.maximum(squared, FACE_FLOOR)
        lookup_arrays.append(
            (
                scaling * normal_part * normal_part,
                scaling * normal_part * across[0],
                scaling * normal_part * across[1],
            )
        )
    return lookup_arrays


def diffuse_thermal(profile, ghost_layer_sites, lookup_arrays, reach, target):
    interior_block = even_reach(target)
    balance = None
    for normal in range(3):
        upper_side = tuple((target + (1 if candidate == normal else 0) for candidate in range(3)))
        backward = unit_step(normal, -1)

        def shifted(offset):
            return sites_placed(profile, ghost_layer_sites, offset, interior_block, upper_side)

        slopes = []
        for rotation in (1, 2):
            other_axis = (normal + rotation) % 3
            forward = unit_step(other_axis, 1)
            rearward = unit_step(other_axis, -1)
            slopes.append(
                0.25
                * (
                    shifted(forward)
                    - shifted(rearward)
                    + shifted(combine_steps(backward, forward))
                    - shifted(combine_steps(backward, rearward))
                )
            )
        along_normal, along_first, along_second = [
            sites_placed(coefficient, reach, REFERENCE_SPOT, interior_block, upper_side)
            for coefficient in lookup_arrays[normal]
        ]
        face_flux = -(
            along_normal * (shifted(REFERENCE_SPOT) - shifted(backward))
            + along_first * slopes[0]
            + along_second * slopes[1]
        )
        length = face_flux.shape[normal]
        change = lax.slice_in_dim(face_flux, 1, length, axis=normal) - lax.slice_in_dim(
            face_flux, 0, length - 1, axis=normal
        )
        balance = -change if balance is None else balance - change
    return balance


def section_weights(total):
    first_rate = 4.0 / (total * total + total - 2)
    factors = [1.0 / 3.0, 1.0 / 3.0, 1.0 / 3.0]
    for ordinal in range(3, total + 1):
        factors.append((ordinal * ordinal + ordinal - 2) / (2.0 * ordinal * (ordinal + 1)))
    layout_recipe = [None, factors[1] * first_rate]
    for ordinal in range(2, total + 1):
        weight_prev = (2.0 * ordinal - 1.0) / ordinal * factors[ordinal] / factors[ordinal - 1]
        weight_older = -(ordinal - 1.0) / ordinal * factors[ordinal] / factors[ordinal - 2]
        rate_prev = weight_prev * first_rate
        rate_zero = -(1.0 - factors[ordinal - 1]) * rate_prev
        layout_recipe.append(
            (weight_prev, weight_older, 1.0 - weight_prev - weight_older, rate_prev, rate_zero)
        )
    return layout_recipe


def subdivision_advance(
    weights,
    interval_increment,
    newest_iterate,
    newest_extended,
    previous_iterate,
    previous_extended,
    initial,
    initial_margin,
    initial_derivative,
    zero_margin,
    lookup_arrays,
    reach,
):
    target = newest_extended - 1
    weight_prev, weight_older, weight_zero, rate_prev, rate_zero = weights
    prev_rate = diffuse_thermal(newest_iterate, newest_extended, lookup_arrays, reach, target)
    return (
        weight_prev * trim_extent(newest_iterate, newest_extended, target)
        + weight_older * trim_extent(previous_iterate, previous_extended, target)
        + weight_zero * trim_extent(initial, initial_margin, target)
        + rate_prev * interval_increment * prev_rate
        + rate_zero * interval_increment * trim_extent(initial_derivative, zero_margin, target)
    )


def fastest_characteristic(
    thermal_state, mass_per_volume, interface_quantities, bulk_motion, ghost_layer_sites
):
    interior_block = even_reach(1)
    centred = []
    for direction in range(3):
        centred.append(
            0.5
            * (
                sites_placed(
                    interface_quantities[direction],
                    ghost_layer_sites,
                    REFERENCE_SPOT,
                    interior_block,
                    interior_block,
                )
                + sites_placed(
                    interface_quantities[direction],
                    ghost_layer_sites,
                    unit_step(direction, 1),
                    interior_block,
                    interior_block,
                )
            )
        )
    moving = [
        sites_placed(
            bulk_motion[direction],
            ghost_layer_sites,
            REFERENCE_SPOT,
            interior_block,
            interior_block,
        )
        for direction in range(3)
    ]
    field_square = centred[0] * centred[0] + centred[1] * centred[1] + centred[2] * centred[2]
    flow_speed = jnp.sqrt(moving[0] * moving[0] + moving[1] * moving[1] + moving[2] * moving[2])
    thermal_energy = sites_placed(
        thermal_state, ghost_layer_sites, REFERENCE_SPOT, interior_block, interior_block
    )
    inertia = sites_placed(
        mass_per_volume, ghost_layer_sites, REFERENCE_SPOT, interior_block, interior_block
    )
    return flow_speed + jnp.sqrt(GAMMA * thermal_energy + field_square / inertia)


def edge_fields(
    interface_quantities, face_margin, bulk_motion, ghost_layer_sites, propagation_rate
):
    low_side = REFERENCE_SPOT
    high_side = (1, 1, 1)
    fields_out = []
    for edge_axis in range(3):
        first_axis = (edge_axis + 1) % 3
        second_axis = (edge_axis + 2) % 3
        back_first = unit_step(first_axis, -1)
        back_second = unit_step(second_axis, -1)
        back_both = combine_steps(back_first, back_second)

        def corner_mean(source, source_margin):
            return 0.25 * (
                sites_placed(source, source_margin, REFERENCE_SPOT, low_side, high_side)
                + sites_placed(source, source_margin, back_first, low_side, high_side)
                + sites_placed(source, source_margin, back_second, low_side, high_side)
                + sites_placed(source, source_margin, back_both, low_side, high_side)
            )

        mean_first = corner_mean(bulk_motion[first_axis], ghost_layer_sites)
        mean_second = corner_mean(bulk_motion[second_axis], ghost_layer_sites)
        mean_speed = corner_mean(propagation_rate, 1)
        first_here = sites_placed(
            interface_quantities[first_axis], face_margin, REFERENCE_SPOT, low_side, high_side
        )
        first_below = sites_placed(
            interface_quantities[first_axis], face_margin, back_second, low_side, high_side
        )
        second_here = sites_placed(
            interface_quantities[second_axis], face_margin, REFERENCE_SPOT, low_side, high_side
        )
        second_below = sites_placed(
            interface_quantities[second_axis], face_margin, back_first, low_side, high_side
        )
        fields_out.append(
            mean_second * (0.5 * (first_here + first_below))
            - mean_first * (0.5 * (second_here + second_below))
            + 0.5 * mean_speed * (second_here - second_below)
            - 0.5 * mean_speed * (first_here - first_below)
        )
    return fields_out


def edge_cells(source, offset):
    return source[
        tuple(
            (
                slice(offset[candidate], offset[candidate] + source.shape[candidate] - 1)
                for candidate in range(3)
            )
        )
    ]


def faraday(interface_quantities, face_margin, edges, interval_increment):
    renewed_result = []
    for normal in range(3):
        next_axis = (normal + 1) % 3
        last_axis = (normal + 2) % 3
        curl_part = (
            edge_cells(edges[last_axis], unit_step(next_axis, 1))
            - edge_cells(edges[last_axis], REFERENCE_SPOT)
            - (
                edge_cells(edges[next_axis], unit_step(last_axis, 1))
                - edge_cells(edges[next_axis], REFERENCE_SPOT)
            )
        )
        renewed_result.append(
            trim_extent(interface_quantities[normal], face_margin, 0)
            - interval_increment * curl_part
        )
    return jnp.stack(renewed_result)


def refresh_section(newest_iterate, subdivision_width):
    return extended(newest_iterate, ((GX, 0), ("gy", 1), ("gz", 2)), subdivision_width)


def on_device(thermal_state, diffusivity, staggered_flux_density, bulk_motion, mass_per_volume):
    subdivision_width = 2
    ghost_width = subdivision_width + 1
    bundle = jnp.concatenate(
        [
            thermal_state[None],
            diffusivity[None],
            staggered_flux_density,
            bulk_motion,
            mass_per_volume[None],
        ],
        axis=0,
    )
    extended_array = extended(bundle, ((GX, 1), ("gy", 2), ("gz", 3)), ghost_width)
    thermal_state_extended = extended_array[0]
    diffusivity_extended = extended_array[1]
    staggered_extended = extended_array[2:5]
    velocity_extended = extended_array[5:8]
    mass_per_volume_extended = extended_array[8]
    diffusion_coefficient = diffusivity_extended * jnp.power(thermal_state_extended, 2.5)
    limit_scale = (SECTIONS * SECTIONS + SECTIONS - 2) / 16.0
    local_step = jnp.min(limit_scale / trim_extent(diffusion_coefficient, ghost_width, 0))
    interval_increment = by_axis(local_step, GX_GY_GZ)
    propagation_rate = fastest_characteristic(
        thermal_state_extended,
        mass_per_volume_extended,
        staggered_extended,
        velocity_extended,
        ghost_width,
    )
    edges_now = edge_fields(
        staggered_extended, ghost_width, velocity_extended, ghost_width, propagation_rate
    )
    faces_mid = faraday(staggered_extended, ghost_width, edges_now, interval_increment)
    faces_mid_pad = faces_mid
    mid_margin = 0
    lookup_arrays = face_coefficients(
        diffusion_coefficient, staggered_extended, ghost_width, subdivision_width
    )
    initial_derivative = diffuse_thermal(
        thermal_state_extended, ghost_width, lookup_arrays, subdivision_width, subdivision_width - 1
    )
    layout_recipe = section_weights(SECTIONS)
    previous_iterate, previous_extended = (thermal_state_extended, ghost_width)
    newest_iterate = (
        trim_extent(thermal_state_extended, ghost_width, subdivision_width - 1)
        + layout_recipe[1] * interval_increment * initial_derivative
    )
    newest_extended = subdivision_width - 1
    for subdivision_number in range(2, SECTIONS + 1):
        if newest_extended == 0:
            if subdivision_number == subdivision_width + 1:
                carried = jnp.concatenate([newest_iterate[None], faces_mid], axis=0)
                received = extended(carried, ((GX, 1), ("gy", 2), ("gz", 3)), subdivision_width)
                newest_iterate = received[0]
                faces_mid_pad = received[1:4]
                mid_margin = subdivision_width
            else:
                newest_iterate = refresh_section(newest_iterate, subdivision_width)
            newest_extended = subdivision_width
        renewed_result = subdivision_advance(
            layout_recipe[subdivision_number],
            interval_increment,
            newest_iterate,
            newest_extended,
            previous_iterate,
            previous_extended,
            thermal_state_extended,
            ghost_width,
            initial_derivative,
            subdivision_width - 1,
            lookup_arrays,
            subdivision_width,
        )
        previous_iterate, previous_extended = (newest_iterate, newest_extended)
        newest_iterate, newest_extended = (renewed_result, newest_extended - 1)
    edges_mid = edge_fields(
        faces_mid_pad, mid_margin, velocity_extended, ghost_width, propagation_rate
    )
    faces_end = faraday(faces_mid_pad, mid_margin, edges_mid, interval_increment)
    face_out = 0.5 * (trim_extent(staggered_extended, ghost_width, 0) + faces_end)
    return (newest_iterate, face_out)


def solution(mesh):
    finer = Mesh(
        mesh.devices.reshape(3, 8, 2, mesh.shape["gy"], mesh.shape["gz"]),
        ("gx_0", "gx_1", "gx_2", "gy", "gz"),
    )
    in_specs = (
        P(GX, "gy", "gz"),
        P(GX, "gy", "gz"),
        P(None, GX, "gy", "gz"),
        P(None, GX, "gy", "gz"),
        P(GX, "gy", "gz"),
    )
    out_specs = (P(GX, "gy", "gz"), P(None, GX, "gy", "gz"))
    return jax.shard_map(
        on_device, mesh=finer, in_specs=in_specs, out_specs=out_specs, check_vma=False
    )
```

profile of v0, /device:TPU:57, one launch (start us, length us, event | category | flops | bytes accessed | tf_op | source)
XLA Modules:
  0.0 278.5 jit_solution(12630819468269088173)
XLA Ops:
  4.7 10.4 %collective-permute-start = (f32[9,3,8,128]{3,2,1,0:T(8,128)S(1)}, f32[9,3,8,128]{3,2,1,0:T(8,128)S(1)}, u32[]{:S(2)}, u32[]{:S(2)}) collective-permute-start(f32[9,3,8,128]{3,2,1,0:T(8,128)S(1)} %get-tuple-element.48), channel_id=1, source_target_pairs={{0,16},{16,32},{32,48},{48,64},{64,80},{80,96},{96,112},{112,128},... | collective-permute-start | bytes 331784 | tf_op jit(solution)/shard_map/ppermute | solution.py:23
  15.1 1.9 collective-permute-start.1
  17.1 10.3 %collective-permute-done.1 = f32[9,3,8,128]{3,2,1,0:T(8,128)S(1)} collective-permute-done((f32[9,3,8,128]{3,2,1,0:T(8,128)S(1)}, f32[9,3,8,128]{3,2,1,0:T(8,128)S(1)}, u32[]{:S(2)}, u32[]{:S(2)}) %collective-permute-start.1) | collective-permute-done | bytes 110624 | tf_op jit(solution)/shard_map/ppermute | solution.py:26
  27.5 3.1 %collective-permute-start.2 = (f32[9,14,3,128]{3,1,2,0:T(8,128)S(1)}, f32[9,14,3,128]{3,1,2,0:T(8,128)S(1)}, u32[]{:S(2)}, u32[]{:S(2)}) collective-permute-start(f32[9,14,3,128]{3,1,2,0:T(8,128)S(1)} %copy.45), channel_id=1, source_target_pairs={{0,4},{4,8},{8,12},{12,0},{1,5},{5,9},{9,13},{13,1},{2,6},{6,10},{... | collective-permute-start | bytes 580616 | tf_op jit(solution)/shard_map/ppermute | solution.py:23
  30.7 3.4 %collective-permute-start.3 = (f32[9,14,3,128]{3,1,2,0:T(8,128)S(1)}, f32[9,14,3,128]{3,1,2,0:T(8,128)S(1)}, u32[]{:S(2)}, u32[]{:S(2)}) collective-permute-start(f32[9,14,3,128]{3,1,2,0:T(8,128)S(1)} %copy.46), channel_id=1, source_target_pairs={{4,0},{8,4},{12,8},{0,12},{5,1},{9,5},{13,9},{1,13},{6,2},{10,6},{... | collective-permute-start | bytes 580616 | tf_op jit(solution)/shard_map/ppermute | solution.py:26
  34.1 5.6 %copy.33 = f32[9,14,8,128]{2,1,3,0:T(8,128)} copy(f32[9,14,8,128]{3,2,1,0:T(8,128)S(1)} %pad_maximum_fusion.3) | data formatting | bytes 1032192 | tf_op jit(solution)/shard_map/concatenate | solution.py:27
  39.7 5.4 %copy.32 = f32[9,14,3,128]{2,1,3,0:T(8,128)} copy(f32[9,14,3,128]{3,1,2,0:T(8,128)S(1)} %collective-permute-done.2) | data formatting | bytes 387072 | tf_op jit(solution)/shard_map/ppermute | solution.py:23
  45.1 5.4 %copy.34 = f32[9,14,3,128]{2,1,3,0:T(8,128)} copy(f32[9,14,3,128]{3,1,2,0:T(8,128)S(1)} %collective-permute-done.3) | data formatting | bytes 387072 | tf_op jit(solution)/shard_map/ppermute | solution.py:26
  50.5 11.1 %pad_maximum_fusion = f32[9,14,14,128]{2,1,3,0:T(8,128)S(1)} fusion(f32[9,14,3,128]{2,1,3,0:T(8,128)} %copy.34, f32[9,14,8,128]{2,1,3,0:T(8,128)} %copy.33, f32[9,14,3,128]{2,1,3,0:T(8,128)} %copy.32), kind=kLoop, calls=%fused_computation | loop fusion | flops 451584 | bytes 1806336 | tf_op jit(solution)/shard_map/concatenate | solution.py:27
  61.6 3.6 %copy-done = f32[9,14,14,128]{2,1,3,0:T(8,128)} copy-done((f32[9,14,14,128]{2,1,3,0:T(8,128)}, f32[9,14,14,128]{2,1,3,0:T(8,128)S(1)}, u32[]{:S(2)}) %copy-start) | copy-done | bytes 903192
  65.2 9.8 %collective-permute-start.5 = (f32[9,14,14,3]{2,1,3,0:T(8,128)S(1)}, f32[9,14,14,3]{2,1,3,0:T(8,128)S(1)}, u32[]{:S(2)}, u32[]{:S(2)}) collective-permute-start(f32[9,14,14,3]{2,1,3,0:T(8,128)S(1)} %get-tuple-element.31), channel_id=1, source_target_pairs={{1,0},{2,1},{3,2},{0,3},{5,4},{6,5},{7,6},{4,7},{9,8},{10,9},{11,1... | collective-permute-start | bytes 63512 | tf_op jit(solution)/shard_map/ppermute | solution.py:26
  75.1 1.9 collective-permute-start.4
  77.0 6.5 %copy.36 = f32[9,14,14,128]{3,2,1,0:T(8,128)S(1)} copy(f32[9,14,14,128]{2,1,3,0:T(8,128)} %copy-done) | data formatting | bytes 1806336 | tf_op jit(solution)/shard_map/concatenate | solution.py:27
  88.4 9.0 %pmin.35 = f32[]{:T(128)} all-reduce(f32[]{:T(128)} %fusion.319), channel_id=1, replica_groups=mesh['gx_0'=3,'gx_1'=8,'gx_2'=2,'gy'=4,'gz'=4] {'gx_0'}, use_global_device_ids=true, to_apply=%region_1.0 | all-reduce | flops 1 | bytes 8 | tf_op jit(solution)/shard_map/pmin | solution.py:33
  97.4 11.1 %pmin.36 = f32[]{:T(128)} all-reduce(f32[]{:T(128)} %pmin.35), channel_id=1, replica_groups=mesh['gx_0'=3,'gx_1'=8,'gx_2'=2,'gy'=4,'gz'=4] {'gx_1'}, use_global_device_ids=true, to_apply=%region_2.0 | all-reduce | flops 1 | bytes 8 | tf_op jit(solution)/shard_map/pmin | solution.py:33
  108.5 2.4 slice_bitcast_fusion.8
  110.9 4.3 %pmin.37 = f32[]{:T(128)} all-reduce(f32[]{:T(128)} %pmin.36), channel_id=1, replica_groups=mesh['gx_0'=3,'gx_1'=8,'gx_2'=2,'gy'=4,'gz'=4] {'gx_2'}, use_global_device_ids=true, to_apply=%region_3.0 | all-reduce | flops 1 | bytes 8 | tf_op jit(solution)/shard_map/pmin | solution.py:33
  117.9 7.5 %pmin.38 = f32[]{:T(128)} all-reduce(f32[]{:T(128)} %pmin.37), channel_id=1, replica_groups=mesh['gx_0'=3,'gx_1'=8,'gx_2'=2,'gy'=4,'gz'=4] {'gy'}, use_global_device_ids=true, to_apply=%region_4.0 | all-reduce | flops 1 | bytes 8 | tf_op jit(solution)/shard_map/pmin | solution.py:33
  126.6 10.7 %pmin.39 = f32[]{:T(128)} all-reduce(f32[]{:T(128)} %pmin.38), channel_id=1, replica_groups=mesh['gx_0'=3,'gx_1'=8,'gx_2'=2,'gy'=4,'gz'=4] {'gz'}, use_global_device_ids=true, to_apply=%region_5.0 | all-reduce | flops 1 | bytes 8 | tf_op jit(solution)/shard_map/pmin | solution.py:33
  143.1 1.5 multiply_add_fusion
  147.1 1.4 multiply_subtract_fusion.4
  150.0 1.5 multiply_subtract_fusion.5
  152.8 1.8 fusion.309
  155.6 9.8 %collective-permute-start.6 = (f32[4,2,8,128]{3,2,1,0:T(8,128)S(1)}, f32[4,2,8,128]{3,2,1,0:T(8,128)S(1)}, u32[]{:S(2)}, u32[]{:S(2)}) collective-permute-start(f32[4,2,8,128]{3,2,1,0:T(8,128)S(1)} %get-tuple-element.67), channel_id=1, source_target_pairs={{0,16},{16,32},{32,48},{48,64},{64,80},{80,96},{96,112},{112,128},... | collective-permute-start | bytes 98312 | tf_op jit(solution)/shard_map/ppermute | solution.py:23
  165.4 1.9 collective-permute-start.7
  167.4 9.3 %collective-permute-done.7 = f32[4,2,8,128]{3,2,1,0:T(8,128)S(1)} collective-permute-done((f32[4,2,8,128]{3,2,1,0:T(8,128)S(1)}, f32[4,2,8,128]{3,2,1,0:T(8,128)S(1)}, u32[]{:S(2)}, u32[]{:S(2)}) %collective-permute-start.7) | collective-permute-done | bytes 32800 | tf_op jit(solution)/shard_map/ppermute | solution.py:26
  176.8 2.7 collective-permute-start.8
  179.4 3.8 %collective-permute-start.9 = (f32[4,12,2,128]{3,0,2,1:T(4,128)S(1)}, f32[4,12,2,128]{3,0,2,1:T(4,128)S(1)}, u32[]{:S(2)}, u32[]{:S(2)}) collective-permute-start(f32[4,12,2,128]{3,0,2,1:T(4,128)S(1)} %copy.57), channel_id=1, source_target_pairs={{4,0},{8,4},{12,8},{0,12},{5,1},{9,5},{13,9},{1,13},{6,2},{10,6},{... | collective-permute-start | bytes 147464 | tf_op jit(solution)/shard_map/ppermute | solution.py:26
  185.4 1.9 collective-permute-start.10
  187.3 5.2 %collective-permute-start.11 = (f32[4,12,12,2]{3,0,2,1:T(4,128)S(1)}, f32[4,12,12,2]{3,0,2,1:T(4,128)}, u32[]{:S(2)}, u32[]{:S(2)}) collective-permute-start(f32[4,12,12,2]{3,0,2,1:T(4,128)S(1)} %get-tuple-element.47), channel_id=1, source_target_pairs={{1,0},{2,1},{3,2},{0,3},{5,4},{6,5},{7,6},{4,7},{9,8},{10,9},{11,1... | collective-permute-start | bytes 13832 | tf_op jit(solution)/shard_map/ppermute | solution.py:26
  195.1 3.0 %collective-permute-done.11 = f32[4,12,12,2]{3,0,2,1:T(4,128)} collective-permute-done((f32[4,12,12,2]{3,0,2,1:T(4,128)S(1)}, f32[4,12,12,2]{3,0,2,1:T(4,128)}, u32[]{:S(2)}, u32[]{:S(2)}) %collective-permute-start.11) | collective-permute-done | bytes 4640 | tf_op jit(solution)/shard_map/ppermute | solution.py:26
  198.0 1.5 pad_maximum_fusion.2
  203.3 4.6 %collective-permute-start.12 = (f32[2,8,128]{2,1,0:T(8,128)S(1)}, f32[2,8,128]{2,1,0:T(8,128)S(1)}, u32[]{:S(2)}, u32[]{:S(2)}) collective-permute-start(f32[2,8,128]{2,1,0:T(8,128)S(1)} %get-tuple-element.83), channel_id=1, source_target_pairs={{0,16},{16,32},{32,48},{48,64},{64,80},{80,96},{96,112},{112,128},... | collective-permute-start | bytes 24584 | tf_op jit(solution)/shard_map/ppermute | solution.py:23
  207.9 1.9 collective-permute-start.13
  215.0 3.9 %collective-permute-done.13 = f32[2,8,128]{2,1,0:T(8,128)S(1)} collective-permute-done((f32[2,8,128]{2,1,0:T(8,128)S(1)}, f32[2,8,128]{2,1,0:T(8,128)S(1)}, u32[]{:S(2)}, u32[]{:S(2)}) %collective-permute-start.13) | collective-permute-done | bytes 8224 | tf_op jit(solution)/shard_map/ppermute | solution.py:26
  218.9 1.9 collective-permute-start.14
  220.9 4.9 %collective-permute-start.15 = (f32[12,2,128]{2,1,0:T(2,128)S(1)}, f32[12,2,128]{2,1,0:T(2,128)S(1)}, u32[]{:S(2)}, u32[]{:S(2)}) collective-permute-start(f32[12,2,128]{2,1,0:T(2,128)S(1)} %get-tuple-element.80), channel_id=1, source_target_pairs={{4,0},{8,4},{12,8},{0,12},{5,1},{9,5},{13,9},{1,13},{6,2},{10,6},{... | collective-permute-start | bytes 36872 | tf_op jit(solution)/shard_map/ppermute | solution.py:26
  226.9 1.9 collective-permute-start.16
  228.8 5.4 %collective-permute-start.17 = (f32[12,12,2]{2,1,0:T(8,128)S(1)}, f32[12,12,2]{2,1,0:T(8,128)S(1)}, u32[]{:S(2)}, u32[]{:S(2)}) collective-permute-start(f32[12,12,2]{2,1,0:T(8,128)S(1)} %get-tuple-element.72), channel_id=1, source_target_pairs={{1,0},{2,1},{3,2},{0,3},{5,4},{6,5},{7,6},{4,7},{9,8},{10,9},{11,1... | collective-permute-start | bytes 3464 | tf_op jit(solution)/shard_map/ppermute | solution.py:26
  234.2 1.6 multiply_subtract_fusion.2
  238.6 7.3 %collective-permute-start.18 = (f32[2,8,128]{2,1,0:T(8,128)S(1)}, f32[2,8,128]{2,1,0:T(8,128)S(1)}, u32[]{:S(2)}, u32[]{:S(2)}) collective-permute-start(f32[2,8,128]{2,1,0:T(8,128)S(1)} %get-tuple-element.81), channel_id=1, source_target_pairs={{0,16},{16,32},{32,48},{48,64},{64,80},{80,96},{96,112},{112,128},... | collective-permute-start | bytes 24584 | tf_op jit(solution)/shard_map/ppermute | solution.py:23
  245.9 1.9 collective-permute-start.19
  249.1 7.8 %collective-permute-done.19 = f32[2,8,128]{2,1,0:T(8,128)S(1)} collective-permute-done((f32[2,8,128]{2,1,0:T(8,128)S(1)}, f32[2,8,128]{2,1,0:T(8,128)S(1)}, u32[]{:S(2)}, u32[]{:S(2)}) %collective-permute-start.19) | collective-permute-done | bytes 8224 | tf_op jit(solution)/shard_map/ppermute | solution.py:26
  256.9 3.3 %collective-permute-start.20 = (f32[12,2,128]{2,1,0:T(2,128)S(1)}, f32[12,2,128]{2,1,0:T(2,128)S(1)}, u32[]{:S(2)}, u32[]{:S(2)}) collective-permute-start(f32[12,2,128]{2,1,0:T(2,128)S(1)} %get-tuple-element.77), channel_id=1, source_target_pairs={{0,4},{4,8},{8,12},{12,0},{1,5},{5,9},{9,13},{13,1},{2,6},{6,10},{... | collective-permute-start | bytes 36872 | tf_op jit(solution)/shard_map/ppermute | solution.py:23
  260.2 3.7 %collective-permute-start.21 = (f32[12,2,128]{2,1,0:T(2,128)S(1)}, f32[12,2,128]{2,1,0:T(2,128)S(1)}, u32[]{:S(2)}, u32[]{:S(2)}) collective-permute-start(f32[12,2,128]{2,1,0:T(2,128)S(1)} %get-tuple-element.78), channel_id=1, source_target_pairs={{4,0},{8,4},{12,8},{0,12},{5,1},{9,5},{13,9},{1,13},{6,2},{10,6},{... | collective-permute-start | bytes 36872 | tf_op jit(solution)/shard_map/ppermute | solution.py:26
  264.0 1.7 fusion.273
  265.8 1.9 collective-permute-start.22
  267.7 5.8 %collective-permute-start.23 = (f32[12,12,2]{2,1,0:T(8,128)S(1)}, f32[12,12,2]{2,1,0:T(8,128)S(1)}, u32[]{:S(2)}, u32[]{:S(2)}) collective-permute-start(f32[12,12,2]{2,1,0:T(8,128)S(1)} %get-tuple-element.70), channel_id=1, source_target_pairs={{1,0},{2,1},{3,2},{0,3},{5,4},{6,5},{7,6},{4,7},{9,8},{10,9},{11,1... | collective-permute-start | bytes 3464 | tf_op jit(solution)/shard_map/ppermute | solution.py:26
  (110 shorter events, 39.0 us)
Async XLA Ops:
  4.7 12.3 %collective-permute-start = (f32[9,3,8,128]{3,2,1,0:T(8,128)S(1)}, f32[9,3,8,128]{3,2,1,0:T(8,128)S(1)}, u32[]{:S(2)}, u32[]{:S(2)}) collective-permute-start(f32[9,3,8,128]{3,2,1,0:T(8,128)S(1)} %get-tuple-element.48), channel_id=1, source_target_pairs={{0,16},{16,32},{32,48},{48,64},{64,80},{80,96},{96,112},{112,128},... | collective-permute-start | bytes 331784 | tf_op jit(solution)/shard_map/ppermute | solution.py:23
  15.1 12.2 %collective-permute-start.1 = (f32[9,3,8,128]{3,2,1,0:T(8,128)S(1)}, f32[9,3,8,128]{3,2,1,0:T(8,128)S(1)}, u32[]{:S(2)}, u32[]{:S(2)}) collective-permute-start(f32[9,3,8,128]{3,2,1,0:T(8,128)S(1)} %get-tuple-element.49), channel_id=1, source_target_pairs={{16,0},{32,16},{48,32},{64,48},{80,64},{96,80},{112,96},{128,112},... | collective-permute-start | bytes 331784 | tf_op jit(solution)/shard_map/ppermute | solution.py:26
  27.5 12.1 %collective-permute-start.2 = (f32[9,14,3,128]{3,1,2,0:T(8,128)S(1)}, f32[9,14,3,128]{3,1,2,0:T(8,128)S(1)}, u32[]{:S(2)}, u32[]{:S(2)}) collective-permute-start(f32[9,14,3,128]{3,1,2,0:T(8,128)S(1)} %copy.45), channel_id=1, source_target_pairs={{0,4},{4,8},{8,12},{12,0},{1,5},{5,9},{9,13},{13,1},{2,6},{6,10},{... | collective-permute-start | bytes 580616 | tf_op jit(solution)/shard_map/ppermute | solution.py:23
  30.7 14.4 %collective-permute-start.3 = (f32[9,14,3,128]{3,1,2,0:T(8,128)S(1)}, f32[9,14,3,128]{3,1,2,0:T(8,128)S(1)}, u32[]{:S(2)}, u32[]{:S(2)}) collective-permute-start(f32[9,14,3,128]{3,1,2,0:T(8,128)S(1)} %copy.46), channel_id=1, source_target_pairs={{4,0},{8,4},{12,8},{0,12},{5,1},{9,5},{13,9},{1,13},{6,2},{10,6},{... | collective-permute-start | bytes 580616 | tf_op jit(solution)/shard_map/ppermute | solution.py:26
  61.6 3.6 %copy-start = (f32[9,14,14,128]{2,1,3,0:T(8,128)}, f32[9,14,14,128]{2,1,3,0:T(8,128)S(1)}, u32[]{:S(2)}) copy-start(f32[9,14,14,128]{2,1,3,0:T(8,128)S(1)} %pad_maximum_fusion) | copy-start | bytes 2709508
  65.2 18.3 %collective-permute-start.5 = (f32[9,14,14,3]{2,1,3,0:T(8,128)S(1)}, f32[9,14,14,3]{2,1,3,0:T(8,128)S(1)}, u32[]{:S(2)}, u32[]{:S(2)}) collective-permute-start(f32[9,14,14,3]{2,1,3,0:T(8,128)S(1)} %get-tuple-element.31), channel_id=1, source_target_pairs={{1,0},{2,1},{3,2},{0,3},{5,4},{6,5},{7,6},{4,7},{9,8},{10,9},{11,1... | collective-permute-start | bytes 63512 | tf_op jit(solution)/shard_map/ppermute | solution.py:26
  75.1 9.4 %collective-permute-start.4 = (f32[9,14,14,3]{2,1,3,0:T(8,128)S(1)}, f32[9,14,14,3]{2,1,3,0:T(8,128)S(1)}, u32[]{:S(2)}, u32[]{:S(2)}) collective-permute-start(f32[9,14,14,3]{2,1,3,0:T(8,128)S(1)} %get-tuple-element.30), channel_id=1, source_target_pairs={{0,1},{1,2},{2,3},{3,0},{4,5},{5,6},{6,7},{7,4},{8,9},{9,10},{10,1... | collective-permute-start | bytes 63512 | tf_op jit(solution)/shard_map/ppermute | solution.py:23
  86.2 1.3 copy-start.1
  140.0 10.0 %copy-start.2 = (f32[12,12,132]{2,1,0:T(8,128)}, f32[12,12,132]{2,1,0:T(8,128)S(1)}, u32[]{:S(2)}) copy-start(f32[12,12,132]{2,1,0:T(8,128)S(1)} %get-tuple-element.56) | copy-start | bytes 228100
  151.5 50.2 %copy-start.3 = (f32[12,12,132]{2,1,0:T(8,128)S(1)}, f32[12,12,132]{2,1,0:T(8,128)}, u32[]{:S(2)}) copy-start(f32[12,12,132]{2,1,0:T(8,128)} %copy-done.2) | copy-start | bytes 228100
  155.6 11.8 %collective-permute-start.6 = (f32[4,2,8,128]{3,2,1,0:T(8,128)S(1)}, f32[4,2,8,128]{3,2,1,0:T(8,128)S(1)}, u32[]{:S(2)}, u32[]{:S(2)}) collective-permute-start(f32[4,2,8,128]{3,2,1,0:T(8,128)S(1)} %get-tuple-element.67), channel_id=1, source_target_pairs={{0,16},{16,32},{32,48},{48,64},{64,80},{80,96},{96,112},{112,128},... | collective-permute-start | bytes 98312 | tf_op jit(solution)/shard_map/ppermute | solution.py:23
  165.4 11.3 %collective-permute-start.7 = (f32[4,2,8,128]{3,2,1,0:T(8,128)S(1)}, f32[4,2,8,128]{3,2,1,0:T(8,128)S(1)}, u32[]{:S(2)}, u32[]{:S(2)}) collective-permute-start(f32[4,2,8,128]{3,2,1,0:T(8,128)S(1)} %get-tuple-element.68), channel_id=1, source_target_pairs={{16,0},{32,16},{48,32},{64,48},{80,64},{96,80},{112,96},{128,112},... | collective-permute-start | bytes 98312 | tf_op jit(solution)/shard_map/ppermute | solution.py:26
  176.8 6.5 %collective-permute-start.8 = (f32[4,12,2,128]{3,0,2,1:T(4,128)S(1)}, f32[4,12,2,128]{3,0,2,1:T(4,128)S(1)}, u32[]{:S(2)}, u32[]{:S(2)}) collective-permute-start(f32[4,12,2,128]{3,0,2,1:T(4,128)S(1)} %copy.56), channel_id=1, source_target_pairs={{0,4},{4,8},{8,12},{12,0},{1,5},{5,9},{9,13},{13,1},{2,6},{6,10},{... | collective-permute-start | bytes 147464 | tf_op jit(solution)/shard_map/ppermute | solution.py:23
  179.4 5.0 %collective-permute-start.9 = (f32[4,12,2,128]{3,0,2,1:T(4,128)S(1)}, f32[4,12,2,128]{3,0,2,1:T(4,128)S(1)}, u32[]{:S(2)}, u32[]{:S(2)}) collective-permute-start(f32[4,12,2,128]{3,0,2,1:T(4,128)S(1)} %copy.57), channel_id=1, source_target_pairs={{4,0},{8,4},{12,8},{0,12},{5,1},{9,5},{13,9},{1,13},{6,2},{10,6},{... | collective-permute-start | bytes 147464 | tf_op jit(solution)/shard_map/ppermute | solution.py:26
  185.4 9.7 %collective-permute-start.10 = (f32[4,12,12,2]{3,0,2,1:T(4,128)}, f32[4,12,12,2]{3,0,2,1:T(4,128)S(1)}, u32[]{:S(2)}, u32[]{:S(2)}) collective-permute-start(f32[4,12,12,2]{3,0,2,1:T(4,128)} %get-tuple-element.46), channel_id=1, source_target_pairs={{0,1},{1,2},{2,3},{3,0},{4,5},{5,6},{6,7},{7,4},{8,9},{9,10},{10,1... | collective-permute-start | bytes 13832 | tf_op jit(solution)/shard_map/ppermute | solution.py:23
  187.3 10.7 %collective-permute-start.11 = (f32[4,12,12,2]{3,0,2,1:T(4,128)S(1)}, f32[4,12,12,2]{3,0,2,1:T(4,128)}, u32[]{:S(2)}, u32[]{:S(2)}) collective-permute-start(f32[4,12,12,2]{3,0,2,1:T(4,128)S(1)} %get-tuple-element.47), channel_id=1, source_target_pairs={{1,0},{2,1},{3,2},{0,3},{5,4},{6,5},{7,6},{4,7},{9,8},{10,9},{11,1... | collective-permute-start | bytes 13832 | tf_op jit(solution)/shard_map/ppermute | solution.py:26
  200.7 35.2 %copy-start.4 = (f32[12,12,132]{2,1,0:T(8,128)}, f32[12,12,132]{2,1,0:T(8,128)S(1)}, u32[]{:S(2)}) copy-start(f32[12,12,132]{2,1,0:T(8,128)S(1)} %get-tuple-element.87) | copy-start | bytes 228100
  203.3 70.3 %copy-start.5 = (f32[3,8,8,128]{3,2,1,0:T(8,128)S(1)}, f32[3,8,8,128]{3,2,1,0:T(8,128)}, u32[]{:S(2)}) copy-start(f32[3,8,8,128]{3,2,1,0:T(8,128)} %param.7) | copy-start | bytes 294916
  203.3 11.7 %collective-permute-start.12 = (f32[2,8,128]{2,1,0:T(8,128)S(1)}, f32[2,8,128]{2,1,0:T(8,128)S(1)}, u32[]{:S(2)}, u32[]{:S(2)}) collective-permute-start(f32[2,8,128]{2,1,0:T(8,128)S(1)} %get-tuple-element.83), channel_id=1, source_target_pairs={{0,16},{16,32},{32,48},{48,64},{64,80},{80,96},{96,112},{112,128},... | collective-permute-start | bytes 24584 | tf_op jit(solution)/shard_map/ppermute | solution.py:23
  207.9 11.0 %collective-permute-start.13 = (f32[2,8,128]{2,1,0:T(8,128)S(1)}, f32[2,8,128]{2,1,0:T(8,128)S(1)}, u32[]{:S(2)}, u32[]{:S(2)}) collective-permute-start(f32[2,8,128]{2,1,0:T(8,128)S(1)} %get-tuple-element.84), channel_id=1, source_target_pairs={{16,0},{32,16},{48,32},{64,48},{80,64},{96,80},{112,96},{128,112},... | collective-permute-start | bytes 24584 | tf_op jit(solution)/shard_map/ppermute | solution.py:26
  218.9 7.9 %collective-permute-start.14 = (f32[12,2,128]{2,1,0:T(2,128)S(1)}, f32[12,2,128]{2,1,0:T(2,128)S(1)}, u32[]{:S(2)}, u32[]{:S(2)}) collective-permute-start(f32[12,2,128]{2,1,0:T(2,128)S(1)} %get-tuple-element.79), channel_id=1, source_target_pairs={{0,4},{4,8},{8,12},{12,0},{1,5},{5,9},{9,13},{13,1},{2,6},{6,10},{... | collective-permute-start | bytes 36872 | tf_op jit(solution)/shard_map/ppermute | solution.py:23
  220.9 5.9 %collective-permute-start.15 = (f32[12,2,128]{2,1,0:T(2,128)S(1)}, f32[12,2,128]{2,1,0:T(2,128)S(1)}, u32[]{:S(2)}, u32[]{:S(2)}) collective-permute-start(f32[12,2,128]{2,1,0:T(2,128)S(1)} %get-tuple-element.80), channel_id=1, source_target_pairs={{4,0},{8,4},{12,8},{0,12},{5,1},{9,5},{13,9},{1,13},{6,2},{10,6},{... | collective-permute-start | bytes 36872 | tf_op jit(solution)/shard_map/ppermute | solution.py:26
  226.9 8.9 %collective-permute-start.16 = (f32[12,12,2]{2,1,0:T(8,128)S(1)}, f32[12,12,2]{2,1,0:T(8,128)S(1)}, u32[]{:S(2)}, u32[]{:S(2)}) collective-permute-start(f32[12,12,2]{2,1,0:T(8,128)S(1)} %get-tuple-element.71), channel_id=1, source_target_pairs={{0,1},{1,2},{2,3},{3,0},{4,5},{5,6},{6,7},{7,4},{8,9},{9,10},{10,1... | collective-permute-start | bytes 3464 | tf_op jit(solution)/shard_map/ppermute | solution.py:23
  228.8 7.0 %collective-permute-start.17 = (f32[12,12,2]{2,1,0:T(8,128)S(1)}, f32[12,12,2]{2,1,0:T(8,128)S(1)}, u32[]{:S(2)}, u32[]{:S(2)}) collective-permute-start(f32[12,12,2]{2,1,0:T(8,128)S(1)} %get-tuple-element.72), channel_id=1, source_target_pairs={{1,0},{2,1},{3,2},{0,3},{5,4},{6,5},{7,6},{4,7},{9,8},{10,9},{11,1... | collective-permute-start | bytes 3464 | tf_op jit(solution)/shard_map/ppermute | solution.py:26
  238.6 10.5 %collective-permute-start.18 = (f32[2,8,128]{2,1,0:T(8,128)S(1)}, f32[2,8,128]{2,1,0:T(8,128)S(1)}, u32[]{:S(2)}, u32[]{:S(2)}) collective-permute-start(f32[2,8,128]{2,1,0:T(8,128)S(1)} %get-tuple-element.81), channel_id=1, source_target_pairs={{0,16},{16,32},{32,48},{48,64},{64,80},{80,96},{96,112},{112,128},... | collective-permute-start | bytes 24584 | tf_op jit(solution)/shard_map/ppermute | solution.py:23
  245.9 11.0 %collective-permute-start.19 = (f32[2,8,128]{2,1,0:T(8,128)S(1)}, f32[2,8,128]{2,1,0:T(8,128)S(1)}, u32[]{:S(2)}, u32[]{:S(2)}) collective-permute-start(f32[2,8,128]{2,1,0:T(8,128)S(1)} %get-tuple-element.82), channel_id=1, source_target_pairs={{16,0},{32,16},{48,32},{64,48},{80,64},{96,80},{112,96},{128,112},... | collective-permute-start | bytes 24584 | tf_op jit(solution)/shard_map/ppermute | solution.py:26
  256.9 8.7 %collective-permute-start.20 = (f32[12,2,128]{2,1,0:T(2,128)S(1)}, f32[12,2,128]{2,1,0:T(2,128)S(1)}, u32[]{:S(2)}, u32[]{:S(2)}) collective-permute-start(f32[12,2,128]{2,1,0:T(2,128)S(1)} %get-tuple-element.77), channel_id=1, source_target_pairs={{0,4},{4,8},{8,12},{12,0},{1,5},{5,9},{9,13},{13,1},{2,6},{6,10},{... | collective-permute-start | bytes 36872 | tf_op jit(solution)/shard_map/ppermute | solution.py:23
  260.2 5.4 %collective-permute-start.21 = (f32[12,2,128]{2,1,0:T(2,128)S(1)}, f32[12,2,128]{2,1,0:T(2,128)S(1)}, u32[]{:S(2)}, u32[]{:S(2)}) collective-permute-start(f32[12,2,128]{2,1,0:T(2,128)S(1)} %get-tuple-element.78), channel_id=1, source_target_pairs={{4,0},{8,4},{12,8},{0,12},{5,1},{9,5},{13,9},{1,13},{6,2},{10,6},{... | collective-permute-start | bytes 36872 | tf_op jit(solution)/shard_map/ppermute | solution.py:26
  265.8 8.4 %collective-permute-start.22 = (f32[12,12,2]{2,1,0:T(8,128)S(1)}, f32[12,12,2]{2,1,0:T(8,128)S(1)}, u32[]{:S(2)}, u32[]{:S(2)}) collective-permute-start(f32[12,12,2]{2,1,0:T(8,128)S(1)} %get-tuple-element.69), channel_id=1, source_target_pairs={{0,1},{1,2},{2,3},{3,0},{4,5},{5,6},{6,7},{7,4},{8,9},{9,10},{10,1... | collective-permute-start | bytes 3464 | tf_op jit(solution)/shard_map/ppermute | solution.py:23
  267.7 7.5 %collective-permute-start.23 = (f32[12,12,2]{2,1,0:T(8,128)S(1)}, f32[12,12,2]{2,1,0:T(8,128)S(1)}, u32[]{:S(2)}, u32[]{:S(2)}) collective-permute-start(f32[12,12,2]{2,1,0:T(8,128)S(1)} %get-tuple-element.70), channel_id=1, source_target_pairs={{1,0},{2,1},{3,2},{0,3},{5,4},{6,5},{7,6},{4,7},{9,8},{10,9},{11,1... | collective-permute-start | bytes 3464 | tf_op jit(solution)/shard_map/ppermute | solution.py:26
where the time goes:
time: 280 us; the launch traced here: 279 us
  starting transfers between devices  101 us (36%)
  other arithmetic  48.1 us (17%)
  blocking collectives  42.7 us (15%)
  local copies, waits for them, and re-layouts  39.9 us (14%)
  waiting for transfers between devices  36.2 us (13%)
  between operations  11.1 us (4%)
    ppermute x12, starting transfers between devices, extended(): lax.ppermute(lax.slice_in_dim(block, block.shape[dim] - width, None, axis...  50.9 us
    ppermute x12, starting transfers between devices, extended(): lax.ppermute(lax.slice_in_dim(block, 0, width, axis=dim), axis, backward)  49.7 us
    pmin x5, blocking collectives, by_axis(): x = lax.pmin(x, axis)  42.7 us
    ppermute x12, waiting for transfers between devices, extended(): lax.ppermute(lax.slice_in_dim(block, 0, width, axis=dim), axis, backward)  36.2 us
    concatenate x11, other arithmetic, extended(): block = jnp.concatenate([low, block, high], axis=dim)  14.3 us
    concatenate x3, local copies, waits for them, and re-layouts, extended(): block = jnp.concatenate([low, block, high], axis=dim)  12.1 us
    neg x24, other arithmetic, diffuse_thermal(): -(along_normal * (shifted(REFERENCE_SPOT) - shifted(backward)) + along_fi...  10.6 us
    unnamed x22, local copies, waits for them, and re-layouts  8.52 us
  transfers between devices with their start and end apart: 24, of which 7 were waited for; matrix products, arithmetic and copies ran while one was open for 9% of the time, Pallas kernels for 0%

commit v1 on v0

v1 whole, which is shorter than its diff:
```python
import functools

import jax
import jax.numpy as jnp
from jax import lax
from jax.experimental import pallas as pl
from jax.experimental.pallas import tpu as pltpu
from jax.sharding import PartitionSpec as P

SECTIONS = 8
GAMMA = 5.0 / 3.0
FACE_FLOOR = 0.25

W = 8
LANES = 128
XE = 3 * W
ROWS = 6 * W
FULL = 5
AUX = 4
AX = 2
XA = W + 2 * AX
SIDE = FULL * W + AUX * AX
TILES = FULL * XE + AUX * XA
PIECES = 16
ZT = -(-TILES // PIECES)
YT = FULL * XE + AUX * XA // 4 + 2 * ZT
FIRST_RATE = 4.0 / (SECTIONS * SECTIONS + SECTIONS - 2)
LIMIT = (SECTIONS * SECTIONS + SECTIONS - 2) / 16.0


def lane_ids(rows):
    return lax.broadcasted_iota(jnp.int32, (rows, LANES), 1)


def lroll(u, amount):
    return pltpu.roll(u, amount % LANES, 1)


def rroll(u, amount):
    return pltpu.roll(u, amount % u.shape[0], 0)


def pack_x(slots, t_ref, d_ref, b_ref, v_ref, r_ref, fwd_ref, bwd_ref, kap_ref, low_ref):
    t = t_ref[...]
    kappa = d_ref[...] * (t * t * jnp.sqrt(t))
    kap_ref[...] = kappa
    low = jnp.min(LIMIT / kappa, axis=0)
    low = jnp.min(jnp.min(low, axis=0, keepdims=True), axis=1, keepdims=True)
    low_ref[...] = jnp.broadcast_to(low.reshape(1, 1, 1), (slots, 1, LANES))
    for ref in (fwd_ref, bwd_ref):
        ref[0:W] = t
        ref[W : 2 * W] = kappa
        for k in range(3):
            ref[(2 + k) * W : (3 + k) * W] = b_ref[k]
    for k in range(AUX):
        at = FULL * W + k * AX
        source = v_ref.at[k] if k < 3 else r_ref
        fwd_ref[at : at + AX] = source[W - AX : W]
        bwd_ref[at : at + AX] = source[0:AX]


def extended_tile(i, lo_ref, hi_ref, own):
    if i < FULL * XE:
        field, plane = divmod(i, XE)
        part, at = divmod(plane, W)
        return (lo_ref, None, hi_ref)[part][field * W + at] if part != 1 else own(field, at)
    field, plane = divmod(i - FULL * XE, XA)
    at = FULL * W + field * AX
    if plane < AX:
        return lo_ref[at + plane]
    if plane < AX + W:
        return own(FULL + field, plane - AX)
    return hi_ref[at + plane - AX - W]


def owner(t_ref, k_ref, b_ref, v_ref, r_ref):
    def own(field, at):
        if field == 0:
            return t_ref[at]
        if field == 1:
            return k_ref[at]
        if field < FULL:
            return b_ref[field - 2, at]
        return v_ref[field - FULL, at] if field < FULL + 3 else r_ref[at]

    return own


def pack_z(lo_ref, hi_ref, t_ref, k_ref, b_ref, v_ref, r_ref, left_ref, right_ref):
    own = owner(t_ref, k_ref, b_ref, v_ref, r_ref)
    lane = lane_ids(W)
    for tile in range(ZT):
        left = jnp.zeros((W, LANES), jnp.float32)
        right = left
        for k in range(PIECES):
            i = tile * PIECES + k
            if i >= TILES:
                break
            u = extended_tile(i, lo_ref, hi_ref, own)
            here = (lane >= 8 * k) & (lane < 8 * k + 8)
            left = jnp.where(here, lroll(u, 8 * k), left)
            right = jnp.where(here, lroll(u, 8 * k - (LANES - 8)), right)
        left_ref[tile] = left
        right_ref[tile] = right


def pack_y(lo_ref, hi_ref, t_ref, k_ref, b_ref, v_ref, r_ref, gl_ref, gr_ref, fwd_ref, bwd_ref):
    own = owner(t_ref, k_ref, b_ref, v_ref, r_ref)
    for i in range(FULL * XE):
        u = extended_tile(i, lo_ref, hi_ref, own)
        fwd_ref[i] = u
        bwd_ref[i] = u
    for i in range(AUX * XA):
        u = extended_tile(FULL * XE + i, lo_ref, hi_ref, own)
        tile, k = FULL * XE + i // 4, i % 4
        fwd_ref[tile, AX * k : AX * k + AX] = u[W - AX : W]
        bwd_ref[tile, AX * k : AX * k + AX] = u[0:AX]
    at = YT - 2 * ZT
    for ref in (fwd_ref, bwd_ref):
        ref[at : at + ZT] = gl_ref[...]
        ref[at + ZT : at + 2 * ZT] = gr_ref[...]


def strips(u, left, right, k, lane):
    inner = jnp.where(lane < 32, lroll(u, 8), lroll(u, 32 - (LANES - 16)))
    edge = jnp.where(lane < 8, lroll(left, -8 * k), lroll(right, 48 - 8 * k))
    return jnp.where((lane < 8) | (lane >= 48), edge, inner)


def advance(
    lo_ref,
    hi_ref,
    t_ref,
    k_ref,
    b_ref,
    v_ref,
    r_ref,
    gl_ref,
    gr_ref,
    ly_ref,
    hy_ref,
    low_ref,
    tout_ref,
    bout_ref,
    full,
    aux,
    coef,
    qa,
    qb,
    ecoef,
    edge,
    mid,
):
    own = owner(t_ref, k_ref, b_ref, v_ref, r_ref)
    lane = lane_ids(W)
    dt = jnp.min(jnp.min(low_ref[...], axis=0), axis=1, keepdims=True)

    at = YT - 2 * ZT
    for i in range(TILES):
        tile, k = divmod(i, PIECES)
        u = extended_tile(i, lo_ref, hi_ref, own)
        mine = (u, gl_ref[tile], gr_ref[tile])
        sides = []
        for ref, row in ((ly_ref, W - AX), (hy_ref, 0)):
            if i < FULL * XE:
                side = ref[i]
            else:
                j = i - FULL * XE
                rows = ref[FULL * XE + j // 4, AX * (j % 4) : AX * (j % 4) + AX]
                side = jnp.concatenate([rows] * 4, axis=0)
            sides.append((side, ref[at + tile], ref[at + ZT + tile]))
        for part, (u, left, right) in enumerate((sides[0], mine, sides[1])):
            s = strips(u, left, right, k, lane)
            if i < FULL * XE:
                field, plane = divmod(i, XE)
                full[field, plane, part * W : part * W + W] = u
                full[field, plane, 3 * W + part * W : 3 * W + part * W + W] = s
            else:
                field, plane = divmod(i - FULL * XE, XA)
                aux[field, plane, part * W : part * W + W] = u
                aux[field, plane, 3 * W + part * W : 3 * W + part * W + W] = s

    def sums(x):
        bx, by, bz = full[2, x], full[3, x], full[4, x]
        sx = bx + full[2, jnp.minimum(x + 1, XE - 1)]
        sy = by + rroll(by, -1)
        sz = bz + lroll(bz, -1)
        return bx, by, bz, sx, sy, sz

    def face(n, x, kk, bn, b1, b2):
        b1, b2 = 0.25 * b1, 0.25 * b2
        q = bn * bn + b1 * b1 + b2 * b2
        s = (0.5 * FIRST_RATE * dt) * kk / jnp.maximum(q, FACE_FLOOR) * bn
        coef[3 * n, x] = s * bn
        coef[3 * n + 1, x] = 0.25 * (s * b1)
        coef[3 * n + 2, x] = 0.25 * (s * b2)

    def faces(x, carry):
        k_m, sy_m, sz_m = carry
        kap = full[1, x]
        bx, by, bz, sx, sy, sz = sums(x)
        face(0, x, kap + k_m, bx, sy + sy_m, sz + sz_m)
        face(1, x, kap + rroll(kap, 1), by, sz + rroll(sz, 1), sx + rroll(sx, 1))
        face(2, x, kap + lroll(kap, 1), bz, sx + lroll(sx, 1), sy + lroll(sy, 1))
        return kap, sy, sz

    _, _, _, _, sy, sz = sums(0)
    lax.fori_loop(1, XE, faces, (full[1, 0], sy, sz))

    source, older = full.at[0], None
    for j in range(1, SECTIONS + 1):
        target = qa if j % 2 else qb
        grow = (2.0 * j - 1.0) / j
        back = (j - 1.0) / j

        def slopes(u):
            return rroll(u, -1) - rroll(u, 1), lroll(u, -1) - lroll(u, 1)

        def flux_x(x, u, u_m, dy, dy_m, dz, dz_m):
            return coef[0, x] * (u - u_m) + coef[1, x] * (dy + dy_m) + coef[2, x] * (dz + dz_m)

        def plane(x, carry, source=source, older=older, target=target, grow=grow, back=back, j=j):
            u_m, u, dy, dz, fx = carry
            u_p = source[x + 1]
            dy_p, dz_p = slopes(u_p)
            fx_p = flux_x(x + 1, u_p, u, dy_p, dy, dz_p, dz)
            dx = u_p - u_m
            fy = (
                coef[3, x] * (u - rroll(u, 1))
                + coef[4, x] * (dz + rroll(dz, 1))
                + coef[5, x] * (dx + rroll(dx, 1))
            )
            fz = (
                coef[6, x] * (u - lroll(u, 1))
                + coef[7, x] * (dx + lroll(dx, 1))
                + coef[8, x] * (dy + lroll(dy, 1))
            )
            rate = (fx_p - fx) + (rroll(fy, -1) - fy) + (lroll(fz, -1) - fz)
            new = u + rate
            if j > 1:
                new = grow * new - back * older[x]
            if j == SECTIONS:
                b = (SECTIONS * SECTIONS + SECTIONS - 2) / (2.0 * SECTIONS * (SECTIONS + 1))
                new = (1.0 - b) * full[0, x] + b * new
            target[x] = new
            return u, u_p, dy_p, dz_p, fx_p

        u_m, u = source[j - 1], source[j]
        dy_m, dz_m = slopes(u_m)
        dy, dz = slopes(u)
        fx = flux_x(j, u, u_m, dy, dy_m, dz, dz_m)
        lax.fori_loop(j, XE - j, plane, (u_m, u, dy, dz, fx))
        source, older = target, source

    def seam(main, strip):
        high = lroll(strip, LANES - 8 - 40)
        return jnp.where(lane < 8, lroll(strip, -8), jnp.where(lane >= LANES - 8, high, main))

    for x in range(W):
        tout_ref[x] = seam(source[W + x, W : 2 * W], source[W + x, 4 * W : 5 * W])

    off = W - AX
    SPEED = 3

    def speed(i, carry):
        x = i + off
        bx, by, bz, sx, sy, sz = sums(x)
        field = 0.25 * (sx * sx + sy * sy + sz * sz)
        vx, vy, vz = aux[0, i], aux[1, i], aux[2, i]
        flow = jnp.sqrt(vx * vx + vy * vy + vz * vz)
        aux[SPEED, i] = flow + jnp.sqrt(GAMMA * full[0, x] + field / aux[SPEED, i])
        return carry

    lax.fori_loop(0, XA, speed, 0)

    def by_axis(u, u_m, axis):
        if axis == 0:
            return u_m
        return rroll(u, 1) if axis == 1 else lroll(u, 1)

    def edges(i, carry):
        for c in range(3):
            a, b = (c + 1) % 3, (c + 2) % 3

            def mean(f):
                if 0 in (a, b):
                    other = a + b
                    u = aux[f, i] + aux[f, i - 1]
                else:
                    other = 2
                    u = aux[f, i]
                    u = u + by_axis(u, None, 1)
                return 0.125 * (u + by_axis(u, None, other))

            va, vb, s = mean(a), mean(b), mean(SPEED)
            ecoef[4 * c, i] = vb - s
            ecoef[4 * c + 1, i] = vb + s
            ecoef[4 * c + 2, i] = s - va
            ecoef[4 * c + 3, i] = -s - va
        return carry

    lax.fori_loop(1, XA, edges, 0)

    def fields(get, first, last):
        def body(i, carry):
            for c in range(3):
                a, b = (c + 1) % 3, (c + 2) % 3
                ua, ub = get(a, i), get(b, i)
                ua_b = by_axis(ua, get(a, i - 1) if b == 0 else None, b)
                ub_a = by_axis(ub, get(b, i - 1) if a == 0 else None, a)
                edge[c, i] = (ecoef[4 * c, i] * ua + ecoef[4 * c + 1, i] * ua_b) + (
                    ecoef[4 * c + 2, i] * ub + ecoef[4 * c + 3, i] * ub_a
                )
            return carry

        lax.fori_loop(first, last, body, 0)

    def ahead(f, i, axis):
        if axis == 0:
            return edge[f, i + 1]
        u = edge[f, i]
        return rroll(u, -1) if axis == 1 else lroll(u, -1)

    def curl(d, i):
        e, f = (d + 1) % 3, (d + 2) % 3
        return (ahead(f, i, e) - edge[f, i]) - (ahead(e, i, f) - edge[e, i])

    fields(lambda d, i: full[2 + d, i + off], 1, XA)

    def middle(i, carry):
        for d in range(3):
            mid[d, i] = full[2 + d, i + off] - dt * curl(d, i)
        return carry

    lax.fori_loop(1, XA - 1, middle, 0)
    fields(lambda d, i: mid[d, i], 2, XA - 1)

    def last(i, carry):
        for d in range(3):
            u = 0.5 * (full[2 + d, i + off] + (mid[d, i] - dt * curl(d, i)))
            bout_ref[d, i - AX] = seam(u[W : 2 * W], u[4 * W : 5 * W])
        return carry

    lax.fori_loop(AX, AX + W, last, 0)


def exchange(low_going, high_going, axis):
    count = lax.axis_size(axis)
    forward = [(i, (i + 1) % count) for i in range(count)]
    backward = [(target, source) for source, target in forward]
    from_low = lax.ppermute(high_going, axis, forward)
    from_high = lax.ppermute(low_going, axis, backward)
    return from_low, from_high


def f32(*shape):
    return jax.ShapeDtypeStruct(shape, jnp.float32)


def on_device(t, diffusivity, b, v, rho):
    yz = lax.axis_size("gy") * lax.axis_size("gz")
    xs = lax.axis_size("gx")
    fwd, bwd, kappa, low = pl.pallas_call(
        functools.partial(pack_x, yz),
        out_shape=(f32(SIDE, W, LANES), f32(SIDE, W, LANES), f32(W, W, LANES), f32(yz, 1, LANES)),
        name="pack_x",
    )(t, diffusivity, b, v, rho)
    from_lo, from_hi = exchange(bwd, fwd, "gx")
    low = lax.all_to_all(low, ("gy", "gz"), 0, 0, tiled=True)
    low = jnp.broadcast_to(jnp.min(low, axis=0, keepdims=True), (xs, 1, LANES))
    own = (t, kappa, b, v, rho)
    left, right = pl.pallas_call(
        pack_z,
        out_shape=(f32(ZT, W, LANES), f32(ZT, W, LANES)),
        name="pack_z",
    )(from_lo, from_hi, *own)
    g_left, g_right = exchange(left, right, "gz")
    fwd, bwd = pl.pallas_call(
        pack_y,
        out_shape=(f32(YT, W, LANES), f32(YT, W, LANES)),
        name="pack_y",
    )(from_lo, from_hi, *own, g_left, g_right)
    y_lo, y_hi = exchange(bwd, fwd, "gy")
    low = lax.all_to_all(low, "gx", 0, 0, tiled=True)
    scratch = [
        pltpu.VMEM((FULL, XE, ROWS, LANES), jnp.float32),
        pltpu.VMEM((AUX, XA, ROWS, LANES), jnp.float32),
        pltpu.VMEM((9, XE, ROWS, LANES), jnp.float32),
        pltpu.VMEM((XE, ROWS, LANES), jnp.float32),
        pltpu.VMEM((XE, ROWS, LANES), jnp.float32),
        pltpu.VMEM((12, XA, ROWS, LANES), jnp.float32),
        pltpu.VMEM((3, XA, ROWS, LANES), jnp.float32),
        pltpu.VMEM((3, XA, ROWS, LANES), jnp.float32),
    ]
    return pl.pallas_call(
        advance,
        out_shape=(f32(W, W, LANES), f32(3, W, W, LANES)),
        scratch_shapes=scratch,
        name="advance",
    )(from_lo, from_hi, *own, g_left, g_right, y_lo, y_hi, low)


def solution(mesh):
    cell = P("gx", "gy", "gz")
    face = P(None, "gx", "gy", "gz")
    return jax.shard_map(
        on_device,
        mesh=mesh,
        in_specs=(cell, cell, face, face, cell),
        out_specs=(cell, face),
        check_vma=False,
    )
```

time: 280 us -> 124 us (0.44)
  the two profiles are of different devices: /device:TPU:57 before, /device:TPU:1 now
where the time goes in v1:
time: 124 us; the launch traced here: 123 us
  blocking collectives  46.1 us (37%)
  Pallas kernels  39.8 us (32%)
  starting transfers between devices  27.8 us (22%)
  waiting for transfers between devices  5.31 us (4%)
  local copies, waits for them, and re-layouts  3.59 us (3%)
    all_to_all x1, blocking collectives, on_device(): low = lax.all_to_all(low, 'gx', 0, 0, tiled=True)  36.2 us
    pallas_call x1, Pallas kernels, on_device(): pl.pallas_call(advance, out_shape=(f32(W, W, LANES), f32(3, W, W, LANES))...  33.4 us
    ppermute x3, starting transfers between devices, exchange(): from_high = lax.ppermute(low_going, axis, backward)  18.4 us
    all_to_all x1, blocking collectives, on_device(): low = lax.all_to_all(low, ('gy', 'gz'), 0, 0, tiled=True)  9.87 us
    ppermute x3, starting transfers between devices, exchange(): from_low = lax.ppermute(high_going, axis, forward)  9.45 us
    ppermute x3, waiting for transfers between devices, exchange(): from_low = lax.ppermute(high_going, axis, forward)  4.07 us
    unnamed x14, local copies, waits for them, and re-layouts  3.57 us
  transfers between devices with their start and end apart: 6, of which 2 were waited for; matrix products, arithmetic and copies ran while one was open for 0% of the time, Pallas kernels for 0%

profile of v1, /device:TPU:1, one launch (start us, length us, event | category | flops | bytes accessed | tf_op | source)
XLA Modules:
  0.0 123.4 jit_solution(12486237855820771906)
XLA Ops:
  0.6 1.8 %pack_x.1 = (f32[48,8,128]{2,1,0:T(8,128)}, f32[48,8,128]{2,1,0:T(8,128)}, f32[8,8,128]{2,1,0:T(8,128)}, f32[16,1,128]{2,1,0:T(1,128)}) custom-call(f32[8,8,128]{2,1,0:T(8,128)} %t_ref.7, f32[8,8,128]{2,1,0:T(8,128)} %d_ref.1, f32[3,8,8,128]{3,2,1,0:T(8,128)} %b_ref.7, f32[3,8,8,128]{3,2,1,0:T(8,128)} %v_ref.7, f32[8,8,128]{2,1,0:T(8,128)} %r_ref.7), custom_call_target="tpu_custom_call" | custom-call | tf_op jit(solution)/shard_map/pack_x/pallas_call | solution.py:363
  2.4 4.6 %collective-permute-start = (f32[48,8,128]{2,1,0:T(8,128)}, f32[48,8,128]{2,1,0:T(8,128)S(1)}, u32[]{:S(2)}, u32[]{:S(2)}) collective-permute-start(f32[48,8,128]{2,1,0:T(8,128)} %get-tuple-element.10), channel_id=1, source_target_pairs={{0,16},{16,32},{32,48},{48,64},{64,80},{80,96},{96,112},{112,128},... | collective-permute-start | bytes 589832 | tf_op jit(solution)/shard_map/ppermute | solution.py:351
  7.0 9.7 %collective-permute-start.1 = (f32[48,8,128]{2,1,0:T(8,128)}, f32[48,8,128]{2,1,0:T(8,128)S(1)}, u32[]{:S(2)}, u32[]{:S(2)}) collective-permute-start(f32[48,8,128]{2,1,0:T(8,128)} %get-tuple-element.11), channel_id=1, source_target_pairs={{16,0},{32,16},{48,32},{64,48},{80,64},{96,80},{112,96},{128,112},... | collective-permute-start | bytes 589832 | tf_op jit(solution)/shard_map/ppermute | solution.py:352
  16.7 0.0 collective-permute-done.lo_ref
  16.7 0.0 copy-start
  16.7 1.2 %collective-permute-done.1.hi_ref = f32[48,8,128]{2,1,0:T(8,128)S(1)} collective-permute-done((f32[48,8,128]{2,1,0:T(8,128)}, f32[48,8,128]{2,1,0:T(8,128)S(1)}, u32[]{:S(2)}, u32[]{:S(2)}) %collective-permute-start.1) | collective-permute-done | bytes 196640 | tf_op jit(solution)/shard_map/ppermute | solution.py:352
  18.0 0.0 copy-start.1
  18.0 0.0 copy-done
  18.0 0.7 copy-done.1
  18.7 2.2 %pack_z.1 = (f32[11,8,128]{2,1,0:T(8,128)}, f32[11,8,128]{2,1,0:T(8,128)}) custom-call(f32[48,8,128]{2,1,0:T(8,128)} %copy-done, f32[48,8,128]{2,1,0:T(8,128)} %copy-done.1, f32[8,8,128]{2,1,0:T(8,128)} %t_ref.7, f32[8,8,128]{2,1,0:T(8,128)} %get-tuple-element.12.k_ref, f32[3,8,8,128]{3,2,1,0:T(8,128)} %b_ref.7, f32[3,8,8,128]{3,2,1,0:T(8,128)} %v_ref.7, ...), custom_call_target="tpu_custom_call" | custom-call | tf_op jit(solution)/shard_map/pack_z/pallas_call | solution.py:372
  20.9 1.9 %collective-permute-start.2 = (f32[11,8,128]{2,1,0:T(8,128)}, f32[11,8,128]{2,1,0:T(8,128)S(1)}, u32[]{:S(2)}, u32[]{:S(2)}) collective-permute-start(f32[11,8,128]{2,1,0:T(8,128)} %get-tuple-element.13), channel_id=1, source_target_pairs={{0,1},{1,2},{2,3},{3,0},{4,5},{5,6},{6,7},{7,4},{8,9},{9,10},{10,1... | collective-permute-start | bytes 135176 | tf_op jit(solution)/shard_map/ppermute | solution.py:351
  22.8 5.2 %collective-permute-start.3 = (f32[11,8,128]{2,1,0:T(8,128)}, f32[11,8,128]{2,1,0:T(8,128)S(1)}, u32[]{:S(2)}, u32[]{:S(2)}) collective-permute-start(f32[11,8,128]{2,1,0:T(8,128)} %get-tuple-element.14), channel_id=1, source_target_pairs={{1,0},{2,1},{3,2},{0,3},{5,4},{6,5},{7,6},{4,7},{9,8},{10,9},{11,1... | collective-permute-start | bytes 135176 | tf_op jit(solution)/shard_map/ppermute | solution.py:352
  27.9 4.1 %collective-permute-done.2.gl_ref = f32[11,8,128]{2,1,0:T(8,128)S(1)} collective-permute-done((f32[11,8,128]{2,1,0:T(8,128)}, f32[11,8,128]{2,1,0:T(8,128)S(1)}, u32[]{:S(2)}, u32[]{:S(2)}) %collective-permute-start.2) | collective-permute-done | bytes 45088 | tf_op jit(solution)/shard_map/ppermute | solution.py:351
  32.0 0.0 copy-start.4
  32.0 0.0 collective-permute-done.3.gr_ref
  32.0 0.6 copy-done.4
  32.6 0.0 copy-start.5
  32.6 0.6 copy-done.5
  33.2 0.0 copy-start.6
  33.2 2.4 %pack_y.1 = (f32[154,8,128]{2,1,0:T(8,128)}, f32[154,8,128]{2,1,0:T(8,128)}) custom-call(f32[48,8,128]{2,1,0:T(8,128)} %copy-done, f32[48,8,128]{2,1,0:T(8,128)} %copy-done.1, f32[8,8,128]{2,1,0:T(8,128)} %t_ref.7, f32[8,8,128]{2,1,0:T(8,128)} %get-tuple-element.12.k_ref, f32[3,8,8,128]{3,2,1,0:T(8,128)} %b_ref.7, f32[3,8,8,128]{3,2,1,0:T(8,128)} %v_ref.7, ...), custom_call_target="tpu_custom_call" | custom-call | tf_op jit(solution)/shard_map/pack_y/pallas_call | solution.py:378
  35.6 3.0 %collective-permute-start.4 = (f32[154,8,128]{2,1,0:T(8,128)}, f32[154,8,128]{2,1,0:T(8,128)S(1)}, u32[]{:S(2)}, u32[]{:S(2)}) collective-permute-start(f32[154,8,128]{2,1,0:T(8,128)} %get-tuple-element.15), channel_id=1, source_target_pairs={{0,4},{4,8},{8,12},{12,0},{1,5},{5,9},{9,13},{13,1},{2,6},{6,10},{... | collective-permute-start | bytes 1892360 | tf_op jit(solution)/shard_map/ppermute | solution.py:351
  38.6 3.5 %collective-permute-start.5 = (f32[154,8,128]{2,1,0:T(8,128)}, f32[154,8,128]{2,1,0:T(8,128)S(1)}, u32[]{:S(2)}, u32[]{:S(2)}) collective-permute-start(f32[154,8,128]{2,1,0:T(8,128)} %get-tuple-element.16), channel_id=1, source_target_pairs={{4,0},{8,4},{12,8},{0,12},{5,1},{9,5},{13,9},{1,13},{6,2},{10,6},{... | collective-permute-start | bytes 1892360 | tf_op jit(solution)/shard_map/ppermute | solution.py:352
  42.1 0.0 copy-done.6
  42.1 9.9 %all_to_all.10 = f32[16,1,128]{2,1,0:T(1,128)S(1)} all-to-all(f32[16,1,128]{2,1,0:T(1,128)S(1)} %copy-done.6), channel_id=1, replica_groups=mesh['gx'=48,'gy'=4,'gz'=4] {'gy','gz'}, dimensions={0} | all-to-all | bytes 16384 | tf_op jit(solution)/shard_map/all_to_all | solution.py:369
  52.0 36.2 %all_to_all.11.low_ref = f32[48,1,128]{2,1,0:T(1,128)} all-to-all(f32[48,1,128]{2,1,0:T(1,128)S(1)} %broadcast_in_dim.2), channel_id=1, replica_groups=mesh['gx'=48,'gy'=4,'gz'=4] {'gx'}, dimensions={0} | all-to-all | bytes 49152 | tf_op jit(solution)/shard_map/all_to_all | solution.py:384
  88.3 0.0 collective-permute-done.4.ly_ref
  88.3 0.0 copy-start.2
  88.3 0.0 collective-permute-done.5.hy_ref
  88.3 0.8 copy-done.2
  89.1 0.0 copy-start.3
  89.1 0.8 copy-done.3
  89.9 33.4 %advance.1 = (f32[8,8,128]{2,1,0:T(8,128)}, f32[3,8,8,128]{3,2,1,0:T(8,128)}) custom-call(f32[48,8,128]{2,1,0:T(8,128)} %copy-done, f32[48,8,128]{2,1,0:T(8,128)} %copy-done.1, f32[8,8,128]{2,1,0:T(8,128)} %t_ref.7, f32[8,8,128]{2,1,0:T(8,128)} %get-tuple-element.12.k_ref, f32[3,8,8,128]{3,2,1,0:T(8,128)} %b_ref.7, f32[3,8,8,128]{3,2,1,0:T(8,128)} %v_ref.7, ...), custom_call_target="tpu_custom_call" | custom-call | tf_op jit(solution)/shard_map/advance/pallas_call | solution.py:395
  (2 shorter events, 0.1 us)
Async XLA Ops:
  2.4 14.3 %collective-permute-start = (f32[48,8,128]{2,1,0:T(8,128)}, f32[48,8,128]{2,1,0:T(8,128)S(1)}, u32[]{:S(2)}, u32[]{:S(2)}) collective-permute-start(f32[48,8,128]{2,1,0:T(8,128)} %get-tuple-element.10), channel_id=1, source_target_pairs={{0,16},{16,32},{32,48},{48,64},{64,80},{80,96},{96,112},{112,128},... | collective-permute-start | bytes 589832 | tf_op jit(solution)/shard_map/ppermute | solution.py:351
  7.0 11.0 %collective-permute-start.1 = (f32[48,8,128]{2,1,0:T(8,128)}, f32[48,8,128]{2,1,0:T(8,128)S(1)}, u32[]{:S(2)}, u32[]{:S(2)}) collective-permute-start(f32[48,8,128]{2,1,0:T(8,128)} %get-tuple-element.11), channel_id=1, source_target_pairs={{16,0},{32,16},{48,32},{64,48},{80,64},{96,80},{112,96},{128,112},... | collective-permute-start | bytes 589832 | tf_op jit(solution)/shard_map/ppermute | solution.py:352
  16.7 1.3 %copy-start = (f32[48,8,128]{2,1,0:T(8,128)}, f32[48,8,128]{2,1,0:T(8,128)S(1)}, u32[]{:S(2)}) copy-start(f32[48,8,128]{2,1,0:T(8,128)S(1)} %collective-permute-done.lo_ref) | copy-start | bytes 589828
  18.0 0.7 copy-start.1
  20.9 11.1 %collective-permute-start.2 = (f32[11,8,128]{2,1,0:T(8,128)}, f32[11,8,128]{2,1,0:T(8,128)S(1)}, u32[]{:S(2)}, u32[]{:S(2)}) collective-permute-start(f32[11,8,128]{2,1,0:T(8,128)} %get-tuple-element.13), channel_id=1, source_target_pairs={{0,1},{1,2},{2,3},{3,0},{4,5},{5,6},{6,7},{7,4},{8,9},{9,10},{10,1... | collective-permute-start | bytes 135176 | tf_op jit(solution)/shard_map/ppermute | solution.py:351
  22.8 9.2 %collective-permute-start.3 = (f32[11,8,128]{2,1,0:T(8,128)}, f32[11,8,128]{2,1,0:T(8,128)S(1)}, u32[]{:S(2)}, u32[]{:S(2)}) collective-permute-start(f32[11,8,128]{2,1,0:T(8,128)} %get-tuple-element.14), channel_id=1, source_target_pairs={{1,0},{2,1},{3,2},{0,3},{5,4},{6,5},{7,6},{4,7},{9,8},{10,9},{11,1... | collective-permute-start | bytes 135176 | tf_op jit(solution)/shard_map/ppermute | solution.py:352
  32.0 0.6 copy-start.4
  32.6 0.6 copy-start.5
  33.2 8.9 %copy-start.6 = (f32[16,1,128]{2,1,0:T(1,128)S(1)}, f32[16,1,128]{2,1,0:T(1,128)}, u32[]{:S(2)}) copy-start(f32[16,1,128]{2,1,0:T(1,128)} %get-tuple-element.17) | copy-start | bytes 24580
  35.6 52.6 %collective-permute-start.4 = (f32[154,8,128]{2,1,0:T(8,128)}, f32[154,8,128]{2,1,0:T(8,128)S(1)}, u32[]{:S(2)}, u32[]{:S(2)}) collective-permute-start(f32[154,8,128]{2,1,0:T(8,128)} %get-tuple-element.15), channel_id=1, source_target_pairs={{0,4},{4,8},{8,12},{12,0},{1,5},{5,9},{9,13},{13,1},{2,6},{6,10},{... | collective-permute-start | bytes 1892360 | tf_op jit(solution)/shard_map/ppermute | solution.py:351
  38.6 49.7 %collective-permute-start.5 = (f32[154,8,128]{2,1,0:T(8,128)}, f32[154,8,128]{2,1,0:T(8,128)S(1)}, u32[]{:S(2)}, u32[]{:S(2)}) collective-permute-start(f32[154,8,128]{2,1,0:T(8,128)} %get-tuple-element.16), channel_id=1, source_target_pairs={{4,0},{8,4},{12,8},{0,12},{5,1},{9,5},{13,9},{1,13},{6,2},{10,6},{... | collective-permute-start | bytes 1892360 | tf_op jit(solution)/shard_map/ppermute | solution.py:352
  88.3 0.8 copy-start.2
  89.1 0.8 copy-start.3

commit v2 on v1

v2 whole, which is shorter than its diff:
```python
import jax
import jax.numpy as jnp
from jax import lax
from jax.experimental import pallas as pl
from jax.experimental.pallas import tpu as pltpu
from jax.sharding import PartitionSpec as P

SECTIONS = 8
GAMMA = 5.0 / 3.0
FACE_FLOOR = 0.25

W = 8
LANES = 128
XE = 3 * W
ROWS = 6 * W
FULL = 5
AUX = 4
AX = 2
XA = W + 2 * AX
PIECES = 16
ZT = (FULL + AUX) * W // PIECES + 1
SPARE = LANES // 2
SIDE = FULL * W + AUX * AX + 2 * ZT
YT = FULL * XE + AUX * XA // 4 + 6 * ZT
FIRST_RATE = 4.0 / (SECTIONS * SECTIONS + SECTIONS - 2)
LIMIT = (SECTIONS * SECTIONS + SECTIONS - 2) / 16.0


def lane_ids(rows):
    return lax.broadcasted_iota(jnp.int32, (rows, LANES), 1)


def lroll(u, amount):
    return pltpu.roll(u, amount % LANES, 1)


def rroll(u, amount):
    return pltpu.roll(u, amount % u.shape[0], 0)


def lowest(u):
    return jnp.min(jnp.min(u, axis=0, keepdims=True), axis=1, keepdims=True)


def neighbours(axis):
    count = lax.axis_size(axis)
    at = lax.axis_index(axis)
    return lax.rem(at + count - 1, count), lax.rem(at + 1, count)


def is_odd(axis):
    return lax.rem(lax.axis_index(axis), 2) == 1


def piece(field, plane):
    return divmod(field * W + plane, PIECES)


def pack_z(t_ref, d_ref, b_ref, v_ref, r_ref, kap_ref, out_ref):
    t = t_ref[...]
    kappa = d_ref[...] * (t * t * jnp.sqrt(t))
    kap_ref[...] = kappa
    low = lowest(jnp.min(LIMIT / kappa, axis=0))
    lane = lane_ids(W)
    left, right = [], []
    for tile in range(ZT):
        below = above = jnp.broadcast_to(low, (W, LANES))
        for k in range(PIECES):
            field, plane = divmod(tile * PIECES + k, W)
            if field >= FULL + AUX:
                break
            if field == 0:
                u = t[plane]
            elif field == 1:
                u = kappa[plane]
            elif field < FULL:
                u = b_ref[field - 2, plane]
            else:
                u = v_ref[field - FULL, plane] if field < FULL + 3 else r_ref[plane]
            here = (lane >= 8 * k) & (lane < 8 * k + 8)
            below = jnp.where(here, lroll(u, 8 * k), below)
            above = jnp.where(here, lroll(u, 8 * k - (LANES - 8)), above)
        left.append(below)
        right.append(above)
    lo, _ = neighbours("gz")
    for slot in range(out_ref.shape[0]):
        for tile in range(ZT):
            out_ref[slot, tile] = jnp.where(lo == slot, left[tile], right[tile])


def pack_x(t_ref, k_ref, b_ref, v_ref, r_ref, z_ref, a_ref, o_ref, low_ref):
    odd = is_odd("gx")
    for ref in (a_ref, o_ref):
        ref[0:W] = t_ref[...]
        ref[W : 2 * W] = k_ref[...]
        for k in range(3):
            ref[(2 + k) * W : (3 + k) * W] = b_ref[k]
    for k in range(AUX):
        at = FULL * W + k * AX
        source = v_ref.at[k] if k < 3 else r_ref
        up, down = source[W - AX : W], source[0:AX]
        a_ref[at : at + AX] = jnp.where(odd, down, up)
        o_ref[at : at + AX] = jnp.where(odd, up, down)
    lo, hi = neighbours("gz")
    at = SIDE - 2 * ZT
    for tile in range(ZT):
        left, right = z_ref[lo, tile], z_ref[hi, tile]
        for ref in (a_ref, o_ref):
            ref[at + tile] = left
            ref[at + ZT + tile] = right
    low = z_ref[0, ZT - 1]
    for slot in range(1, z_ref.shape[0]):
        low = jnp.minimum(low, z_ref[slot, ZT - 1])
    low = lowest(jnp.where(lane_ids(W) >= SPARE, low, jnp.max(low)))
    low_ref[...] = jnp.broadcast_to(low.reshape(1, 1, 1), low_ref.shape)


def pack_y(own_ref, v_ref, r_ref, xa_ref, xo_ref, gy_ref, a_ref, o_ref, aux_ref, low_ref):
    odd_x, odd_y = is_odd("gx"), is_odd("gy")

    def below(i):
        return jnp.where(odd_x, xa_ref[i], xo_ref[i])

    def above(i):
        return jnp.where(odd_x, xo_ref[i], xa_ref[i])

    for field in range(FULL):
        for plane in range(W):
            i = field * W + plane
            for part, u in enumerate((below(i), own_ref[i], above(i))):
                a_ref[field * XE + part * W + plane] = u
                o_ref[field * XE + part * W + plane] = u
    for field in range(AUX):
        for plane in range(XA):
            at = FULL * W + field * AX + plane
            if plane < AX:
                u = below(at)
            elif plane < AX + W:
                u = v_ref[field, plane - AX] if field < 3 else r_ref[plane - AX]
            else:
                u = above(at - AX - W)
            i = field * XA + plane
            aux_ref[i] = u
            tile, k = FULL * XE + i // 4, i % 4
            up, down = u[W - AX : W], u[0:AX]
            a_ref[tile, AX * k : AX * k + AX] = jnp.where(odd_y, down, up)
            o_ref[tile, AX * k : AX * k + AX] = jnp.where(odd_y, up, down)
    at = SIDE - 2 * ZT
    for i in range(2 * ZT):
        for part, u in enumerate((below(at + i), own_ref[at + i], above(at + i))):
            a_ref[YT - (6 - 2 * part) * ZT + i] = u
            o_ref[YT - (6 - 2 * part) * ZT + i] = u
    low = lowest(jnp.min(gy_ref[...], axis=0))
    low_ref[...] = jnp.broadcast_to(low.reshape(1, 1, 1), low_ref.shape)


def strips(u, left, right, k, lane):
    inner = jnp.where(lane < 32, lroll(u, 8), lroll(u, 32 - (LANES - 16)))
    edge = jnp.where(lane < 8, lroll(left, -8 * k), lroll(right, 48 - 8 * k))
    return jnp.where((lane < 8) | (lane >= 48), edge, inner)


def sweep(first, last, body, carry, by):
    trips = (last - first) // by

    def several(i, carry):
        for k in range(by):
            carry = body(first + i * by + k, carry)
        return carry

    if trips:
        carry = lax.fori_loop(0, trips, several, carry)
    for x in range(first + trips * by, last):
        carry = body(x, carry)
    return carry


def advance(
    own_ref, aux_ref, ya_ref, yo_ref, low_ref, tout_ref, bout_ref,
    us, full, aux, coef, ecoef, edge, mid,
):
    lane = lane_ids(W)
    dt = lowest(jnp.min(low_ref[...], axis=0))
    odd = is_odd("gy")

    def below(i):
        return jnp.where(odd, ya_ref[i], yo_ref[i])

    def above(i):
        return jnp.where(odd, yo_ref[i], ya_ref[i])

    def lay(put, field, plane, x, parts):
        part_x, at = divmod(x, W)
        tile, k = piece(field, at)
        z = YT - (6 - 2 * part_x) * ZT + tile
        for part, (u, get) in enumerate(zip(parts, (below, own_ref.__getitem__, above))):
            put(plane, part * W, u)
            put(plane, 3 * W + part * W, strips(u, get(z), get(z + ZT), k, lane))

    def put_field(field):
        def put(x, row, u):
            if field == 0:
                us[0, 0, x, row : row + W] = u
            else:
                full[field - 1, x, row : row + W] = u

        return put

    def put_aux(field):
        def put(i, row, u):
            aux[field, i, row : row + W] = u

        return put

    off = W - AX
    for field in range(FULL):
        for x in range(XE):
            i = field * XE + x
            lay(put_field(field), field, x, x, (below(i), own_ref[i], above(i)))
    for field in range(AUX):
        for plane in range(XA):
            i = field * XA + plane
            tile, k = FULL * XE + i // 4, i % 4

            def spread(get, k=k, tile=tile):
                return get(tile)[AX * k : AX * k + AX]

            lo = jnp.concatenate([spread(below)] * 4, axis=0)
            hi = jnp.concatenate([spread(above)] * 4, axis=0)
            lay(put_aux(field), FULL + field, plane, plane + off, (lo, aux_ref[i], hi))

    def sums(x, x_p):
        bx, by, bz = full[1, x], full[2, x], full[3, x]
        sx = bx + full[1, x_p]
        sy = by + rroll(by, -1)
        sz = bz + lroll(bz, -1)
        return bx, by, bz, sx, sy, sz

    def face(n, x, kk, bn, b1, b2):
        b1, b2 = 0.25 * b1, 0.25 * b2
        q = bn * bn + b1 * b1 + b2 * b2
        s = (0.5 * FIRST_RATE * dt) * kk / jnp.maximum(q, FACE_FLOOR) * bn
        coef[3 * n, x] = s * bn
        coef[3 * n + 1, x] = 0.25 * (s * b1)
        coef[3 * n + 2, x] = 0.25 * (s * b2)

    def faces(x, carry):
        k_m, sy_m, sz_m = carry
        kap = full[0, x]
        u = us[0, 0, x]
        us[0, 1, x] = lroll(u, -1)
        us[0, 2, x] = lroll(u, 1)
        x_p = jnp.minimum(x + 1, XE - 1)
        bx, by, bz, sx, sy, sz = sums(x, x_p)
        face(0, x, kap + k_m, bx, sy + sy_m, sz + sz_m)
        face(1, x, kap + rroll(kap, 1), by, sz + rroll(sz, 1), sx + rroll(sx, 1))
        face(2, x, kap + lroll(kap, 1), bz, sx + lroll(sx, 1), sy + lroll(sy, 1))
        return kap, sy, sz

    _, _, _, _, sy, sz = sums(0, 1)
    sweep(0, XE, faces, (full[0, 0], sy, sz), 2)

    def upper(x, carry):
        for k in range(3):
            coef[9 + k, x] = lroll(coef[6 + k, x], -1)
        return carry

    sweep(1, XE - 1, upper, 0, 4)

    source, older = us.at[0], None
    for j in range(1, SECTIONS + 1):
        target = us.at[2 - j % 2]
        grow = (2.0 * j - 1.0) / j
        back = (j - 1.0) / j

        def rolled(u, u_p, u_m):
            down = rroll(u, 1)
            return down, rroll(u, -1) - down, u_p - u_m

        def flux_x(x, du, sum_y, sum_z):
            return coef[0, x] * du + coef[1, x] * sum_y + coef[2, x] * sum_z

        def plane(x, carry, source=source, older=older, target=target, grow=grow, back=back, j=j):
            dy, dz, fx, down, new = carry
            if j < SECTIONS:
                target[1, x - 1] = lroll(new, -1)
                target[2, x - 1] = lroll(new, 1)
            u, p, m = source[0, x], source[1, x], source[2, x]
            u_p, p_p, m_p = source[0, x + 1], source[1, x + 1], source[2, x + 1]
            down_p, dy_p, dz_p = rolled(u_p, p_p, m_p)
            fx_p = flux_x(x + 1, u_p - u, dy_p + dy, dz_p + dz)
            dx = u_p - source[0, x - 1]
            dx_zp = p_p - source[1, x - 1]
            dx_zm = m_p - source[2, x - 1]
            p_down, m_down = rroll(p, 1), rroll(m, 1)
            dy_zp = rroll(p, -1) - p_down
            dy_zm = rroll(m, -1) - m_down
            fy = (
                coef[3, x] * (u - down)
                + coef[4, x] * (dz + (p_down - m_down))
                + coef[5, x] * (dx + rroll(dx, 1))
            )
            fz = coef[6, x] * (u - m) + coef[7, x] * (dx + dx_zm) + coef[8, x] * (dy + dy_zm)
            fz_p = coef[9, x] * (p - u) + coef[10, x] * (dx_zp + dx) + coef[11, x] * (dy_zp + dy)
            rate = (fx_p - fx) + (rroll(fy, -1) - fy) + (fz_p - fz)
            new = u + rate
            if j > 1:
                new = grow * new - back * older[0, x]
            if j == SECTIONS:
                b = (SECTIONS * SECTIONS + SECTIONS - 2) / (2.0 * SECTIONS * (SECTIONS + 1))
                new = (1.0 - b) * us[0, 0, x] + b * new
            target[0, x] = new
            return dy_p, dz_p, fx_p, down_p, new

        u_m, u = source[0, j - 1], source[0, j]
        _, dy_m, dz_m = rolled(u_m, source[1, j - 1], source[2, j - 1])
        down, dy, dz = rolled(u, source[1, j], source[2, j])
        fx = flux_x(j, u - u_m, dy + dy_m, dz + dz_m)
        *_, new = sweep(j, XE - j, plane, (dy, dz, fx, down, u), 2)
        if j < SECTIONS:
            target[1, XE - j - 1] = lroll(new, -1)
            target[2, XE - j - 1] = lroll(new, 1)
        source, older = target, source

    def seam(main, strip):
        high = lroll(strip, LANES - 8 - 40)
        return jnp.where(lane < 8, lroll(strip, -8), jnp.where(lane >= LANES - 8, high, main))

    for x in range(W):
        tout_ref[x] = seam(source[0, W + x, W : 2 * W], source[0, W + x, 4 * W : 5 * W])

    SPEED = 3
    for i in range(XA):
        x = i + off
        _, _, _, sx, sy, sz = sums(x, x + 1)
        field = 0.25 * (sx * sx + sy * sy + sz * sz)
        vx, vy, vz = aux[0, i], aux[1, i], aux[2, i]
        flow = jnp.sqrt(vx * vx + vy * vy + vz * vz)
        aux[SPEED, i] = flow + jnp.sqrt(GAMMA * us[0, 0, x] + field / aux[SPEED, i])

    def by_axis(u, u_m, axis):
        if axis == 0:
            return u_m
        return rroll(u, 1) if axis == 1 else lroll(u, 1)

    for i in range(1, XA):
        for c in range(3):
            a, b = (c + 1) % 3, (c + 2) % 3

            def mean(f, i=i, a=a, b=b):
                if 0 in (a, b):
                    other = a + b
                    u = aux[f, i] + aux[f, i - 1]
                else:
                    other = 2
                    u = aux[f, i]
                    u = u + by_axis(u, None, 1)
                return 0.125 * (u + by_axis(u, None, other))

            va, vb, s = mean(a), mean(b), mean(SPEED)
            ecoef[4 * c, i] = vb - s
            ecoef[4 * c + 1, i] = vb + s
            ecoef[4 * c + 2, i] = s - va
            ecoef[4 * c + 3, i] = -s - va

    def fields(get, first, last):
        for i in range(first, last):
            for c in range(3):
                a, b = (c + 1) % 3, (c + 2) % 3
                ua, ub = get(a, i), get(b, i)
                ua_b = by_axis(ua, get(a, i - 1) if b == 0 else None, b)
                ub_a = by_axis(ub, get(b, i - 1) if a == 0 else None, a)
                edge[c, i] = (ecoef[4 * c, i] * ua + ecoef[4 * c + 1, i] * ua_b) + (
                    ecoef[4 * c + 2, i] * ub + ecoef[4 * c + 3, i] * ub_a
                )

    def ahead(f, i, axis):
        if axis == 0:
            return edge[f, i + 1]
        u = edge[f, i]
        return rroll(u, -1) if axis == 1 else lroll(u, -1)

    def curl(d, i):
        e, f = (d + 1) % 3, (d + 2) % 3
        return (ahead(f, i, e) - edge[f, i]) - (ahead(e, i, f) - edge[e, i])

    fields(lambda d, i: full[1 + d, i + off], 1, XA)
    for i in range(1, XA - 1):
        for d in range(3):
            mid[d, i] = full[1 + d, i + off] - dt * curl(d, i)
    fields(lambda d, i: mid[d, i], 2, XA - 1)
    for i in range(AX, AX + W):
        for d in range(3):
            u = 0.5 * (full[1 + d, i + off] + (mid[d, i] - dt * curl(d, i)))
            bout_ref[d, i - AX] = seam(u[W : 2 * W], u[4 * W : 5 * W])


def exchange(first, second, axis):
    count = lax.axis_size(axis)
    swaps = [(i, i + 1) for i in range(0, count, 2)] + [(i + 1, i) for i in range(0, count, 2)]
    others = [((a + 1) % count, (b + 1) % count) for a, b in swaps]
    return lax.ppermute(first, axis, swaps), lax.ppermute(second, axis, others)


def f32(*shape):
    return jax.ShapeDtypeStruct(shape, jnp.float32)


def on_core(kernel, out, *args, scratch=()):
    space = pl.BlockSpec(memory_space=pltpu.VMEM)
    return pl.pallas_call(
        kernel,
        out_shape=out,
        in_specs=[space] * len(args),
        out_specs=(space,) * len(out),
        scratch_shapes=[pltpu.VMEM(shape, jnp.float32) for shape in scratch],
        name=kernel.__name__,
    )(*args)


def on_device(t, diffusivity, b, v, rho):
    xs, ys, zs = (lax.axis_size(axis) for axis in ("gx", "gy", "gz"))
    out = (f32(W, W, LANES), f32(zs, ZT, W, LANES))
    kappa, edges = on_core(pack_z, out, t, diffusivity, b, v, rho)
    edges = lax.all_to_all(edges, "gz", 0, 0, tiled=True)
    out = (f32(SIDE, W, LANES), f32(SIDE, W, LANES), f32(ys, 1, LANES))
    first, second, low = on_core(pack_x, out, t, kappa, b, v, rho, edges)
    x_first, x_second = exchange(first, second, "gx")
    low = lax.all_to_all(low, "gy", 0, 0, tiled=True)
    out = (f32(YT, W, LANES), f32(YT, W, LANES), f32(AUX * XA, W, LANES), f32(xs, 1, LANES))
    first, second, aux, low = on_core(pack_y, out, first, v, rho, x_first, x_second, low)
    y_first, y_second = exchange(first, second, "gy")
    low = lax.all_to_all(low, "gx", 0, 0, tiled=True)
    scratch = [
        (3, 3, XE, ROWS, LANES),
        (FULL - 1, XE, ROWS, LANES),
        (AUX, XA, ROWS, LANES),
        (12, XE, ROWS, LANES),
        (12, XA, ROWS, LANES),
        (3, XA, ROWS, LANES),
        (3, XA, ROWS, LANES),
    ]
    out = (f32(W, W, LANES), f32(3, W, W, LANES))
    return on_core(advance, out, first, aux, y_first, y_second, low, scratch=scratch)


def solution(mesh):
    cell = P("gx", "gy", "gz")
    face = P(None, "gx", "gy", "gz")
    return jax.shard_map(
        on_device,
        mesh=mesh,
        in_specs=(cell, cell, face, face, cell),
        out_specs=(cell, face),
        check_vma=False,
    )
```

time: 124 us -> 96 us (0.77)
  Pallas kernels: 39.8 us -> 26.9 us
  starting transfers between devices: 27.8 us -> 21.4 us
  waiting for transfers between devices: 5.31 us -> 0.01 us
  blocking collectives: 46.1 us -> 44 us
    all_to_all x1, blocking collectives: 36.2 us -> 23.2 us  [on_device(): low = lax.all_to_all(low, 'gx', 0, 0, tiled=True)]
    pallas_call x4, Pallas kernels: 39.8 us -> 26.9 us  [on_core(): pl.pallas_call(kernel, out_shape=out, in_specs=[space] * len(args), out_s...]
    all_to_all x1 -> x2, blocking collectives: 9.87 us -> 20.8 us  [the longest x1 12.5 us: on_device(): edges = lax.all_to_all(edges, 'gz', 0, 0, tiled=True)]
    ppermute x6 -> x4, starting transfers between devices: 27.8 us -> 21.4 us  [the longest x2 13.5 us: exchange(): lax.ppermute(first, axis, swaps)]
    ppermute x6 -> x4, waiting for transfers between devices: 5.31 us -> 0.01 us  [the longest x2 0.01 us: exchange(): lax.ppermute(second, axis, others)]
    unnamed x14 -> x10, local copies, waits for them, and re-layouts: 3.57 us -> 2.46 us
  transfers between devices with their start and end apart: 6 -> 4, of which waited for: 2 -> 0; matrix products, arithmetic and copies ran while one was open for 0% -> 0% of each run, Pallas kernels for 0% -> 0%
where the time goes in v2:
time: 96 us; the launch traced here: 95.5 us
  blocking collectives  44 us (46%)
  Pallas kernels  26.9 us (28%)
  starting transfers between devices  21.4 us (22%)
  local copies, waits for them, and re-layouts  2.46 us (3%)
    pallas_call x4, Pallas kernels, on_core(): pl.pallas_call(kernel, out_shape=out, in_specs=[space] * len(args), out_s...  26.9 us
    all_to_all x1, blocking collectives, on_device(): low = lax.all_to_all(low, 'gx', 0, 0, tiled=True)  23.2 us
    ppermute x2, starting transfers between devices, exchange(): lax.ppermute(first, axis, swaps)  13.5 us
    all_to_all x1, blocking collectives, on_device(): edges = lax.all_to_all(edges, 'gz', 0, 0, tiled=True)  12.5 us
    all_to_all x1, blocking collectives, on_device(): low = lax.all_to_all(low, 'gy', 0, 0, tiled=True)  8.24 us
    ppermute x2, starting transfers between devices, exchange(): lax.ppermute(second, axis, others)  7.91 us
    unnamed x10, local copies, waits for them, and re-layouts  2.46 us
  transfers between devices with their start and end apart: 4, of which 0 were waited for; matrix products, arithmetic and copies ran while one was open for 0% of the time, Pallas kernels for 0%

profile of v2, /device:TPU:1, one launch (start us, length us, event | category | flops | bytes accessed | tf_op | source)
XLA Modules:
  0.0 95.5 jit_solution(8422463185828942189)
XLA Ops:
  0.6 1.9 %pack_z.1 = (f32[8,8,128]{2,1,0:T(8,128)}, f32[4,5,8,128]{3,2,1,0:T(8,128)}) custom-call(f32[8,8,128]{2,1,0:T(8,128)} %t_ref.3, f32[8,8,128]{2,1,0:T(8,128)} %d_ref.1, f32[3,8,8,128]{3,2,1,0:T(8,128)} %b_ref.3, f32[3,8,8,128]{3,2,1,0:T(8,128)} %v_ref.5, f32[8,8,128]{2,1,0:T(8,128)} %r_ref.5), custom_call_target="tpu_custom_call" | custom-call | tf_op jit(solution)/shard_map/pack_z/pallas_call | solution.py:411
  2.5 12.5 %all_to_all.15.z_ref = f32[4,5,8,128]{3,2,1,0:T(8,128)} all-to-all(f32[4,5,8,128]{3,2,1,0:T(8,128)} %get-tuple-element.12), channel_id=1, replica_groups=mesh['gx'=48,'gy'=4,'gz'=4] {'gz'}, dimensions={0} | all-to-all | bytes 163840 | tf_op jit(solution)/shard_map/all_to_all | solution.py:425
  15.0 2.0 %pack_x.1 = (f32[58,8,128]{2,1,0:T(8,128)}, f32[58,8,128]{2,1,0:T(8,128)}, f32[4,1,128]{2,1,0:T(1,128)}) custom-call(f32[8,8,128]{2,1,0:T(8,128)} %t_ref.3, f32[8,8,128]{2,1,0:T(8,128)} %get-tuple-element.11.k_ref, f32[3,8,8,128]{3,2,1,0:T(8,128)} %b_ref.3, f32[3,8,8,128]{3,2,1,0:T(8,128)} %v_ref.5, f32[8,8,128]{2,1,0:T(8,128)} %r_ref.5, ...), custom_call_target="tpu_custom_call" | custom-call | tf_op jit(solution)/shard_map/pack_x/pallas_call | solution.py:411
  17.0 0.0 copy-start.4
  17.0 5.3 %collective-permute-start.1 = (f32[58,8,128]{2,1,0:T(8,128)}, f32[58,8,128]{2,1,0:T(8,128)S(1)}, u32[]{:S(2)}, u32[]{:S(2)}) collective-permute-start(f32[58,8,128]{2,1,0:T(8,128)} %get-tuple-element.14), channel_id=1, source_target_pairs={{16,32},{48,64},{80,96},{112,128},{144,160},{176,192},{208,224},{2... | collective-permute-start | bytes 712712 | tf_op jit(solution)/shard_map/ppermute | solution.py:402
  22.3 11.6 %collective-permute-start = (f32[58,8,128]{2,1,0:T(8,128)}, f32[58,8,128]{2,1,0:T(8,128)S(1)}, u32[]{:S(2)}, u32[]{:S(2)}) collective-permute-start(f32[58,8,128]{2,1,0:T(8,128)} %get-tuple-element.13.own_ref), channel_id=1, source_target_pairs={{0,16},{32,48},{64,80},{96,112},{128,144},{160,176},{192,208},{224... | collective-permute-start | bytes 712712 | tf_op jit(solution)/shard_map/ppermute | solution.py:402
  33.9 0.0 copy-done.4
  33.9 8.2 %all_to_all.16.gy_ref = f32[4,1,128]{2,1,0:T(1,128)} all-to-all(f32[4,1,128]{2,1,0:T(1,128)S(1)} %copy-done.4), channel_id=1, replica_groups=mesh['gx'=48,'gy'=4,'gz'=4] {'gy'}, dimensions={0} | all-to-all | bytes 4096 | tf_op jit(solution)/shard_map/all_to_all | solution.py:429
  42.2 0.0 collective-permute-done.1.xo_ref
  42.2 0.0 copy-start.2
  42.2 0.0 collective-permute-done.xa_ref
  42.2 0.7 copy-done.2
  42.9 0.0 copy-start.3
  42.9 0.7 copy-done.3
  43.6 2.5 %pack_y.1 = (f32[162,8,128]{2,1,0:T(8,128)}, f32[162,8,128]{2,1,0:T(8,128)}, f32[48,8,128]{2,1,0:T(8,128)}, f32[48,1,128]{2,1,0:T(1,128)}) custom-call(f32[58,8,128]{2,1,0:T(8,128)} %get-tuple-element.13.own_ref, f32[3,8,8,128]{3,2,1,0:T(8,128)} %v_ref.5, f32[8,8,128]{2,1,0:T(8,128)} %r_ref.5, f32[58,8,128]{2,1,0:T(8,128)} %copy-done.3, ...), custom_call_target="tpu_custom_call" | custom-call | tf_op jit(solution)/shard_map/pack_y/pallas_call | solution.py:411
  46.0 2.6 %collective-permute-start.3 = (f32[162,8,128]{2,1,0:T(8,128)}, f32[162,8,128]{2,1,0:T(8,128)S(1)}, u32[]{:S(2)}, u32[]{:S(2)}) collective-permute-start(f32[162,8,128]{2,1,0:T(8,128)} %get-tuple-element.18), channel_id=1, source_target_pairs={{4,8},{12,0},{8,4},{0,12},{5,9},{13,1},{9,5},{1,13},{6,10},{14,2},... | collective-permute-start | bytes 1990664 | tf_op jit(solution)/shard_map/ppermute | solution.py:402
  48.7 1.9 %collective-permute-start.2 = (f32[162,8,128]{2,1,0:T(8,128)}, f32[162,8,128]{2,1,0:T(8,128)S(1)}, u32[]{:S(2)}, u32[]{:S(2)}) collective-permute-start(f32[162,8,128]{2,1,0:T(8,128)} %get-tuple-element.16.own_ref), channel_id=1, source_target_pairs={{0,4},{8,12},{4,0},{12,8},{1,5},{9,13},{5,1},{13,9},{2,6},{10,14},... | collective-permute-start | bytes 1990664 | tf_op jit(solution)/shard_map/ppermute | solution.py:402
  50.6 23.2 %all_to_all.17.low_ref = f32[48,1,128]{2,1,0:T(1,128)} all-to-all(f32[48,1,128]{2,1,0:T(1,128)} %get-tuple-element.19), channel_id=1, replica_groups=mesh['gx'=48,'gy'=4,'gz'=4] {'gx'}, dimensions={0} | all-to-all | bytes 49152 | tf_op jit(solution)/shard_map/all_to_all | solution.py:433
  73.8 0.0 collective-permute-done.3.yo_ref
  73.8 0.0 copy-start
  73.8 0.0 collective-permute-done.2.ya_ref
  73.8 0.0 copy-start.1
  73.8 0.8 copy-done
  74.6 0.2 copy-done.1
  74.8 20.6 %advance.1 = (f32[8,8,128]{2,1,0:T(8,128)}, f32[3,8,8,128]{3,2,1,0:T(8,128)}) custom-call(f32[162,8,128]{2,1,0:T(8,128)} %get-tuple-element.16.own_ref, f32[48,8,128]{2,1,0:T(8,128)} %get-tuple-element.17.aux_ref, f32[162,8,128]{2,1,0:T(8,128)} %copy-done.1, f32[162,8,128]{2,1,0:T(8,128)} %copy-done, f32[48,1,128]{2,1,0:T(1,128)} %all_to_all.17.low_ref), custom_call_target="tpu_custom_call" | custom-call | tf_op jit(solution)/shard_map/advance/pallas_call | solution.py:411
Async XLA Ops:
  17.0 16.9 %copy-start.4 = (f32[4,1,128]{2,1,0:T(1,128)S(1)}, f32[4,1,128]{2,1,0:T(1,128)}, u32[]{:S(2)}) copy-start(f32[4,1,128]{2,1,0:T(1,128)} %get-tuple-element.15) | copy-start | bytes 6148
  17.0 25.2 %collective-permute-start.1 = (f32[58,8,128]{2,1,0:T(8,128)}, f32[58,8,128]{2,1,0:T(8,128)S(1)}, u32[]{:S(2)}, u32[]{:S(2)}) collective-permute-start(f32[58,8,128]{2,1,0:T(8,128)} %get-tuple-element.14), channel_id=1, source_target_pairs={{16,32},{48,64},{80,96},{112,128},{144,160},{176,192},{208,224},{2... | collective-permute-start | bytes 712712 | tf_op jit(solution)/shard_map/ppermute | solution.py:402
  22.3 19.9 %collective-permute-start = (f32[58,8,128]{2,1,0:T(8,128)}, f32[58,8,128]{2,1,0:T(8,128)S(1)}, u32[]{:S(2)}, u32[]{:S(2)}) collective-permute-start(f32[58,8,128]{2,1,0:T(8,128)} %get-tuple-element.13.own_ref), channel_id=1, source_target_pairs={{0,16},{32,48},{64,80},{96,112},{128,144},{160,176},{192,208},{224... | collective-permute-start | bytes 712712 | tf_op jit(solution)/shard_map/ppermute | solution.py:402
  42.2 0.7 copy-start.2
  42.9 0.7 copy-start.3
  46.0 27.7 %collective-permute-start.3 = (f32[162,8,128]{2,1,0:T(8,128)}, f32[162,8,128]{2,1,0:T(8,128)S(1)}, u32[]{:S(2)}, u32[]{:S(2)}) collective-permute-start(f32[162,8,128]{2,1,0:T(8,128)} %get-tuple-element.18), channel_id=1, source_target_pairs={{4,8},{12,0},{8,4},{0,12},{5,9},{13,1},{9,5},{1,13},{6,10},{14,2},... | collective-permute-start | bytes 1990664 | tf_op jit(solution)/shard_map/ppermute | solution.py:402
  48.7 25.1 %collective-permute-start.2 = (f32[162,8,128]{2,1,0:T(8,128)}, f32[162,8,128]{2,1,0:T(8,128)S(1)}, u32[]{:S(2)}, u32[]{:S(2)}) collective-permute-start(f32[162,8,128]{2,1,0:T(8,128)} %get-tuple-element.16.own_ref), channel_id=1, source_target_pairs={{0,4},{8,12},{4,0},{12,8},{1,5},{9,13},{5,1},{13,9},{2,6},{10,14},... | collective-permute-start | bytes 1990664 | tf_op jit(solution)/shard_map/ppermute | solution.py:402
  73.8 0.8 copy-start
  73.8 1.1 %copy-start.1 = (f32[162,8,128]{2,1,0:T(8,128)}, f32[162,8,128]{2,1,0:T(8,128)S(1)}, u32[]{:S(2)}) copy-start(f32[162,8,128]{2,1,0:T(8,128)S(1)} %collective-permute-done.2.ya_ref) | copy-start | bytes 1990660

commit v3 on v2

--- a/solution.py
+++ b/solution.py
@@ -3,12 +3,14 @@
 from jax import lax
 from jax.experimental import pallas as pl
 from jax.experimental.pallas import tpu as pltpu
+from jax.sharding import Mesh
 from jax.sharding import PartitionSpec as P
 
 SECTIONS = 8
 GAMMA = 5.0 / 3.0
 FACE_FLOOR = 0.25
 
+GX = ("gx_0", "gx_1", "gx_2")
 W = 8
 LANES = 128
 XE = 3 * W
@@ -89,7 +91,7 @@
 
 
 def pack_x(t_ref, k_ref, b_ref, v_ref, r_ref, z_ref, a_ref, o_ref, low_ref):
-    odd = is_odd("gx")
+    odd = is_odd(GX)
     for ref in (a_ref, o_ref):
         ref[0:W] = t_ref[...]
         ref[W : 2 * W] = k_ref[...]
@@ -116,7 +118,7 @@
 
 
 def pack_y(own_ref, v_ref, r_ref, xa_ref, xo_ref, gy_ref, a_ref, o_ref, aux_ref, low_ref):
-    odd_x, odd_y = is_odd("gx"), is_odd("gy")
+    odd_x, odd_y = is_odd(GX), is_odd("gy")
 
     def below(i):
         return jnp.where(odd_x, xa_ref[i], xo_ref[i])
@@ -402,35 +404,42 @@
     return lax.ppermute(first, axis, swaps), lax.ppermute(second, axis, others)
 
 
-def f32(*shape):
-    return jax.ShapeDtypeStruct(shape, jnp.float32)
-
-
-def on_core(kernel, out, *args, scratch=()):
+def on_core(kernel, out, *args, scratch=(), last=False):
     space = pl.BlockSpec(memory_space=pltpu.VMEM)
+    shape = [
+        jax.ShapeDtypeStruct(o, jnp.float32) if last else pltpu.VMEM(o, jnp.float32) for o in out
+    ]
     return pl.pallas_call(
         kernel,
-        out_shape=out,
+        out_shape=shape,
         in_specs=[space] * len(args),
-        out_specs=(space,) * len(out),
+        out_specs=[space] * len(out),
         scratch_shapes=[pltpu.VMEM(shape, jnp.float32) for shape in scratch],
         name=kernel.__name__,
     )(*args)
 
 
+def held(*arrays):
+    return [pltpu.with_memory_space_constraint(a, pltpu.VMEM) for a in arrays]
+
+
 def on_device(t, diffusivity, b, v, rho):
-    xs, ys, zs = (lax.axis_size(axis) for axis in ("gx", "gy", "gz"))
-    out = (f32(W, W, LANES), f32(zs, ZT, W, LANES))
+    zs = lax.axis_size("gz")
+    outer = lax.axis_size("gx_0") * lax.axis_size("gy")
+    inner = lax.axis_size("gx_1") * lax.axis_size("gx_2")
+    out = [(W, W, LANES), (zs, ZT, W, LANES)]
     kappa, edges = on_core(pack_z, out, t, diffusivity, b, v, rho)
     edges = lax.all_to_all(edges, "gz", 0, 0, tiled=True)
-    out = (f32(SIDE, W, LANES), f32(SIDE, W, LANES), f32(ys, 1, LANES))
+    kappa, edges = held(kappa, edges)
+    out = [(SIDE, W, LANES), (SIDE, W, LANES), (outer, 1, LANES)]
     first, second, low = on_core(pack_x, out, t, kappa, b, v, rho, edges)
-    x_first, x_second = exchange(first, second, "gx")
-    low = lax.all_to_all(low, "gy", 0, 0, tiled=True)
-    out = (f32(YT, W, LANES), f32(YT, W, LANES), f32(AUX * XA, W, LANES), f32(xs, 1, LANES))
+    x_first, x_second = exchange(first, second, GX)
+    low = lax.all_to_all(low, ("gx_0", "gy"), 0, 0, tiled=True)
+    first, x_first, x_second, low = held(first, x_first, x_second, low)
+    out = [(YT, W, LANES), (YT, W, LANES), (AUX * XA, W, LANES), (inner, 1, LANES)]
     first, second, aux, low = on_core(pack_y, out, first, v, rho, x_first, x_second, low)
     y_first, y_second = exchange(first, second, "gy")
-    low = lax.all_to_all(low, "gx", 0, 0, tiled=True)
+    low = lax.all_to_all(low, ("gx_1", "gx_2"), 0, 0, tiled=True)
     scratch = [
         (3, 3, XE, ROWS, LANES),
         (FULL - 1, XE, ROWS, LANES),
@@ -440,16 +449,20 @@
         (3, XA, ROWS, LANES),
         (3, XA, ROWS, LANES),
     ]
-    out = (f32(W, W, LANES), f32(3, W, W, LANES))
-    return on_core(advance, out, first, aux, y_first, y_second, low, scratch=scratch)
+    out = [(W, W, LANES), (3, W, W, LANES)]
+    args = held(first, aux, y_first, y_second, low)
+    return tuple(on_core(advance, out, *args, scratch=scratch, last=True))
 
 
 def solution(mesh):
-    cell = P("gx", "gy", "gz")
-    face = P(None, "gx", "gy", "gz")
+    gx, gy, gz = (mesh.shape[axis] for axis in ("gx", "gy", "gz"))
+    outer = 3 if gx % 6 == 0 else 1
+    finer = Mesh(mesh.devices.reshape(outer, gx // outer // 2, 2, gy, gz), (*GX, "gy", "gz"))
+    cell = P(GX, "gy", "gz")
+    face = P(None, GX, "gy", "gz")
     return jax.shard_map(
         on_device,
-        mesh=mesh,
+        mesh=finer,
         in_specs=(cell, cell, face, face, cell),
         out_specs=(cell, face),
         check_vma=False,

time: 96 us -> 87.6 us (0.912)
  blocking collectives: 44 us -> 40 us
  Pallas kernels: 26.9 us -> 23.3 us
  local copies, waits for them, and re-layouts: 2.46 us -> 0 us
    pallas_call x4, Pallas kernels: 26.9 us -> 23.3 us  [on_core(): pl.pallas_call(kernel, out_shape=shape, in_specs=[space] * len(args), out...]
    all_to_all x2, blocking collectives: 31.4 us -> 27.7 us  [the longest x1 13.9 us: on_device(): low = lax.all_to_all(low, ('gx_0', 'gy'), 0, 0, tiled=True)]
    unnamed x10 -> x0, local copies, waits for them, and re-layouts: 2.46 us -> none
  transfers between devices with their start and end apart: 4 -> 4, of which waited for: 0 -> 1; matrix products, arithmetic and copies ran while one was open for 0% -> 0% of each run, Pallas kernels for 0% -> 0%
where the time goes in v3:
time: 87.6 us; the launch traced here: 86.3 us
  blocking collectives  40 us (46%)
  Pallas kernels  23.3 us (27%)
  starting transfers between devices  21.5 us (25%)
  waiting for transfers between devices  0.91 us (1%)
    pallas_call x4, Pallas kernels, on_core(): pl.pallas_call(kernel, out_shape=shape, in_specs=[space] * len(args), out...  23.3 us
    all_to_all x1, blocking collectives, on_device(): low = lax.all_to_all(low, ('gx_0', 'gy'), 0, 0, tiled=True)  13.9 us
    all_to_all x1, blocking collectives, on_device(): low = lax.all_to_all(low, ('gx_1', 'gx_2'), 0, 0, tiled=True)  13.8 us
    ppermute x2, starting transfers between devices, exchange(): lax.ppermute(first, axis, swaps)  13.5 us
    all_to_all x1, blocking collectives, on_device(): edges = lax.all_to_all(edges, 'gz', 0, 0, tiled=True)  12.2 us
    ppermute x2, starting transfers between devices, exchange(): lax.ppermute(second, axis, others)  7.97 us
  transfers between devices with their start and end apart: 4, of which 1 were waited for; matrix products, arithmetic and copies ran while one was open for 0% of the time, Pallas kernels for 0%

profile of v3, /device:TPU:1, one launch (start us, length us, event | category | flops | bytes accessed | tf_op | source)
XLA Modules:
  0.0 86.3 jit_solution(2042724168455763222)
XLA Ops:
  0.6 1.2 %pack_z.1 = (f32[8,8,128]{2,1,0:T(8,128)S(1)}, f32[4,5,8,128]{3,2,1,0:T(8,128)S(1)}) custom-call(f32[8,8,128]{2,1,0:T(8,128)} %t_ref.3, f32[8,8,128]{2,1,0:T(8,128)} %d_ref.1, f32[3,8,8,128]{3,2,1,0:T(8,128)} %b_ref.3, f32[3,8,8,128]{3,2,1,0:T(8,128)} %v_ref.5, f32[8,8,128]{2,1,0:T(8,128)} %r_ref.5), custom_call_target="tpu_custom_call" | custom-call | tf_op jit(solution)/shard_map/pack_z/pallas_call | solution.py:412
  1.8 12.2 %all_to_all.15.z_ref = f32[4,5,8,128]{3,2,1,0:T(8,128)S(1)} all-to-all(f32[4,5,8,128]{3,2,1,0:T(8,128)S(1)} %get-tuple-element.12), channel_id=1, replica_groups=mesh['gx_0'=3,'gx_1'=8,'gx_2'=2,'gy'=4,'gz'=4] {'gz'}, dimensions={0} | all-to-all | bytes 163840 | tf_op jit(solution)/shard_map/all_to_all | solution.py:432
  14.1 1.2 %pack_x.1 = (f32[58,8,128]{2,1,0:T(8,128)S(1)}, f32[58,8,128]{2,1,0:T(8,128)S(1)}, f32[12,1,128]{2,1,0:T(1,128)S(1)}) custom-call(f32[8,8,128]{2,1,0:T(8,128)} %t_ref.3, f32[8,8,128]{2,1,0:T(8,128)S(1)} %get-tuple-element.11.k_ref, f32[3,8,8,128]{3,2,1,0:T(8,128)} %b_ref.3, f32[3,8,8,128]{3,2,1,0:T(8,128)} %v_ref.5, f32[8,8,128]{2,1,0:T(8,128)} %r_ref.5, ...), custom_call_target="tpu_custom_call" | custom-call | tf_op jit(solution)/shard_map/pack_x/pallas_call | solution.py:412
  15.3 5.2 %collective-permute-start.1 = (f32[58,8,128]{2,1,0:T(8,128)S(1)}, f32[58,8,128]{2,1,0:T(8,128)S(1)}, u32[]{:S(2)}, u32[]{:S(2)}) collective-permute-start(f32[58,8,128]{2,1,0:T(8,128)S(1)} %get-tuple-element.14), channel_id=1, source_target_pairs={{16,32},{48,64},{80,96},{112,128},{144,160},{176,192},{208,224},{2... | collective-permute-start | bytes 712712 | tf_op jit(solution)/shard_map/ppermute | solution.py:404
  20.4 11.6 %collective-permute-start = (f32[58,8,128]{2,1,0:T(8,128)S(1)}, f32[58,8,128]{2,1,0:T(8,128)S(1)}, u32[]{:S(2)}, u32[]{:S(2)}) collective-permute-start(f32[58,8,128]{2,1,0:T(8,128)S(1)} %get-tuple-element.13.own_ref), channel_id=1, source_target_pairs={{0,16},{32,48},{64,80},{96,112},{128,144},{160,176},{192,208},{224... | collective-permute-start | bytes 712712 | tf_op jit(solution)/shard_map/ppermute | solution.py:404
  32.0 13.9 %all_to_all.16.gy_ref = f32[12,1,128]{2,1,0:T(1,128)S(1)} all-to-all(f32[12,1,128]{2,1,0:T(1,128)S(1)} %get-tuple-element.15), channel_id=1, replica_groups=mesh['gx_0'=3,'gx_1'=8,'gx_2'=2,'gy'=4,'gz'=4] {'gx_0','gy'}, dimensions={0} | all-to-all | bytes 12288 | tf_op jit(solution)/shard_map/all_to_all | solution.py:437
  46.0 0.0 collective-permute-done.1.xo_ref
  46.0 0.0 collective-permute-done.xa_ref
  46.0 1.9 %pack_y.1 = (f32[162,8,128]{2,1,0:T(8,128)S(1)}, f32[162,8,128]{2,1,0:T(8,128)}, f32[48,8,128]{2,1,0:T(8,128)S(1)}, f32[16,1,128]{2,1,0:T(1,128)S(1)}) custom-call(f32[58,8,128]{2,1,0:T(8,128)S(1)} %get-tuple-element.13.own_ref, f32[3,8,8,128]{3,2,1,0:T(8,128)} %v_ref.5, f32[8,8,128]{2,1,0:T(8,128)} %r_ref.5, f32[58,8,128]{2,1,0:T(8,128)S(1)} %collective-permute-done.xa_ref, ...), custom_call_target="tpu_custom_call" | custom-call | tf_op jit(solution)/shard_map/pack_y/pallas_call | solution.py:412
  47.9 2.8 %collective-permute-start.3 = (f32[162,8,128]{2,1,0:T(8,128)}, f32[162,8,128]{2,1,0:T(8,128)S(1)}, u32[]{:S(2)}, u32[]{:S(2)}) collective-permute-start(f32[162,8,128]{2,1,0:T(8,128)} %get-tuple-element.18), channel_id=1, source_target_pairs={{4,8},{12,0},{8,4},{0,12},{5,9},{13,1},{9,5},{1,13},{6,10},{14,2},... | collective-permute-start | bytes 1990664 | tf_op jit(solution)/shard_map/ppermute | solution.py:404
  50.6 1.9 %collective-permute-start.2 = (f32[162,8,128]{2,1,0:T(8,128)S(1)}, f32[162,8,128]{2,1,0:T(8,128)S(1)}, u32[]{:S(2)}, u32[]{:S(2)}) collective-permute-start(f32[162,8,128]{2,1,0:T(8,128)S(1)} %get-tuple-element.16.own_ref), channel_id=1, source_target_pairs={{0,4},{8,12},{4,0},{12,8},{1,5},{9,13},{5,1},{13,9},{2,6},{10,14},... | collective-permute-start | bytes 1990664 | tf_op jit(solution)/shard_map/ppermute | solution.py:404
  52.6 13.8 %all_to_all.17.low_ref = f32[16,1,128]{2,1,0:T(1,128)S(1)} all-to-all(f32[16,1,128]{2,1,0:T(1,128)S(1)} %get-tuple-element.19), channel_id=1, replica_groups=mesh['gx_0'=3,'gx_1'=8,'gx_2'=2,'gy'=4,'gz'=4] {'gx_1','gx_2'}, dimensions={0} | all-to-all | bytes 16384 | tf_op jit(solution)/shard_map/all_to_all | solution.py:442
  66.4 0.0 collective-permute-done.3.yo_ref
  66.4 0.9 %collective-permute-done.2.ya_ref = f32[162,8,128]{2,1,0:T(8,128)S(1)} collective-permute-done((f32[162,8,128]{2,1,0:T(8,128)S(1)}, f32[162,8,128]{2,1,0:T(8,128)S(1)}, u32[]{:S(2)}, u32[]{:S(2)}) %collective-permute-start.2) | collective-permute-done | bytes 663584 | tf_op jit(solution)/shard_map/ppermute | solution.py:404
  67.3 19.0 %advance.1 = (f32[8,8,128]{2,1,0:T(8,128)}, f32[3,8,8,128]{3,2,1,0:T(8,128)}) custom-call(f32[162,8,128]{2,1,0:T(8,128)S(1)} %get-tuple-element.16.own_ref, f32[48,8,128]{2,1,0:T(8,128)S(1)} %get-tuple-element.17.aux_ref, f32[162,8,128]{2,1,0:T(8,128)S(1)} %collective-permute-done.2.ya_ref, f32[162,8,128]{2,1,0:T(8,128)S(1)} %collective-permute-done.3.yo_ref, ...), custom_call_target="tpu_custom_call" | custom-call | tf_op jit(solution)/shard_map/advance/pallas_call | solution.py:412
Async XLA Ops:
  15.3 30.7 %collective-permute-start.1 = (f32[58,8,128]{2,1,0:T(8,128)S(1)}, f32[58,8,128]{2,1,0:T(8,128)S(1)}, u32[]{:S(2)}, u32[]{:S(2)}) collective-permute-start(f32[58,8,128]{2,1,0:T(8,128)S(1)} %get-tuple-element.14), channel_id=1, source_target_pairs={{16,32},{48,64},{80,96},{112,128},{144,160},{176,192},{208,224},{2... | collective-permute-start | bytes 712712 | tf_op jit(solution)/shard_map/ppermute | solution.py:404
  20.4 25.5 %collective-permute-start = (f32[58,8,128]{2,1,0:T(8,128)S(1)}, f32[58,8,128]{2,1,0:T(8,128)S(1)}, u32[]{:S(2)}, u32[]{:S(2)}) collective-permute-start(f32[58,8,128]{2,1,0:T(8,128)S(1)} %get-tuple-element.13.own_ref), channel_id=1, source_target_pairs={{0,16},{32,48},{64,80},{96,112},{128,144},{160,176},{192,208},{224... | collective-permute-start | bytes 712712 | tf_op jit(solution)/shard_map/ppermute | solution.py:404
  47.9 18.5 %collective-permute-start.3 = (f32[162,8,128]{2,1,0:T(8,128)}, f32[162,8,128]{2,1,0:T(8,128)S(1)}, u32[]{:S(2)}, u32[]{:S(2)}) collective-permute-start(f32[162,8,128]{2,1,0:T(8,128)} %get-tuple-element.18), channel_id=1, source_target_pairs={{4,8},{12,0},{8,4},{0,12},{5,9},{13,1},{9,5},{1,13},{6,10},{14,2},... | collective-permute-start | bytes 1990664 | tf_op jit(solution)/shard_map/ppermute | solution.py:404
  50.6 16.6 %collective-permute-start.2 = (f32[162,8,128]{2,1,0:T(8,128)S(1)}, f32[162,8,128]{2,1,0:T(8,128)S(1)}, u32[]{:S(2)}, u32[]{:S(2)}) collective-permute-start(f32[162,8,128]{2,1,0:T(8,128)S(1)} %get-tuple-element.16.own_ref), channel_id=1, source_target_pairs={{0,4},{8,12},{4,0},{12,8},{1,5},{9,13},{5,1},{13,9},{2,6},{10,14},... | collective-permute-start | bytes 1990664 | tf_op jit(solution)/shard_map/ppermute | solution.py:404

commit v4 on v3

v4 whole, which is shorter than its diff:
```python
import jax
import jax.numpy as jnp
from jax import lax
from jax.experimental import pallas as pl
from jax.experimental.pallas import tpu as pltpu
from jax.sharding import Mesh
from jax.sharding import PartitionSpec as P

SECTIONS = 8
GAMMA = 5.0 / 3.0
FACE_FLOOR = 0.25

GX = ("gx_0", "gx_1", "gx_2")
W = 8
LANES = 128
XE = 3 * W
WIDE = 4 * W
GROUPS = LANES // WIDE
XG = XE // GROUPS
LOW, HIGH = XE, XE + XG + 1
PLANES = HIGH + 1
ROWS = 3 * W
FULL = 5
AUX = 4
AX = 2
XA = W + 2 * AX
OFF = W - AX
A_LOW, A_HIGH = XA, XA + XG + 1
A_PLANES = A_HIGH + 1
ZT = (FULL + AUX) * W // 16 + 1
SPARE = LANES // 2
SIDE = FULL * W + AUX * AX + FULL + 1
A_TILES = AUX * (XA + XG)
Y_FULL = FULL * (XE + XG)
YT = Y_FULL + A_TILES // 4
FIRST_RATE = 4.0 / (SECTIONS * SECTIONS + SECTIONS - 2)
LIMIT = (SECTIONS * SECTIONS + SECTIONS - 2) / 16.0


def lane_ids(rows):
    return lax.broadcasted_iota(jnp.int32, (rows, LANES), 1)


def lroll(u, amount):
    return pltpu.roll(u, amount % LANES, 1)


def rroll(u, amount):
    return pltpu.roll(u, amount % u.shape[0], 0)


def lowest(u):
    return jnp.min(jnp.min(u, axis=0, keepdims=True), axis=1, keepdims=True)


def neighbours(axis):
    count = lax.axis_size(axis)
    at = lax.axis_index(axis)
    return lax.rem(at + count - 1, count), lax.rem(at + 1, count)


def is_odd(axis):
    return lax.rem(lax.axis_index(axis), 2) == 1


def piece(field, plane):
    return divmod(field * W + plane, 16)


def pack_z(t_ref, d_ref, b_ref, v_ref, r_ref, kap_ref, out_ref):
    t = t_ref[...]
    kappa = d_ref[...] * (t * t * jnp.sqrt(t))
    kap_ref[...] = kappa
    low = lowest(jnp.min(LIMIT / kappa, axis=0))
    lane = lane_ids(W)
    left, right = [], []
    for tile in range(ZT):
        below = above = jnp.broadcast_to(low, (W, LANES))
        for k in range(16):
            field, plane = divmod(tile * 16 + k, W)
            if field >= FULL + AUX:
                break
            if field == 0:
                u = t[plane]
            elif field == 1:
                u = kappa[plane]
            elif field < FULL:
                u = b_ref[field - 2, plane]
            else:
                u = v_ref[field - FULL, plane] if field < FULL + 3 else r_ref[plane]
            here = (lane >= 8 * k) & (lane < 8 * k + 8)
            below = jnp.where(here, lroll(u, 8 * k), below)
            above = jnp.where(here, lroll(u, 8 * k - (LANES - 8)), above)
        left.append(below)
        right.append(above)
    lo, _ = neighbours("gz")
    for slot in range(out_ref.shape[0]):
        for tile in range(ZT):
            out_ref[slot, tile] = jnp.where(lo == slot, left[tile], right[tile])


def pack_x(t_ref, k_ref, b_ref, v_ref, r_ref, z_ref, a_ref, o_ref, aux_ref, low_ref):
    odd = is_odd(GX)
    lo, hi = neighbours("gz")
    lane = lane_ids(W)
    left = [z_ref[lo, tile] for tile in range(ZT)]
    right = [z_ref[hi, tile] for tile in range(ZT)]
    up_ends = down_ends = jnp.zeros((W, LANES), jnp.float32)
    for field in range(FULL + AUX):
        ends = jnp.zeros((W, LANES), jnp.float32)
        for plane in range(W):
            if field < FULL:
                u = (t_ref, k_ref, b_ref.at[0], b_ref.at[1], b_ref.at[2])[field][plane]
            else:
                u = v_ref[field - FULL, plane] if field < FULL + 3 else r_ref[plane]
            tile, k = piece(field, plane)
            main = jnp.where(lane < 8, lroll(left[tile], -8 * k), lroll(u, 8))
            to = 16 * plane
            end = jnp.where(
                lane < to + 8, lroll(u, to + 8 - LANES), lroll(right[tile], to + 8 - 8 * k)
            )
            ends = jnp.where(lane < to, ends, end)
            if field < FULL:
                a_ref[field * W + plane] = main
                o_ref[field * W + plane] = main
                continue
            aux_ref[(field - FULL) * W + plane] = main
            at = FULL * W + (field - FULL) * AX
            if plane < AX:
                a_ref[at + plane] = main
                o_ref[at + plane] = main
            elif plane >= W - AX:
                i = at + plane - (W - AX)
                down = a_ref[i]
                a_ref[i] = jnp.where(odd, down, main)
                o_ref[i] = jnp.where(odd, main, down)
        if field < FULL:
            a_ref[FULL * W + AUX * AX + field] = ends
            o_ref[FULL * W + AUX * AX + field] = ends
        else:
            f = field - FULL
            aux_ref[AUX * W + f] = ends
            here = lane >= 32 * f
            down_ends = jnp.where(here, lroll(ends, 32 * f), down_ends)
            up_ends = jnp.where(here, lroll(ends, 32 * f - (LANES - 32)), up_ends)
    a_ref[SIDE - 1] = jnp.where(odd, down_ends, up_ends)
    o_ref[SIDE - 1] = jnp.where(odd, up_ends, down_ends)
    low = z_ref[0, ZT - 1]
    for slot in range(1, z_ref.shape[0]):
        low = jnp.minimum(low, z_ref[slot, ZT - 1])
    low = lowest(jnp.where(lane >= SPARE, low, jnp.max(low)))
    low_ref[...] = jnp.broadcast_to(low.reshape(1, 1, 1), low_ref.shape)


def pack_y(own_ref, ownaux_ref, xa_ref, xo_ref, min_ref, a_ref, o_ref, aux_ref, low_ref):
    odd_x, odd_y = is_odd(GX), is_odd("gy")
    lane = lane_ids(W)

    def below(i):
        return jnp.where(odd_x, xa_ref[i], xo_ref[i])

    def above(i):
        return jnp.where(odd_x, xo_ref[i], xa_ref[i])

    sides = (below, own_ref.__getitem__, above)

    def send(i, u):
        a_ref[i] = u
        o_ref[i] = u

    ends_at = FULL * W + AUX * AX
    for field in range(FULL):
        ends = [get(ends_at + field) for get in sides]
        mains = []
        for x in range(XE):
            part, at = divmod(x, W)
            mains.append(sides[part](field * W + at))
            send(field * XE + x, mains[x])
        for k in range(XG):
            strip = None
            for g in range(GROUPS):
                part, at = divmod(g * XG + k, W)
                to = g * WIDE
                new = jnp.where(
                    lane < to + 16,
                    lroll(mains[g * XG + k], to + 16 - LANES),
                    lroll(ends[part], to + 16 - 16 * at),
                )
                strip = jnp.where(lane < to, strip, new) if g else new
            send(FULL * XE + field * XG + k, strip)

    def put(i, u):
        aux_ref[i] = u
        tile, k = Y_FULL + i // 4, AX * (i % 4)
        up, down = u[W - AX : W], u[0:AX]
        a_ref[tile, k : k + AX] = jnp.where(odd_y, down, up)
        o_ref[tile, k : k + AX] = jnp.where(odd_y, up, down)

    outer = below(SIDE - 1), above(SIDE - 1)
    for field in range(AUX):
        mains, ends = [], []
        at = FULL * W + field * AX
        for i in range(XA):
            if i < AX:
                mains.append(below(at + i))
                ends.append((outer[0], field * AX + i))
            elif i < AX + W:
                mains.append(ownaux_ref[field * W + i - AX])
                ends.append((ownaux_ref[AUX * W + field], i - AX))
            else:
                mains.append(above(at + i - AX - W))
                ends.append((outer[1], field * AX + i - AX - W))
            put(field * XA + i, mains[i])
        for k in range(XG):
            strip = None
            for g in range(XA // XG):
                u, (end, at_end) = mains[g * XG + k], ends[g * XG + k]
                to = (g + OFF // XG) * WIDE
                new = lroll(u, to + 16 - LANES)
                strip = jnp.where(lane < to, strip, new) if g else new
                new = lroll(end, to + 16 - 16 * at_end)
                strip = jnp.where((lane >= to + 16) & (lane < to + 32), new, strip)
            put(AUX * XA + field * XG + k, strip)
    low = lowest(jnp.min(min_ref[...], axis=0))
    low_ref[...] = jnp.broadcast_to(low.reshape(1, 1, 1), low_ref.shape)


def sweep(first, last, body, carry, by):
    trips = (last - first) // by

    def several(i, carry):
        for k in range(by):
            carry = body(first + i * by + k, carry)
        return carry

    if trips:
        carry = lax.fori_loop(0, trips, several, carry)
    for x in range(first + trips * by, last):
        carry = body(x, carry)
    return carry


def advance(
    own_ref, aux_ref, ya_ref, yo_ref, low_ref, tout_ref, bout_ref,
    us, full, aux, coef, ecoef, edge, mid,
):
    lane = lane_ids(W)
    dt = lowest(jnp.min(low_ref[...], axis=0))
    odd = is_odd("gy")

    sides = (
        lambda i: jnp.where(odd, ya_ref[i], yo_ref[i]),
        own_ref.__getitem__,
        lambda i: jnp.where(odd, yo_ref[i], ya_ref[i]),
    )
    for field in range(FULL):
        to = us.at[0, 0] if field == 0 else full.at[field - 1]
        for x in range(XE + XG):
            i, plane = field * XE + x, x
            if x >= XE:
                i, plane = FULL * XE + field * XG + x - XE, x + 1
            for part in range(3):
                to[plane, part * W : part * W + W] = sides[part](i)
    for field in range(AUX):
        for x in range(XA + XG):
            i, plane = field * XA + x, x
            if x >= XA:
                i, plane = AUX * XA + field * XG + x - XA, x + 1
            tile, k = Y_FULL + i // 4, AX * (i % 4)
            for part in range(3):
                u = aux_ref[i] if part == 1 else jnp.tile(sides[part](tile)[k : k + AX], (4, 1))
                aux[field, plane, part * W : part * W + W] = u

    def beside(ref, low, high):
        ref[low] = lroll(ref[high - 1], WIDE)
        ref[high] = lroll(ref[low + 1], -WIDE)

    beside(us.at[0, 0], LOW, HIGH)
    for k in range(FULL - 1):
        beside(full.at[k], LOW, HIGH)

    def sums(x, x_p):
        bx, by, bz = full[1, x], full[2, x], full[3, x]
        sx = bx + full[1, x_p]
        sy = by + rroll(by, -1)
        sz = bz + lroll(bz, -1)
        return bx, by, bz, sx, sy, sz

    def face(n, x, kk, bn, b1, b2):
        b1, b2 = 0.25 * b1, 0.25 * b2
        q = bn * bn + b1 * b1 + b2 * b2
        s = (0.5 * FIRST_RATE * dt) * kk / jnp.maximum(q, FACE_FLOOR) * bn
        coef[3 * n, x] = s * bn
        coef[3 * n + 1, x] = 0.25 * (s * b1)
        coef[3 * n + 2, x] = 0.25 * (s * b2)

    def faces(x, carry):
        k_m, sy_m, sz_m = carry
        kap = full[0, x]
        u = us[0, 0, x]
        us[0, 1, x] = lroll(u, -1)
        us[0, 2, x] = lroll(u, 1)
        x_p = jnp.minimum(x + 1, PLANES - 1)
        bx, by, bz, sx, sy, sz = sums(x, x_p)
        face(0, x, kap + k_m, bx, sy + sy_m, sz + sz_m)
        face(1, x, kap + rroll(kap, 1), by, sz + rroll(sz, 1), sx + rroll(sx, 1))
        face(2, x, kap + lroll(kap, 1), bz, sx + lroll(sx, 1), sy + lroll(sy, 1))
        return kap, sy, sz

    for first, last in ((0, XE), (LOW, PLANES)):
        _, _, _, _, sy, sz = sums(first, first + 1)
        sweep(first, last, faces, (full[0, first], sy, sz), 4)

    def upper(x, carry):
        for k in range(3):
            coef[9 + k, x] = lroll(coef[6 + k, x], -1)
        return carry

    sweep(0, PLANES, upper, 0, 8)

    source, older = us.at[0], None
    for j in range(1, SECTIONS + 1):
        target = us.at[2 - j % 2]
        grow = (2.0 * j - 1.0) / j
        back = (j - 1.0) / j

        def rolled(u, u_p, u_m):
            down = rroll(u, 1)
            return down, rroll(u, -1) - down, u_p - u_m

        def flux_x(x, du, sum_y, sum_z):
            return coef[0, x] * du + coef[1, x] * sum_y + coef[2, x] * sum_z

        def plane(x, carry, source=source, older=older, target=target, grow=grow, back=back, j=j):
            dy, dz, fx, down = carry
            u, p, m = source[0, x], source[1, x], source[2, x]
            u_p, p_p, m_p = source[0, x + 1], source[1, x + 1], source[2, x + 1]
            down_p, dy_p, dz_p = rolled(u_p, p_p, m_p)
            fx_p = flux_x(x + 1, u_p - u, dy_p + dy, dz_p + dz)
            dx = u_p - source[0, x - 1]
            dx_zp = p_p - source[1, x - 1]
            dx_zm = m_p - source[2, x - 1]
            p_down, m_down = rroll(p, 1), rroll(m, 1)
            dy_zp = rroll(p, -1) - p_down
            dy_zm = rroll(m, -1) - m_down
            fy = (
                coef[3, x] * (u - down)
                + coef[4, x] * (dz + (p_down - m_down))
                + coef[5, x] * (dx + rroll(dx, 1))
            )
            fz = coef[6, x] * (u - m) + coef[7, x] * (dx + dx_zm) + coef[8, x] * (dy + dy_zm)
            fz_p = coef[9, x] * (p - u) + coef[10, x] * (dx_zp + dx) + coef[11, x] * (dy_zp + dy)
            rate = (fx_p - fx) + (rroll(fy, -1) - fy) + (fz_p - fz)
            new = u + rate
            if j > 1:
                new = grow * new - back * older[0, x]
            if j == SECTIONS:
                b = (SECTIONS * SECTIONS + SECTIONS - 2) / (2.0 * SECTIONS * (SECTIONS + 1))
                new = (1.0 - b) * us[0, 0, x] + b * new
            target[0, x] = new
            return dy_p, dz_p, fx_p, down_p

        def start(x, source=source):
            u_m, u = source[0, x - 1], source[0, x]
            _, dy_m, dz_m = rolled(u_m, source[1, x - 1], source[2, x - 1])
            down, dy, dz = rolled(u, source[1, x], source[2, x])
            return dy, dz, flux_x(x, u - u_m, dy + dy_m, dz + dz_m), down

        def turn(x, target=target):
            u = target[0, x]
            target[1, x] = lroll(u, -1)
            target[2, x] = lroll(u, 1)

        carry = start(LOW + 1)
        for x in range(LOW + 1, HIGH):
            carry = plane(x, carry)
        if j < SECTIONS:
            for x in range(LOW + 1, HIGH):
                turn(x)
            beside(target.at[0], LOW, HIGH)
            turn(LOW)
            turn(HIGH)

        def two(i, carry, target=target, plane=plane, turn=turn, j=j):
            x = j + 2 * i
            if j < SECTIONS:
                turn(jnp.maximum(x - 2, 0))
                turn(jnp.maximum(x - 1, 0))
            return plane(x + 1, plane(x, carry))

        lax.fori_loop(0, (XE - 2 * j) // 2, two, start(j))
        if j < SECTIONS:
            turn(XE - j - 2)
            turn(XE - j - 1)
        source, older = target, source

    def seam(main, strip, g):
        return jnp.where(
            lane < LANES - 16, lroll(main, -8), lroll(strip, LANES - 16 - 8 - WIDE * g)
        )

    for x in range(W):
        g, k = divmod(W + x, XG)
        tout_ref[x] = seam(source[0, W + x, W : 2 * W], source[0, LOW + 1 + k, W : 2 * W], g)

    SPEED = 3
    strip = range(A_LOW + 1, A_HIGH)

    def within(i):
        return i + OFF if i < XA else i - A_LOW + LOW

    for i in (*range(XA), *strip):
        x = within(i)
        _, _, _, sx, sy, sz = sums(x, x + 1)
        field = 0.25 * (sx * sx + sy * sy + sz * sz)
        vx, vy, vz = aux[0, i], aux[1, i], aux[2, i]
        flow = jnp.sqrt(vx * vx + vy * vy + vz * vz)
        aux[SPEED, i] = flow + jnp.sqrt(GAMMA * us[0, 0, x] + field / aux[SPEED, i])
    for k in range(AUX):
        aux[k, A_LOW] = lroll(aux[k, A_HIGH - 1], WIDE)

    def by_axis(u, u_m, axis):
        if axis == 0:
            return u_m
        return rroll(u, 1) if axis == 1 else lroll(u, 1)

    for i in (*range(1, XA), *strip):
        for c in range(3):
            a, b = (c + 1) % 3, (c + 2) % 3

            def mean(f, i=i, a=a, b=b):
                if 0 in (a, b):
                    other = a + b
                    u = aux[f, i] + aux[f, i - 1]
                else:
                    other = 2
                    u = aux[f, i]
                    u = u + by_axis(u, None, 1)
                return 0.125 * (u + by_axis(u, None, other))

            va, vb, s = mean(a), mean(b), mean(SPEED)
            ecoef[4 * c, i] = vb - s
            ecoef[4 * c + 1, i] = vb + s
            ecoef[4 * c + 2, i] = s - va
            ecoef[4 * c + 3, i] = -s - va

    def fields(get, first, last):
        for i in (*range(first, last), *strip):
            for c in range(3):
                a, b = (c + 1) % 3, (c + 2) % 3
                ua, ub = get(a, i), get(b, i)
                ua_b = by_axis(ua, get(a, i - 1) if b == 0 else None, b)
                ub_a = by_axis(ub, get(b, i - 1) if a == 0 else None, a)
                edge[c, i] = (ecoef[4 * c, i] * ua + ecoef[4 * c + 1, i] * ua_b) + (
                    ecoef[4 * c + 2, i] * ub + ecoef[4 * c + 3, i] * ub_a
                )
        for c in range(1, 3):
            edge[c, A_HIGH] = lroll(edge[c, A_LOW + 1], -WIDE)

    def ahead(f, i, axis):
        if axis == 0:
            return edge[f, i + 1]
        u = edge[f, i]
        return rroll(u, -1) if axis == 1 else lroll(u, -1)

    def curl(d, i):
        e, f = (d + 1) % 3, (d + 2) % 3
        return (ahead(f, i, e) - edge[f, i]) - (ahead(e, i, f) - edge[e, i])

    fields(lambda d, i: full[1 + d, within(i)], 1, XA)
    for i in (*range(1, XA - 1), *strip):
        for d in range(3):
            mid[d, i] = full[1 + d, within(i)] - dt * curl(d, i)
    for d in range(1, 3):
        mid[d, A_LOW] = lroll(mid[d, A_HIGH - 1], WIDE)
    fields(lambda d, i: mid[d, i], 2, XA - 1)

    def final(d, i):
        u = 0.5 * (full[1 + d, within(i)] + (mid[d, i] - dt * curl(d, i)))
        return u[W : 2 * W]

    for d in range(3):
        ends = [final(d, i) for i in strip]
        for x in range(W):
            g, k = divmod(W + x, XG)
            bout_ref[d, x] = seam(final(d, x + AX), ends[k], g)


def exchange(first, second, axis):
    count = lax.axis_size(axis)
    swaps = [(i, i + 1) for i in range(0, count, 2)] + [(i + 1, i) for i in range(0, count, 2)]
    others = [((a + 1) % count, (b + 1) % count) for a, b in swaps]
    return lax.ppermute(first, axis, swaps), lax.ppermute(second, axis, others)


def on_core(kernel, out, *args, scratch=(), last=False):
    space = pl.BlockSpec(memory_space=pltpu.VMEM)
    shape = [
        jax.ShapeDtypeStruct(o, jnp.float32) if last else pltpu.VMEM(o, jnp.float32) for o in out
    ]
    return pl.pallas_call(
        kernel,
        out_shape=shape,
        in_specs=[space] * len(args),
        out_specs=[space] * len(out),
        scratch_shapes=[pltpu.VMEM(shape, jnp.float32) for shape in scratch],
        name=kernel.__name__,
    )(*args)


def held(*arrays):
    return [pltpu.with_memory_space_constraint(a, pltpu.VMEM) for a in arrays]


def on_device(t, diffusivity, b, v, rho):
    zs = lax.axis_size("gz")
    outer = lax.axis_size("gx_0") * lax.axis_size("gy")
    inner = lax.axis_size("gx_1") * lax.axis_size("gx_2")
    out = [(W, W, LANES), (zs, ZT, W, LANES)]
    kappa, edges = on_core(pack_z, out, t, diffusivity, b, v, rho)
    edges = lax.all_to_all(edges, "gz", 0, 0, tiled=True)
    kappa, edges = held(kappa, edges)
    out = [(SIDE, W, LANES)] * 2 + [((W + 1) * AUX, W, LANES), (outer, 1, LANES)]
    first, second, aux, low = on_core(pack_x, out, t, kappa, b, v, rho, edges)
    x_first, x_second = exchange(first, second, GX)
    low = lax.all_to_all(low, ("gx_0", "gy"), 0, 0, tiled=True)
    args = held(first, aux, x_first, x_second, low)
    out = [(YT, W, LANES)] * 2 + [(A_TILES, W, LANES), (inner, 1, LANES)]
    first, second, aux, low = on_core(pack_y, out, *args)
    y_first, y_second = exchange(first, second, "gy")
    low = lax.all_to_all(low, ("gx_1", "gx_2"), 0, 0, tiled=True)
    scratch = [
        (3, 3, PLANES, ROWS, LANES),
        (FULL - 1, PLANES, ROWS, LANES),
        (AUX, A_PLANES, ROWS, LANES),
        (12, PLANES, ROWS, LANES),
        (12, A_PLANES, ROWS, LANES),
        (3, A_PLANES, ROWS, LANES),
        (3, A_PLANES, ROWS, LANES),
    ]
    out = [(W, W, LANES), (3, W, W, LANES)]
    args = held(first, aux, y_first, y_second, low)
    return tuple(on_core(advance, out, *args, scratch=scratch, last=True))


def solution(mesh):
    gx, gy, gz = (mesh.shape[axis] for axis in ("gx", "gy", "gz"))
    outer = 3 if gx % 6 == 0 else 1
    finer = Mesh(mesh.devices.reshape(outer, gx // outer // 2, 2, gy, gz), (*GX, "gy", "gz"))
    cell = P(GX, "gy", "gz")
    face = P(None, GX, "gy", "gz")
    return jax.shard_map(
        on_device,
        mesh=finer,
        in_specs=(cell, cell, face, face, cell),
        out_specs=(cell, face),
        check_vma=False,
    )
```

time: 87.6 us -> 86.8 us (level)
  Pallas kernels: 23.3 us -> 22 us
    pallas_call x4, Pallas kernels: 23.3 us -> 22 us  [on_core(): pl.pallas_call(kernel, out_shape=shape, in_specs=[space] * len(args), out...]
  transfers between devices with their start and end apart: 4 -> 4, of which waited for: 1 -> 2; matrix products, arithmetic and copies ran while one was open for 0% -> 0% of each run, Pallas kernels for 0% -> 0%
where the time goes in v4:
time: 86.8 us; the launch traced here: 85.5 us
  blocking collectives  40 us (46%)
  Pallas kernels  22 us (25%)
  starting transfers between devices  21.5 us (25%)
  waiting for transfers between devices  1.43 us (2%)
    pallas_call x4, Pallas kernels, on_core(): pl.pallas_call(kernel, out_shape=shape, in_specs=[space] * len(args), out...  22 us
    all_to_all x1, blocking collectives, on_device(): low = lax.all_to_all(low, ('gx_0', 'gy'), 0, 0, tiled=True)  13.9 us
    all_to_all x1, blocking collectives, on_device(): low = lax.all_to_all(low, ('gx_1', 'gx_2'), 0, 0, tiled=True)  13.8 us
    ppermute x2, starting transfers between devices, exchange(): lax.ppermute(first, axis, swaps)  13.5 us
    all_to_all x1, blocking collectives, on_device(): edges = lax.all_to_all(edges, 'gz', 0, 0, tiled=True)  12.2 us
    ppermute x2, starting transfers between devices, exchange(): lax.ppermute(second, axis, others)  7.98 us
  transfers between devices with their start and end apart: 4, of which 2 were waited for; matrix products, arithmetic and copies ran while one was open for 0% of the time, Pallas kernels for 0%

profile of v4, /device:TPU:1, one launch (start us, length us, event | category | flops | bytes accessed | tf_op | source)
XLA Modules:
  0.0 85.5 jit_solution(9729994940596157777)
XLA Ops:
  0.6 1.2 %pack_z.1 = (f32[8,8,128]{2,1,0:T(8,128)S(1)}, f32[4,5,8,128]{3,2,1,0:T(8,128)S(1)}) custom-call(f32[8,8,128]{2,1,0:T(8,128)} %t_ref.3, f32[8,8,128]{2,1,0:T(8,128)} %d_ref.1, f32[3,8,8,128]{3,2,1,0:T(8,128)} %b_ref.3, f32[3,8,8,128]{3,2,1,0:T(8,128)} %v_ref.3, f32[8,8,128]{2,1,0:T(8,128)} %r_ref.3), custom_call_target="tpu_custom_call" | custom-call | tf_op jit(solution)/shard_map/pack_z/pallas_call | solution.py:501
  1.8 12.2 %all_to_all.15.z_ref = f32[4,5,8,128]{3,2,1,0:T(8,128)S(1)} all-to-all(f32[4,5,8,128]{3,2,1,0:T(8,128)S(1)} %get-tuple-element.13), channel_id=1, replica_groups=mesh['gx_0'=3,'gx_1'=8,'gx_2'=2,'gy'=4,'gz'=4] {'gz'}, dimensions={0} | all-to-all | bytes 163840 | tf_op jit(solution)/shard_map/all_to_all | solution.py:521
  14.1 1.5 %pack_x.1 = (f32[54,8,128]{2,1,0:T(8,128)S(1)}, f32[54,8,128]{2,1,0:T(8,128)S(1)}, f32[36,8,128]{2,1,0:T(8,128)S(1)}, f32[12,1,128]{2,1,0:T(1,128)S(1)}) custom-call(f32[8,8,128]{2,1,0:T(8,128)} %t_ref.3, f32[8,8,128]{2,1,0:T(8,128)S(1)} %get-tuple-element.12.k_ref, f32[3,8,8,128]{3,2,1,0:T(8,128)} %b_ref.3, f32[3,8,8,128]{3,2,1,0:T(8,128)} %v_ref.3, ...), custom_call_target="tpu_custom_call" | custom-call | tf_op jit(solution)/shard_map/pack_x/pallas_call | solution.py:501
  15.6 5.2 %collective-permute-start.1 = (f32[54,8,128]{2,1,0:T(8,128)S(1)}, f32[54,8,128]{2,1,0:T(8,128)S(1)}, u32[]{:S(2)}, u32[]{:S(2)}) collective-permute-start(f32[54,8,128]{2,1,0:T(8,128)S(1)} %get-tuple-element.16), channel_id=1, source_target_pairs={{16,32},{48,64},{80,96},{112,128},{144,160},{176,192},{208,224},{2... | collective-permute-start | bytes 663560 | tf_op jit(solution)/shard_map/ppermute | solution.py:493
  20.8 11.6 %collective-permute-start = (f32[54,8,128]{2,1,0:T(8,128)S(1)}, f32[54,8,128]{2,1,0:T(8,128)S(1)}, u32[]{:S(2)}, u32[]{:S(2)}) collective-permute-start(f32[54,8,128]{2,1,0:T(8,128)S(1)} %get-tuple-element.14.own_ref), channel_id=1, source_target_pairs={{0,16},{32,48},{64,80},{96,112},{128,144},{160,176},{192,208},{224... | collective-permute-start | bytes 663560 | tf_op jit(solution)/shard_map/ppermute | solution.py:493
  32.4 13.9 %all_to_all.16.min_ref = f32[12,1,128]{2,1,0:T(1,128)S(1)} all-to-all(f32[12,1,128]{2,1,0:T(1,128)S(1)} %get-tuple-element.17), channel_id=1, replica_groups=mesh['gx_0'=3,'gx_1'=8,'gx_2'=2,'gy'=4,'gz'=4] {'gx_0','gy'}, dimensions={0} | all-to-all | bytes 12288 | tf_op jit(solution)/shard_map/all_to_all | solution.py:526
  46.3 0.0 collective-permute-done.1.xo_ref
  46.3 0.0 collective-permute-done.xa_ref
  46.3 1.3 %pack_y.1 = (f32[168,8,128]{2,1,0:T(8,128)S(1)}, f32[168,8,128]{2,1,0:T(8,128)}, f32[72,8,128]{2,1,0:T(8,128)S(1)}, f32[16,1,128]{2,1,0:T(1,128)S(1)}) custom-call(f32[54,8,128]{2,1,0:T(8,128)S(1)} %get-tuple-element.14.own_ref, f32[36,8,128]{2,1,0:T(8,128)S(1)} %get-tuple-element.15.ownaux_ref, f32[54,8,128]{2,1,0:T(8,128)S(1)} %collective-permute-done.xa_ref, ...), custom_call_target="tpu_custom_call" | custom-call | tf_op jit(solution)/shard_map/pack_y/pallas_call | solution.py:501
  47.6 2.8 %collective-permute-start.3 = (f32[168,8,128]{2,1,0:T(8,128)}, f32[168,8,128]{2,1,0:T(8,128)S(1)}, u32[]{:S(2)}, u32[]{:S(2)}) collective-permute-start(f32[168,8,128]{2,1,0:T(8,128)} %get-tuple-element.20), channel_id=1, source_target_pairs={{4,8},{12,0},{8,4},{0,12},{5,9},{13,1},{9,5},{1,13},{6,10},{14,2},... | collective-permute-start | bytes 2064392 | tf_op jit(solution)/shard_map/ppermute | solution.py:493
  50.4 1.9 %collective-permute-start.2 = (f32[168,8,128]{2,1,0:T(8,128)S(1)}, f32[168,8,128]{2,1,0:T(8,128)S(1)}, u32[]{:S(2)}, u32[]{:S(2)}) collective-permute-start(f32[168,8,128]{2,1,0:T(8,128)S(1)} %get-tuple-element.18.own_ref), channel_id=1, source_target_pairs={{0,4},{8,12},{4,0},{12,8},{1,5},{9,13},{5,1},{13,9},{2,6},{10,14},... | collective-permute-start | bytes 2064392 | tf_op jit(solution)/shard_map/ppermute | solution.py:493
  52.3 13.8 %all_to_all.17.low_ref = f32[16,1,128]{2,1,0:T(1,128)S(1)} all-to-all(f32[16,1,128]{2,1,0:T(1,128)S(1)} %get-tuple-element.21), channel_id=1, replica_groups=mesh['gx_0'=3,'gx_1'=8,'gx_2'=2,'gy'=4,'gz'=4] {'gx_1','gx_2'}, dimensions={0} | all-to-all | bytes 16384 | tf_op jit(solution)/shard_map/all_to_all | solution.py:531
  66.1 0.3 collective-permute-done.3.yo_ref
  66.4 1.1 %collective-permute-done.2.ya_ref = f32[168,8,128]{2,1,0:T(8,128)S(1)} collective-permute-done((f32[168,8,128]{2,1,0:T(8,128)S(1)}, f32[168,8,128]{2,1,0:T(8,128)S(1)}, u32[]{:S(2)}, u32[]{:S(2)}) %collective-permute-start.2) | collective-permute-done | bytes 688160 | tf_op jit(solution)/shard_map/ppermute | solution.py:493
  67.5 18.0 %advance.1 = (f32[8,8,128]{2,1,0:T(8,128)}, f32[3,8,8,128]{3,2,1,0:T(8,128)}) custom-call(f32[168,8,128]{2,1,0:T(8,128)S(1)} %get-tuple-element.18.own_ref, f32[72,8,128]{2,1,0:T(8,128)S(1)} %get-tuple-element.19.aux_ref, f32[168,8,128]{2,1,0:T(8,128)S(1)} %collective-permute-done.2.ya_ref, f32[168,8,128]{2,1,0:T(8,128)S(1)} %collective-permute-done.3.yo_ref, ...), custom_call_target="tpu_custom_call" | custom-call | tf_op jit(solution)/shard_map/advance/pallas_call | solution.py:501
Async XLA Ops:
  15.6 30.7 %collective-permute-start.1 = (f32[54,8,128]{2,1,0:T(8,128)S(1)}, f32[54,8,128]{2,1,0:T(8,128)S(1)}, u32[]{:S(2)}, u32[]{:S(2)}) collective-permute-start(f32[54,8,128]{2,1,0:T(8,128)S(1)} %get-tuple-element.16), channel_id=1, source_target_pairs={{16,32},{48,64},{80,96},{112,128},{144,160},{176,192},{208,224},{2... | collective-permute-start | bytes 663560 | tf_op jit(solution)/shard_map/ppermute | solution.py:493
  20.8 25.5 %collective-permute-start = (f32[54,8,128]{2,1,0:T(8,128)S(1)}, f32[54,8,128]{2,1,0:T(8,128)S(1)}, u32[]{:S(2)}, u32[]{:S(2)}) collective-permute-start(f32[54,8,128]{2,1,0:T(8,128)S(1)} %get-tuple-element.14.own_ref), channel_id=1, source_target_pairs={{0,16},{32,48},{64,80},{96,112},{128,144},{160,176},{192,208},{224... | collective-permute-start | bytes 663560 | tf_op jit(solution)/shard_map/ppermute | solution.py:493
  47.6 18.8 %collective-permute-start.3 = (f32[168,8,128]{2,1,0:T(8,128)}, f32[168,8,128]{2,1,0:T(8,128)S(1)}, u32[]{:S(2)}, u32[]{:S(2)}) collective-permute-start(f32[168,8,128]{2,1,0:T(8,128)} %get-tuple-element.20), channel_id=1, source_target_pairs={{4,8},{12,0},{8,4},{0,12},{5,9},{13,1},{9,5},{1,13},{6,10},{14,2},... | collective-permute-start | bytes 2064392 | tf_op jit(solution)/shard_map/ppermute | solution.py:493
  50.4 17.2 %collective-permute-start.2 = (f32[168,8,128]{2,1,0:T(8,128)S(1)}, f32[168,8,128]{2,1,0:T(8,128)S(1)}, u32[]{:S(2)}, u32[]{:S(2)}) collective-permute-start(f32[168,8,128]{2,1,0:T(8,128)S(1)} %get-tuple-element.18.own_ref), channel_id=1, source_target_pairs={{0,4},{8,12},{4,0},{12,8},{1,5},{9,13},{5,1},{13,9},{2,6},{10,14},... | collective-permute-start | bytes 2064392 | tf_op jit(solution)/shard_map/ppermute | solution.py:493

commit v5 on v4

--- a/solution.py
+++ b/solution.py
@@ -33,6 +33,15 @@
 A_TILES = AUX * (XA + XG)
 Y_FULL = FULL * (XE + XG)
 YT = Y_FULL + A_TILES // 4
+SCRATCH = [(PLANES, ROWS, LANES)] * 9 + [
+    (FULL - 1, PLANES, ROWS, LANES),
+    (AUX, A_PLANES, ROWS, LANES),
+    (9, PLANES, ROWS, LANES),
+    (3, PLANES, ROWS, LANES),
+    (12, A_PLANES, ROWS, LANES),
+    (3, A_PLANES, ROWS, LANES),
+    (3, A_PLANES, ROWS, LANES),
+]
 FIRST_RATE = 4.0 / (SECTIONS * SECTIONS + SECTIONS - 2)
 LIMIT = (SECTIONS * SECTIONS + SECTIONS - 2) / 16.0
 
@@ -242,7 +251,7 @@
 
 def advance(
     own_ref, aux_ref, ya_ref, yo_ref, low_ref, tout_ref, bout_ref,
-    us, full, aux, coef, ecoef, edge, mid,
+    y00, y01, y02, y10, y11, y12, y20, y21, y22, full, aux, coef, coef_up, ecoef, edge, mid,
 ):
     lane = lane_ids(W)
     dt = lowest(jnp.min(low_ref[...], axis=0))
@@ -254,7 +263,7 @@
         lambda i: jnp.where(odd, yo_ref[i], ya_ref[i]),
     )
     for field in range(FULL):
-        to = us.at[0, 0] if field == 0 else full.at[field - 1]
+        to = y00 if field == 0 else full.at[field - 1]
         for x in range(XE + XG):
             i, plane = field * XE + x, x
             if x >= XE:
@@ -275,7 +284,7 @@
         ref[low] = lroll(ref[high - 1], WIDE)
         ref[high] = lroll(ref[low + 1], -WIDE)
 
-    beside(us.at[0, 0], LOW, HIGH)
+    beside(y00, LOW, HIGH)
     for k in range(FULL - 1):
         beside(full.at[k], LOW, HIGH)
 
@@ -297,9 +306,9 @@
     def faces(x, carry):
         k_m, sy_m, sz_m = carry
         kap = full[0, x]
-        u = us[0, 0, x]
-        us[0, 1, x] = lroll(u, -1)
-        us[0, 2, x] = lroll(u, 1)
+        u = y00[x]
+        y01[x] = lroll(u, -1)
+        y02[x] = lroll(u, 1)
         x_p = jnp.minimum(x + 1, PLANES - 1)
         bx, by, bz, sx, sy, sz = sums(x, x_p)
         face(0, x, kap + k_m, bx, sy + sy_m, sz + sz_m)
@@ -313,14 +322,15 @@
 
     def upper(x, carry):
         for k in range(3):
-            coef[9 + k, x] = lroll(coef[6 + k, x], -1)
+            coef_up[k, x] = lroll(coef[6 + k, x], -1)
         return carry
 
     sweep(0, PLANES, upper, 0, 8)
 
-    source, older = us.at[0], None
+    arrays = ((y00, y01, y02), (y10, y11, y12), (y20, y21, y22))
+    source, older = arrays[0], None
     for j in range(1, SECTIONS + 1):
-        target = us.at[2 - j % 2]
+        target = arrays[2 - j % 2]
         grow = (2.0 * j - 1.0) / j
         back = (j - 1.0) / j
 
@@ -333,13 +343,13 @@
 
         def plane(x, carry, source=source, older=older, target=target, grow=grow, back=back, j=j):
             dy, dz, fx, down = carry
-            u, p, m = source[0, x], source[1, x], source[2, x]
-            u_p, p_p, m_p = source[0, x + 1], source[1, x + 1], source[2, x + 1]
+            u, p, m = source[0][x], source[1][x], source[2][x]
+            u_p, p_p, m_p = source[0][x + 1], source[1][x + 1], source[2][x + 1]
             down_p, dy_p, dz_p = rolled(u_p, p_p, m_p)
             fx_p = flux_x(x + 1, u_p - u, dy_p + dy, dz_p + dz)
-            dx = u_p - source[0, x - 1]
-            dx_zp = p_p - source[1, x - 1]
-            dx_zm = m_p - source[2, x - 1]
+            dx = u_p - source[0][x - 1]
+            dx_zp = p_p - source[1][x - 1]
+            dx_zm = m_p - source[2][x - 1]
             p_down, m_down = rroll(p, 1), rroll(m, 1)
             dy_zp = rroll(p, -1) - p_down
             dy_zm = rroll(m, -1) - m_down
@@ -349,49 +359,54 @@
                 + coef[5, x] * (dx + rroll(dx, 1))
             )
             fz = coef[6, x] * (u - m) + coef[7, x] * (dx + dx_zm) + coef[8, x] * (dy + dy_zm)
-            fz_p = coef[9, x] * (p - u) + coef[10, x] * (dx_zp + dx) + coef[11, x] * (dy_zp + dy)
+            fz_p = coef_up[0, x] * (p - u) + coef_up[1, x] * (dx_zp + dx) + coef_up[2, x] * (dy_zp + dy)
             rate = (fx_p - fx) + (rroll(fy, -1) - fy) + (fz_p - fz)
             new = u + rate
             if j > 1:
-                new = grow * new - back * older[0, x]
+                new = grow * new - back * older[0][x]
             if j == SECTIONS:
                 b = (SECTIONS * SECTIONS + SECTIONS - 2) / (2.0 * SECTIONS * (SECTIONS + 1))
-                new = (1.0 - b) * us[0, 0, x] + b * new
-            target[0, x] = new
-            return dy_p, dz_p, fx_p, down_p
+                new = (1.0 - b) * y00[x] + b * new
+            target[0][x] = new
+            return (dy_p, dz_p, fx_p, down_p), new
 
         def start(x, source=source):
-            u_m, u = source[0, x - 1], source[0, x]
-            _, dy_m, dz_m = rolled(u_m, source[1, x - 1], source[2, x - 1])
-            down, dy, dz = rolled(u, source[1, x], source[2, x])
+            u_m, u = source[0][x - 1], source[0][x]
+            _, dy_m, dz_m = rolled(u_m, source[1][x - 1], source[2][x - 1])
+            down, dy, dz = rolled(u, source[1][x], source[2][x])
             return dy, dz, flux_x(x, u - u_m, dy + dy_m, dz + dz_m), down
 
-        def turn(x, target=target):
-            u = target[0, x]
-            target[1, x] = lroll(u, -1)
-            target[2, x] = lroll(u, 1)
-
+        def two(i, carry, target=target, plane=plane, j=j):
+            x = j + 2 * i
+            carry, *made = carry
+            turned = [(lroll(u, -1), lroll(u, 1)) for u in made]
+            carry, first = plane(x, carry)
+            carry, second = plane(x + 1, carry)
+            if j < SECTIONS:
+                for k, (up, down) in enumerate(turned):
+                    at = jnp.maximum(x - 2 + k, 0)
+                    target[1][at] = up
+                    target[2][at] = down
+            return carry, first, second
+
+        carry = start(j)
+        _, *made = lax.fori_loop(0, (XE - 2 * j) // 2, two, (carry, carry[3], carry[3]))
         carry = start(LOW + 1)
+        strip = []
         for x in range(LOW + 1, HIGH):
-            carry = plane(x, carry)
+            carry, new = plane(x, carry)
+            strip.append(new)
         if j < SECTIONS:
-            for x in range(LOW + 1, HIGH):
-                turn(x)
-            beside(target.at[0], LOW, HIGH)
-            turn(LOW)
-            turn(HIGH)
-
-        def two(i, carry, target=target, plane=plane, turn=turn, j=j):
-            x = j + 2 * i
-            if j < SECTIONS:
-                turn(jnp.maximum(x - 2, 0))
-                turn(jnp.maximum(x - 1, 0))
-            return plane(x + 1, plane(x, carry))
-
-        lax.fori_loop(0, (XE - 2 * j) // 2, two, start(j))
-        if j < SECTIONS:
-            turn(XE - j - 2)
-            turn(XE - j - 1)
+            for k, u in enumerate(made):
+                target[1][XE - j - 2 + k] = lroll(u, -1)
+                target[2][XE - j - 2 + k] = lroll(u, 1)
+            for at, u, by in ((HIGH, strip[0], -WIDE), (LOW, strip[-1], WIDE)):
+                target[0][at] = lroll(u, by)
+                target[1][at] = lroll(u, by - 1)
+                target[2][at] = lroll(u, by + 1)
+            for k, u in enumerate(strip):
+                target[1][LOW + 1 + k] = lroll(u, -1)
+                target[2][LOW + 1 + k] = lroll(u, 1)
         source, older = target, source
 
     def seam(main, strip, g):
@@ -401,7 +416,7 @@
 
     for x in range(W):
         g, k = divmod(W + x, XG)
-        tout_ref[x] = seam(source[0, W + x, W : 2 * W], source[0, LOW + 1 + k, W : 2 * W], g)
+        tout_ref[x] = seam(source[0][W + x, W : 2 * W], source[0][LOW + 1 + k, W : 2 * W], g)
 
     SPEED = 3
     strip = range(A_LOW + 1, A_HIGH)
@@ -415,7 +430,7 @@
         field = 0.25 * (sx * sx + sy * sy + sz * sz)
         vx, vy, vz = aux[0, i], aux[1, i], aux[2, i]
         flow = jnp.sqrt(vx * vx + vy * vy + vz * vz)
-        aux[SPEED, i] = flow + jnp.sqrt(GAMMA * us[0, 0, x] + field / aux[SPEED, i])
+        aux[SPEED, i] = flow + jnp.sqrt(GAMMA * y00[x] + field / aux[SPEED, i])
     for k in range(AUX):
         aux[k, A_LOW] = lroll(aux[k, A_HIGH - 1], WIDE)
 
@@ -529,18 +544,9 @@
     first, second, aux, low = on_core(pack_y, out, *args)
     y_first, y_second = exchange(first, second, "gy")
     low = lax.all_to_all(low, ("gx_1", "gx_2"), 0, 0, tiled=True)
-    scratch = [
-        (3, 3, PLANES, ROWS, LANES),
-        (FULL - 1, PLANES, ROWS, LANES),
-        (AUX, A_PLANES, ROWS, LANES),
-        (12, PLANES, ROWS, LANES),
-        (12, A_PLANES, ROWS, LANES),
-        (3, A_PLANES, ROWS, LANES),
-        (3, A_PLANES, ROWS, LANES),
-    ]
     out = [(W, W, LANES), (3, W, W, LANES)]
     args = held(first, aux, y_first, y_second, low)
-    return tuple(on_core(advance, out, *args, scratch=scratch, last=True))
+    return tuple(on_core(advance, out, *args, scratch=SCRATCH, last=True))
 
 
 def solution(mesh):

time: 86.8 us -> 79.5 us (0.916)
  Pallas kernels: 22 us -> 14.7 us
    pallas_call x4, Pallas kernels: 22 us -> 14.7 us  [on_core(): pl.pallas_call(kernel, out_shape=shape, in_specs=[space] * len(args), out...]
where the time goes in v5:
time: 79.5 us; the launch traced here: 78.3 us
  blocking collectives  40 us (50%)
  starting transfers between devices  21.5 us (27%)
  Pallas kernels  14.7 us (18%)
  waiting for transfers between devices  1.43 us (2%)
    pallas_call x4, Pallas kernels, on_core(): pl.pallas_call(kernel, out_shape=shape, in_specs=[space] * len(args), out...  14.7 us
    all_to_all x1, blocking collectives, on_device(): low = lax.all_to_all(low, ('gx_0', 'gy'), 0, 0, tiled=True)  13.9 us
    all_to_all x1, blocking collectives, on_device(): low = lax.all_to_all(low, ('gx_1', 'gx_2'), 0, 0, tiled=True)  13.8 us
    ppermute x2, starting transfers between devices, exchange(): lax.ppermute(first, axis, swaps)  13.5 us
    all_to_all x1, blocking collectives, on_device(): edges = lax.all_to_all(edges, 'gz', 0, 0, tiled=True)  12.2 us
    ppermute x2, starting transfers between devices, exchange(): lax.ppermute(second, axis, others)  7.98 us
  transfers between devices with their start and end apart: 4, of which 2 were waited for; matrix products, arithmetic and copies ran while one was open for 0% of the time, Pallas kernels for 0%

profile of v5, /device:TPU:1, one launch (start us, length us, event | category | flops | bytes accessed | tf_op | source)
XLA Modules:
  0.0 78.3 jit_solution(15431372328471278162)
XLA Ops:
  0.6 1.2 %pack_z.1 = (f32[8,8,128]{2,1,0:T(8,128)S(1)}, f32[4,5,8,128]{3,2,1,0:T(8,128)S(1)}) custom-call(f32[8,8,128]{2,1,0:T(8,128)} %t_ref.3, f32[8,8,128]{2,1,0:T(8,128)} %d_ref.1, f32[3,8,8,128]{3,2,1,0:T(8,128)} %b_ref.3, f32[3,8,8,128]{3,2,1,0:T(8,128)} %v_ref.3, f32[8,8,128]{2,1,0:T(8,128)} %r_ref.3), custom_call_target="tpu_custom_call" | custom-call | tf_op jit(solution)/shard_map/pack_z/pallas_call | solution.py:516
  1.8 12.2 %all_to_all.15.z_ref = f32[4,5,8,128]{3,2,1,0:T(8,128)S(1)} all-to-all(f32[4,5,8,128]{3,2,1,0:T(8,128)S(1)} %get-tuple-element.13), channel_id=1, replica_groups=mesh['gx_0'=3,'gx_1'=8,'gx_2'=2,'gy'=4,'gz'=4] {'gz'}, dimensions={0} | all-to-all | bytes 163840 | tf_op jit(solution)/shard_map/all_to_all | solution.py:536
  14.1 1.5 %pack_x.1 = (f32[54,8,128]{2,1,0:T(8,128)S(1)}, f32[54,8,128]{2,1,0:T(8,128)S(1)}, f32[36,8,128]{2,1,0:T(8,128)S(1)}, f32[12,1,128]{2,1,0:T(1,128)S(1)}) custom-call(f32[8,8,128]{2,1,0:T(8,128)} %t_ref.3, f32[8,8,128]{2,1,0:T(8,128)S(1)} %get-tuple-element.12.k_ref, f32[3,8,8,128]{3,2,1,0:T(8,128)} %b_ref.3, f32[3,8,8,128]{3,2,1,0:T(8,128)} %v_ref.3, ...), custom_call_target="tpu_custom_call" | custom-call | tf_op jit(solution)/shard_map/pack_x/pallas_call | solution.py:516
  15.6 5.2 %collective-permute-start.1 = (f32[54,8,128]{2,1,0:T(8,128)S(1)}, f32[54,8,128]{2,1,0:T(8,128)S(1)}, u32[]{:S(2)}, u32[]{:S(2)}) collective-permute-start(f32[54,8,128]{2,1,0:T(8,128)S(1)} %get-tuple-element.16), channel_id=1, source_target_pairs={{16,32},{48,64},{80,96},{112,128},{144,160},{176,192},{208,224},{2... | collective-permute-start | bytes 663560 | tf_op jit(solution)/shard_map/ppermute | solution.py:508
  20.8 11.6 %collective-permute-start = (f32[54,8,128]{2,1,0:T(8,128)S(1)}, f32[54,8,128]{2,1,0:T(8,128)S(1)}, u32[]{:S(2)}, u32[]{:S(2)}) collective-permute-start(f32[54,8,128]{2,1,0:T(8,128)S(1)} %get-tuple-element.14.own_ref), channel_id=1, source_target_pairs={{0,16},{32,48},{64,80},{96,112},{128,144},{160,176},{192,208},{224... | collective-permute-start | bytes 663560 | tf_op jit(solution)/shard_map/ppermute | solution.py:508
  32.4 13.9 %all_to_all.16.min_ref = f32[12,1,128]{2,1,0:T(1,128)S(1)} all-to-all(f32[12,1,128]{2,1,0:T(1,128)S(1)} %get-tuple-element.17), channel_id=1, replica_groups=mesh['gx_0'=3,'gx_1'=8,'gx_2'=2,'gy'=4,'gz'=4] {'gx_0','gy'}, dimensions={0} | all-to-all | bytes 12288 | tf_op jit(solution)/shard_map/all_to_all | solution.py:541
  46.3 0.0 collective-permute-done.1.xo_ref
  46.3 0.0 collective-permute-done.xa_ref
  46.3 1.3 %pack_y.1 = (f32[168,8,128]{2,1,0:T(8,128)S(1)}, f32[168,8,128]{2,1,0:T(8,128)}, f32[72,8,128]{2,1,0:T(8,128)S(1)}, f32[16,1,128]{2,1,0:T(1,128)S(1)}) custom-call(f32[54,8,128]{2,1,0:T(8,128)S(1)} %get-tuple-element.14.own_ref, f32[36,8,128]{2,1,0:T(8,128)S(1)} %get-tuple-element.15.ownaux_ref, f32[54,8,128]{2,1,0:T(8,128)S(1)} %collective-permute-done.xa_ref, ...), custom_call_target="tpu_custom_call" | custom-call | tf_op jit(solution)/shard_map/pack_y/pallas_call | solution.py:516
  47.6 2.8 %collective-permute-start.3 = (f32[168,8,128]{2,1,0:T(8,128)}, f32[168,8,128]{2,1,0:T(8,128)S(1)}, u32[]{:S(2)}, u32[]{:S(2)}) collective-permute-start(f32[168,8,128]{2,1,0:T(8,128)} %get-tuple-element.20), channel_id=1, source_target_pairs={{4,8},{12,0},{8,4},{0,12},{5,9},{13,1},{9,5},{1,13},{6,10},{14,2},... | collective-permute-start | bytes 2064392 | tf_op jit(solution)/shard_map/ppermute | solution.py:508
  50.4 1.9 %collective-permute-start.2 = (f32[168,8,128]{2,1,0:T(8,128)S(1)}, f32[168,8,128]{2,1,0:T(8,128)S(1)}, u32[]{:S(2)}, u32[]{:S(2)}) collective-permute-start(f32[168,8,128]{2,1,0:T(8,128)S(1)} %get-tuple-element.18.own_ref), channel_id=1, source_target_pairs={{0,4},{8,12},{4,0},{12,8},{1,5},{9,13},{5,1},{13,9},{2,6},{10,14},... | collective-permute-start | bytes 2064392 | tf_op jit(solution)/shard_map/ppermute | solution.py:508
  52.3 13.8 %all_to_all.17.low_ref = f32[16,1,128]{2,1,0:T(1,128)S(1)} all-to-all(f32[16,1,128]{2,1,0:T(1,128)S(1)} %get-tuple-element.21), channel_id=1, replica_groups=mesh['gx_0'=3,'gx_1'=8,'gx_2'=2,'gy'=4,'gz'=4] {'gx_1','gx_2'}, dimensions={0} | all-to-all | bytes 16384 | tf_op jit(solution)/shard_map/all_to_all | solution.py:546
  66.1 0.3 collective-permute-done.3.yo_ref
  66.4 1.1 %collective-permute-done.2.ya_ref = f32[168,8,128]{2,1,0:T(8,128)S(1)} collective-permute-done((f32[168,8,128]{2,1,0:T(8,128)S(1)}, f32[168,8,128]{2,1,0:T(8,128)S(1)}, u32[]{:S(2)}, u32[]{:S(2)}) %collective-permute-start.2) | collective-permute-done | bytes 688160 | tf_op jit(solution)/shard_map/ppermute | solution.py:508
  67.5 10.7 %advance.1 = (f32[8,8,128]{2,1,0:T(8,128)}, f32[3,8,8,128]{3,2,1,0:T(8,128)}) custom-call(f32[168,8,128]{2,1,0:T(8,128)S(1)} %get-tuple-element.18.own_ref, f32[72,8,128]{2,1,0:T(8,128)S(1)} %get-tuple-element.19.aux_ref, f32[168,8,128]{2,1,0:T(8,128)S(1)} %collective-permute-done.2.ya_ref, f32[168,8,128]{2,1,0:T(8,128)S(1)} %collective-permute-done.3.yo_ref, ...), custom_call_target="tpu_custom_call" | custom-call | tf_op jit(solution)/shard_map/advance/pallas_call | solution.py:516
Async XLA Ops:
  15.6 30.7 %collective-permute-start.1 = (f32[54,8,128]{2,1,0:T(8,128)S(1)}, f32[54,8,128]{2,1,0:T(8,128)S(1)}, u32[]{:S(2)}, u32[]{:S(2)}) collective-permute-start(f32[54,8,128]{2,1,0:T(8,128)S(1)} %get-tuple-element.16), channel_id=1, source_target_pairs={{16,32},{48,64},{80,96},{112,128},{144,160},{176,192},{208,224},{2... | collective-permute-start | bytes 663560 | tf_op jit(solution)/shard_map/ppermute | solution.py:508
  20.8 25.5 %collective-permute-start = (f32[54,8,128]{2,1,0:T(8,128)S(1)}, f32[54,8,128]{2,1,0:T(8,128)S(1)}, u32[]{:S(2)}, u32[]{:S(2)}) collective-permute-start(f32[54,8,128]{2,1,0:T(8,128)S(1)} %get-tuple-element.14.own_ref), channel_id=1, source_target_pairs={{0,16},{32,48},{64,80},{96,112},{128,144},{160,176},{192,208},{224... | collective-permute-start | bytes 663560 | tf_op jit(solution)/shard_map/ppermute | solution.py:508
  47.6 18.8 %collective-permute-start.3 = (f32[168,8,128]{2,1,0:T(8,128)}, f32[168,8,128]{2,1,0:T(8,128)S(1)}, u32[]{:S(2)}, u32[]{:S(2)}) collective-permute-start(f32[168,8,128]{2,1,0:T(8,128)} %get-tuple-element.20), channel_id=1, source_target_pairs={{4,8},{12,0},{8,4},{0,12},{5,9},{13,1},{9,5},{1,13},{6,10},{14,2},... | collective-permute-start | bytes 2064392 | tf_op jit(solution)/shard_map/ppermute | solution.py:508
  50.4 17.2 %collective-permute-start.2 = (f32[168,8,128]{2,1,0:T(8,128)S(1)}, f32[168,8,128]{2,1,0:T(8,128)S(1)}, u32[]{:S(2)}, u32[]{:S(2)}) collective-permute-start(f32[168,8,128]{2,1,0:T(8,128)S(1)} %get-tuple-element.18.own_ref), channel_id=1, source_target_pairs={{0,4},{8,12},{4,0},{12,8},{1,5},{9,13},{5,1},{13,9},{2,6},{10,14},... | collective-permute-start | bytes 2064392 | tf_op jit(solution)/shard_map/ppermute | solution.py:508

commit v6 on v5

--- a/solution.py
+++ b/solution.py
@@ -529,8 +529,8 @@
 
 def on_device(t, diffusivity, b, v, rho):
     zs = lax.axis_size("gz")
-    outer = lax.axis_size("gx_0") * lax.axis_size("gy")
-    inner = lax.axis_size("gx_1") * lax.axis_size("gx_2")
+    outer = lax.axis_size("gx_2") * lax.axis_size("gy")
+    inner = lax.axis_size("gx_0") * lax.axis_size("gx_1")
     out = [(W, W, LANES), (zs, ZT, W, LANES)]
     kappa, edges = on_core(pack_z, out, t, diffusivity, b, v, rho)
     edges = lax.all_to_all(edges, "gz", 0, 0, tiled=True)
@@ -538,12 +538,12 @@
     out = [(SIDE, W, LANES)] * 2 + [((W + 1) * AUX, W, LANES), (outer, 1, LANES)]
     first, second, aux, low = on_core(pack_x, out, t, kappa, b, v, rho, edges)
     x_first, x_second = exchange(first, second, GX)
-    low = lax.all_to_all(low, ("gx_0", "gy"), 0, 0, tiled=True)
+    low = lax.all_to_all(low, ("gx_2", "gy"), 0, 0, tiled=True)
     args = held(first, aux, x_first, x_second, low)
     out = [(YT, W, LANES)] * 2 + [(A_TILES, W, LANES), (inner, 1, LANES)]
     first, second, aux, low = on_core(pack_y, out, *args)
     y_first, y_second = exchange(first, second, "gy")
-    low = lax.all_to_all(low, ("gx_1", "gx_2"), 0, 0, tiled=True)
+    low = lax.all_to_all(low, ("gx_0", "gx_1"), 0, 0, tiled=True)
     out = [(W, W, LANES), (3, W, W, LANES)]
     args = held(first, aux, y_first, y_second, low)
     return tuple(on_core(advance, out, *args, scratch=SCRATCH, last=True))

time: 79.5 us -> 78.5 us (0.987); the launches traced: 78.3 us -> 78.1 us
  waiting for transfers between devices: 1.43 us -> 0.01 us
  blocking collectives: 40 us -> 41.2 us
    all_to_all x2, blocking collectives: 27.7 us -> 29 us  [the longest x1 20.2 us: on_device(): low = lax.all_to_all(low, ('gx_0', 'gx_1'), 0, 0, tiled=True)]
    ppermute x2, waiting for transfers between devices: 1.12 us -> 0.01 us  [exchange(): lax.ppermute(first, axis, swaps)]
  transfers between devices with their start and end apart: 4 -> 4, of which waited for: 2 -> 0; matrix products, arithmetic and copies ran while one was open for 0% -> 0% of each run, Pallas kernels for 0% -> 0%
where the time goes in v6:
time: 78.5 us; the launch traced here: 78.1 us
  blocking collectives  41.2 us (52%)
  starting transfers between devices  21.5 us (27%)
  Pallas kernels  14.7 us (19%)
    all_to_all x1, blocking collectives, on_device(): low = lax.all_to_all(low, ('gx_0', 'gx_1'), 0, 0, tiled=True)  20.2 us
    pallas_call x4, Pallas kernels, on_core(): pl.pallas_call(kernel, out_shape=shape, in_specs=[space] * len(args), out...  14.7 us
    ppermute x2, starting transfers between devices, exchange(): lax.ppermute(first, axis, swaps)  13.5 us
    all_to_all x1, blocking collectives, on_device(): edges = lax.all_to_all(edges, 'gz', 0, 0, tiled=True)  12.2 us
    all_to_all x1, blocking collectives, on_device(): low = lax.all_to_all(low, ('gx_2', 'gy'), 0, 0, tiled=True)  8.8 us
    ppermute x2, starting transfers between devices, exchange(): lax.ppermute(second, axis, others)  7.98 us
  transfers between devices with their start and end apart: 4, of which 0 were waited for; matrix products, arithmetic and copies ran while one was open for 0% of the time, Pallas kernels for 0%

profile of v6, /device:TPU:1, one launch (start us, length us, event | category | flops | bytes accessed | tf_op | source)
XLA Modules:
  0.0 78.1 jit_solution(2679440284119569895)
XLA Ops:
  0.6 1.2 %pack_z.1 = (f32[8,8,128]{2,1,0:T(8,128)S(1)}, f32[4,5,8,128]{3,2,1,0:T(8,128)S(1)}) custom-call(f32[8,8,128]{2,1,0:T(8,128)} %t_ref.3, f32[8,8,128]{2,1,0:T(8,128)} %d_ref.1, f32[3,8,8,128]{3,2,1,0:T(8,128)} %b_ref.3, f32[3,8,8,128]{3,2,1,0:T(8,128)} %v_ref.3, f32[8,8,128]{2,1,0:T(8,128)} %r_ref.3), custom_call_target="tpu_custom_call" | custom-call | tf_op jit(solution)/shard_map/pack_z/pallas_call | solution.py:516
  1.8 12.2 %all_to_all.15.z_ref = f32[4,5,8,128]{3,2,1,0:T(8,128)S(1)} all-to-all(f32[4,5,8,128]{3,2,1,0:T(8,128)S(1)} %get-tuple-element.13), channel_id=1, replica_groups=mesh['gx_0'=3,'gx_1'=8,'gx_2'=2,'gy'=4,'gz'=4] {'gz'}, dimensions={0} | all-to-all | bytes 163840 | tf_op jit(solution)/shard_map/all_to_all | solution.py:536
  14.1 1.5 %pack_x.1 = (f32[54,8,128]{2,1,0:T(8,128)S(1)}, f32[54,8,128]{2,1,0:T(8,128)S(1)}, f32[36,8,128]{2,1,0:T(8,128)S(1)}, f32[8,1,128]{2,1,0:T(1,128)S(1)}) custom-call(f32[8,8,128]{2,1,0:T(8,128)} %t_ref.3, f32[8,8,128]{2,1,0:T(8,128)S(1)} %get-tuple-element.12.k_ref, f32[3,8,8,128]{3,2,1,0:T(8,128)} %b_ref.3, f32[3,8,8,128]{3,2,1,0:T(8,128)} %v_ref.3, ...), custom_call_target="tpu_custom_call" | custom-call | tf_op jit(solution)/shard_map/pack_x/pallas_call | solution.py:516
  15.6 5.2 %collective-permute-start.1 = (f32[54,8,128]{2,1,0:T(8,128)S(1)}, f32[54,8,128]{2,1,0:T(8,128)S(1)}, u32[]{:S(2)}, u32[]{:S(2)}) collective-permute-start(f32[54,8,128]{2,1,0:T(8,128)S(1)} %get-tuple-element.16), channel_id=1, source_target_pairs={{16,32},{48,64},{80,96},{112,128},{144,160},{176,192},{208,224},{2... | collective-permute-start | bytes 663560 | tf_op jit(solution)/shard_map/ppermute | solution.py:508
  20.8 11.6 %collective-permute-start = (f32[54,8,128]{2,1,0:T(8,128)S(1)}, f32[54,8,128]{2,1,0:T(8,128)S(1)}, u32[]{:S(2)}, u32[]{:S(2)}) collective-permute-start(f32[54,8,128]{2,1,0:T(8,128)S(1)} %get-tuple-element.14.own_ref), channel_id=1, source_target_pairs={{0,16},{32,48},{64,80},{96,112},{128,144},{160,176},{192,208},{224... | collective-permute-start | bytes 663560 | tf_op jit(solution)/shard_map/ppermute | solution.py:508
  32.4 8.8 %all_to_all.16.min_ref = f32[8,1,128]{2,1,0:T(1,128)S(1)} all-to-all(f32[8,1,128]{2,1,0:T(1,128)S(1)} %get-tuple-element.17), channel_id=1, replica_groups=mesh['gx_0'=3,'gx_1'=8,'gx_2'=2,'gy'=4,'gz'=4] {'gx_2','gy'}, dimensions={0} | all-to-all | bytes 8192 | tf_op jit(solution)/shard_map/all_to_all | solution.py:541
  41.2 0.0 collective-permute-done.1.xo_ref
  41.2 0.0 collective-permute-done.xa_ref
  41.2 1.3 %pack_y.1 = (f32[168,8,128]{2,1,0:T(8,128)S(1)}, f32[168,8,128]{2,1,0:T(8,128)}, f32[72,8,128]{2,1,0:T(8,128)S(1)}, f32[24,1,128]{2,1,0:T(1,128)S(1)}) custom-call(f32[54,8,128]{2,1,0:T(8,128)S(1)} %get-tuple-element.14.own_ref, f32[36,8,128]{2,1,0:T(8,128)S(1)} %get-tuple-element.15.ownaux_ref, f32[54,8,128]{2,1,0:T(8,128)S(1)} %collective-permute-done.xa_ref, ...), custom_call_target="tpu_custom_call" | custom-call | tf_op jit(solution)/shard_map/pack_y/pallas_call | solution.py:516
  42.5 2.8 %collective-permute-start.3 = (f32[168,8,128]{2,1,0:T(8,128)}, f32[168,8,128]{2,1,0:T(8,128)S(1)}, u32[]{:S(2)}, u32[]{:S(2)}) collective-permute-start(f32[168,8,128]{2,1,0:T(8,128)} %get-tuple-element.20), channel_id=1, source_target_pairs={{4,8},{12,0},{8,4},{0,12},{5,9},{13,1},{9,5},{1,13},{6,10},{14,2},... | collective-permute-start | bytes 2064392 | tf_op jit(solution)/shard_map/ppermute | solution.py:508
  45.2 1.9 %collective-permute-start.2 = (f32[168,8,128]{2,1,0:T(8,128)S(1)}, f32[168,8,128]{2,1,0:T(8,128)S(1)}, u32[]{:S(2)}, u32[]{:S(2)}) collective-permute-start(f32[168,8,128]{2,1,0:T(8,128)S(1)} %get-tuple-element.18.own_ref), channel_id=1, source_target_pairs={{0,4},{8,12},{4,0},{12,8},{1,5},{9,13},{5,1},{13,9},{2,6},{10,14},... | collective-permute-start | bytes 2064392 | tf_op jit(solution)/shard_map/ppermute | solution.py:508
  47.2 20.2 %all_to_all.17.low_ref = f32[24,1,128]{2,1,0:T(1,128)S(1)} all-to-all(f32[24,1,128]{2,1,0:T(1,128)S(1)} %get-tuple-element.21), channel_id=1, replica_groups=mesh['gx_0'=3,'gx_1'=8,'gx_2'=2,'gy'=4,'gz'=4] {'gx_0','gx_1'}, dimensions={0} | all-to-all | bytes 24576 | tf_op jit(solution)/shard_map/all_to_all | solution.py:546
  67.4 0.0 collective-permute-done.3.yo_ref
  67.4 0.0 collective-permute-done.2.ya_ref
  67.4 10.7 %advance.1 = (f32[8,8,128]{2,1,0:T(8,128)}, f32[3,8,8,128]{3,2,1,0:T(8,128)}) custom-call(f32[168,8,128]{2,1,0:T(8,128)S(1)} %get-tuple-element.18.own_ref, f32[72,8,128]{2,1,0:T(8,128)S(1)} %get-tuple-element.19.aux_ref, f32[168,8,128]{2,1,0:T(8,128)S(1)} %collective-permute-done.2.ya_ref, f32[168,8,128]{2,1,0:T(8,128)S(1)} %collective-permute-done.3.yo_ref, ...), custom_call_target="tpu_custom_call" | custom-call | tf_op jit(solution)/shard_map/advance/pallas_call | solution.py:516
Async XLA Ops:
  15.6 25.6 %collective-permute-start.1 = (f32[54,8,128]{2,1,0:T(8,128)S(1)}, f32[54,8,128]{2,1,0:T(8,128)S(1)}, u32[]{:S(2)}, u32[]{:S(2)}) collective-permute-start(f32[54,8,128]{2,1,0:T(8,128)S(1)} %get-tuple-element.16), channel_id=1, source_target_pairs={{16,32},{48,64},{80,96},{112,128},{144,160},{176,192},{208,224},{2... | collective-permute-start | bytes 663560 | tf_op jit(solution)/shard_map/ppermute | solution.py:508
  20.8 20.4 %collective-permute-start = (f32[54,8,128]{2,1,0:T(8,128)S(1)}, f32[54,8,128]{2,1,0:T(8,128)S(1)}, u32[]{:S(2)}, u32[]{:S(2)}) collective-permute-start(f32[54,8,128]{2,1,0:T(8,128)S(1)} %get-tuple-element.14.own_ref), channel_id=1, source_target_pairs={{0,16},{32,48},{64,80},{96,112},{128,144},{160,176},{192,208},{224... | collective-permute-start | bytes 663560 | tf_op jit(solution)/shard_map/ppermute | solution.py:508
  42.5 24.9 %collective-permute-start.3 = (f32[168,8,128]{2,1,0:T(8,128)}, f32[168,8,128]{2,1,0:T(8,128)S(1)}, u32[]{:S(2)}, u32[]{:S(2)}) collective-permute-start(f32[168,8,128]{2,1,0:T(8,128)} %get-tuple-element.20), channel_id=1, source_target_pairs={{4,8},{12,0},{8,4},{0,12},{5,9},{13,1},{9,5},{1,13},{6,10},{14,2},... | collective-permute-start | bytes 2064392 | tf_op jit(solution)/shard_map/ppermute | solution.py:508
  45.2 22.1 %collective-permute-start.2 = (f32[168,8,128]{2,1,0:T(8,128)S(1)}, f32[168,8,128]{2,1,0:T(8,128)S(1)}, u32[]{:S(2)}, u32[]{:S(2)}) collective-permute-start(f32[168,8,128]{2,1,0:T(8,128)S(1)} %get-tuple-element.18.own_ref), channel_id=1, source_target_pairs={{0,4},{8,12},{4,0},{12,8},{1,5},{9,13},{5,1},{13,9},{2,6},{10,14},... | collective-permute-start | bytes 2064392 | tf_op jit(solution)/shard_map/ppermute | solution.py:508

commit v7 on v6

--- a/solution.py
+++ b/solution.py
@@ -42,6 +42,7 @@
     (3, A_PLANES, ROWS, LANES),
     (3, A_PLANES, ROWS, LANES),
 ]
+LATE = 5
 FIRST_RATE = 4.0 / (SECTIONS * SECTIONS + SECTIONS - 2)
 LIMIT = (SECTIONS * SECTIONS + SECTIONS - 2) / 16.0
 
@@ -309,7 +310,7 @@
         u = y00[x]
         y01[x] = lroll(u, -1)
         y02[x] = lroll(u, 1)
-        x_p = jnp.minimum(x + 1, PLANES - 1)
+        x_p = min(x + 1, PLANES - 1)
         bx, by, bz, sx, sy, sz = sums(x, x_p)
         face(0, x, kap + k_m, bx, sy + sy_m, sz + sz_m)
         face(1, x, kap + rroll(kap, 1), by, sz + rroll(sz, 1), sx + rroll(sx, 1))
@@ -318,17 +319,13 @@
 
     for first, last in ((0, XE), (LOW, PLANES)):
         _, _, _, _, sy, sz = sums(first, first + 1)
-        sweep(first, last, faces, (full[0, first], sy, sz), 4)
-
-    def upper(x, carry):
-        for k in range(3):
-            coef_up[k, x] = lroll(coef[6 + k, x], -1)
-        return carry
-
-    sweep(0, PLANES, upper, 0, 8)
+        carry = full[0, first], sy, sz
+        for x in range(first, last):
+            carry = faces(x, carry)
 
     arrays = ((y00, y01, y02), (y10, y11, y12), (y20, y21, y22))
     source, older = arrays[0], None
+    begun = []
     for j in range(1, SECTIONS + 1):
         target = arrays[2 - j % 2]
         grow = (2.0 * j - 1.0) / j
@@ -341,34 +338,38 @@
         def flux_x(x, du, sum_y, sum_z):
             return coef[0, x] * du + coef[1, x] * sum_y + coef[2, x] * sum_z
 
-        def plane(x, carry, source=source, older=older, target=target, grow=grow, back=back, j=j):
+        def plane(x, carry, source=source):
             dy, dz, fx, down = carry
             u, p, m = source[0][x], source[1][x], source[2][x]
             u_p, p_p, m_p = source[0][x + 1], source[1][x + 1], source[2][x + 1]
             down_p, dy_p, dz_p = rolled(u_p, p_p, m_p)
             fx_p = flux_x(x + 1, u_p - u, dy_p + dy, dz_p + dz)
             dx = u_p - source[0][x - 1]
-            dx_zp = p_p - source[1][x - 1]
             dx_zm = m_p - source[2][x - 1]
-            p_down, m_down = rroll(p, 1), rroll(m, 1)
-            dy_zp = rroll(p, -1) - p_down
+            m_down = rroll(m, 1)
             dy_zm = rroll(m, -1) - m_down
             fy = (
                 coef[3, x] * (u - down)
-                + coef[4, x] * (dz + (p_down - m_down))
+                + coef[4, x] * (dz + rroll(dz, 1))
                 + coef[5, x] * (dx + rroll(dx, 1))
             )
             fz = coef[6, x] * (u - m) + coef[7, x] * (dx + dx_zm) + coef[8, x] * (dy + dy_zm)
-            fz_p = coef_up[0, x] * (p - u) + coef_up[1, x] * (dx_zp + dx) + coef_up[2, x] * (dy_zp + dy)
-            rate = (fx_p - fx) + (rroll(fy, -1) - fy) + (fz_p - fz)
-            new = u + rate
+            ahead_z = lroll(fz, -1)
+            rate = (fx_p - fx) + (rroll(fy, -1) - fy) - fz
+            return (dy_p, dz_p, fx_p, down_p), u + rate, ahead_z
+
+        def finish(x, new, ahead_z, target=target, older=older, grow=grow, back=back, j=j):
+            new = new + ahead_z
             if j > 1:
                 new = grow * new - back * older[0][x]
             if j == SECTIONS:
                 b = (SECTIONS * SECTIONS + SECTIONS - 2) / (2.0 * SECTIONS * (SECTIONS + 1))
                 new = (1.0 - b) * y00[x] + b * new
             target[0][x] = new
-            return (dy_p, dz_p, fx_p, down_p), new
+            if j < SECTIONS:
+                target[1][x] = lroll(new, -1)
+                target[2][x] = lroll(new, 1)
+            return new
 
         def start(x, source=source):
             u_m, u = source[0][x - 1], source[0][x]
@@ -376,38 +377,27 @@
             down, dy, dz = rolled(u, source[1][x], source[2][x])
             return dy, dz, flux_x(x, u - u_m, dy + dy_m, dz + dz_m), down
 
-        def two(i, carry, target=target, plane=plane, j=j):
-            x = j + 2 * i
-            carry, *made = carry
-            turned = [(lroll(u, -1), lroll(u, 1)) for u in made]
-            carry, first = plane(x, carry)
-            carry, second = plane(x + 1, carry)
-            if j < SECTIONS:
-                for k, (up, down) in enumerate(turned):
-                    at = jnp.maximum(x - 2 + k, 0)
-                    target[1][at] = up
-                    target[2][at] = down
-            return carry, first, second
-
-        carry = start(j)
-        _, *made = lax.fori_loop(0, (XE - 2 * j) // 2, two, (carry, carry[3], carry[3]))
-        carry = start(LOW + 1)
         strip = []
-        for x in range(LOW + 1, HIGH):
-            carry, new = plane(x, carry)
-            strip.append(new)
-        if j < SECTIONS:
-            for k, u in enumerate(made):
-                target[1][XE - j - 2 + k] = lroll(u, -1)
-                target[2][XE - j - 2 + k] = lroll(u, 1)
-            for at, u, by in ((HIGH, strip[0], -WIDE), (LOW, strip[-1], WIDE)):
-                target[0][at] = lroll(u, by)
-                target[1][at] = lroll(u, by - 1)
-                target[2][at] = lroll(u, by + 1)
-            for k, u in enumerate(strip):
-                target[1][LOW + 1 + k] = lroll(u, -1)
-                target[2][LOW + 1 + k] = lroll(u, 1)
+
+        def finish_strip(x, new, ahead_z, finish=finish, strip=strip, target=target, j=j):
+            strip.append(finish(x, new, ahead_z))
+            if x == HIGH - 1 and j < SECTIONS:
+                for at, u, by in ((HIGH, strip[0], -WIDE), (LOW, strip[-1], WIDE)):
+                    target[0][at] = lroll(u, by)
+                    target[1][at] = lroll(u, by - 1)
+                    target[2][at] = lroll(u, by + 1)
+
+        for first, last, then in ((LOW + 1, HIGH, finish_strip), (j, XE - j, finish)):
+            carry = start(first)
+            for x in range(first, last):
+                carry, *parts = plane(x, carry)
+                begun.append((then, x, *parts))
+                if len(begun) > LATE:
+                    then_, *parts = begun.pop(0)
+                    then_(*parts)
         source, older = target, source
+    for then, *parts in begun:
+        then(*parts)
 
     def seam(main, strip, g):
         return jnp.where(

time: 78.5 us -> 75 us (0.955)
  Pallas kernels: 14.7 us -> 11.3 us
    pallas_call x4, Pallas kernels: 14.7 us -> 11.3 us  [on_core(): pl.pallas_call(kernel, out_shape=shape, in_specs=[space] * len(args), out...]
where the time goes in v7:
time: 75 us; the launch traced here: 74.7 us
  blocking collectives  41.2 us (55%)
  starting transfers between devices  21.5 us (29%)
  Pallas kernels  11.3 us (15%)
    all_to_all x1, blocking collectives, on_device(): low = lax.all_to_all(low, ('gx_0', 'gx_1'), 0, 0, tiled=True)  20.2 us
    ppermute x2, starting transfers between devices, exchange(): lax.ppermute(first, axis, swaps)  13.5 us
    all_to_all x1, blocking collectives, on_device(): edges = lax.all_to_all(edges, 'gz', 0, 0, tiled=True)  12.2 us
    pallas_call x4, Pallas kernels, on_core(): pl.pallas_call(kernel, out_shape=shape, in_specs=[space] * len(args), out...  11.3 us
    all_to_all x1, blocking collectives, on_device(): low = lax.all_to_all(low, ('gx_2', 'gy'), 0, 0, tiled=True)  8.8 us
    ppermute x2, starting transfers between devices, exchange(): lax.ppermute(second, axis, others)  7.98 us
  transfers between devices with their start and end apart: 4, of which 0 were waited for; matrix products, arithmetic and copies ran while one was open for 0% of the time, Pallas kernels for 0%

profile of v7, /device:TPU:1, one launch (start us, length us, event | category | flops | bytes accessed | tf_op | source)
XLA Modules:
  0.0 74.7 jit_solution(16640750563297230058)
XLA Ops:
  0.6 1.2 %pack_z.1 = (f32[8,8,128]{2,1,0:T(8,128)S(1)}, f32[4,5,8,128]{3,2,1,0:T(8,128)S(1)}) custom-call(f32[8,8,128]{2,1,0:T(8,128)} %t_ref.3, f32[8,8,128]{2,1,0:T(8,128)} %d_ref.1, f32[3,8,8,128]{3,2,1,0:T(8,128)} %b_ref.3, f32[3,8,8,128]{3,2,1,0:T(8,128)} %v_ref.3, f32[8,8,128]{2,1,0:T(8,128)} %r_ref.3), custom_call_target="tpu_custom_call" | custom-call | tf_op jit(solution)/shard_map/pack_z/pallas_call | solution.py:506
  1.8 12.2 %all_to_all.15.z_ref = f32[4,5,8,128]{3,2,1,0:T(8,128)S(1)} all-to-all(f32[4,5,8,128]{3,2,1,0:T(8,128)S(1)} %get-tuple-element.13), channel_id=1, replica_groups=mesh['gx_0'=3,'gx_1'=8,'gx_2'=2,'gy'=4,'gz'=4] {'gz'}, dimensions={0} | all-to-all | bytes 163840 | tf_op jit(solution)/shard_map/all_to_all | solution.py:526
  14.1 1.5 %pack_x.1 = (f32[54,8,128]{2,1,0:T(8,128)S(1)}, f32[54,8,128]{2,1,0:T(8,128)S(1)}, f32[36,8,128]{2,1,0:T(8,128)S(1)}, f32[8,1,128]{2,1,0:T(1,128)S(1)}) custom-call(f32[8,8,128]{2,1,0:T(8,128)} %t_ref.3, f32[8,8,128]{2,1,0:T(8,128)S(1)} %get-tuple-element.12.k_ref, f32[3,8,8,128]{3,2,1,0:T(8,128)} %b_ref.3, f32[3,8,8,128]{3,2,1,0:T(8,128)} %v_ref.3, ...), custom_call_target="tpu_custom_call" | custom-call | tf_op jit(solution)/shard_map/pack_x/pallas_call | solution.py:506
  15.6 5.2 %collective-permute-start.1 = (f32[54,8,128]{2,1,0:T(8,128)S(1)}, f32[54,8,128]{2,1,0:T(8,128)S(1)}, u32[]{:S(2)}, u32[]{:S(2)}) collective-permute-start(f32[54,8,128]{2,1,0:T(8,128)S(1)} %get-tuple-element.16), channel_id=1, source_target_pairs={{16,32},{48,64},{80,96},{112,128},{144,160},{176,192},{208,224},{2... | collective-permute-start | bytes 663560 | tf_op jit(solution)/shard_map/ppermute | solution.py:498
  20.8 11.6 %collective-permute-start = (f32[54,8,128]{2,1,0:T(8,128)S(1)}, f32[54,8,128]{2,1,0:T(8,128)S(1)}, u32[]{:S(2)}, u32[]{:S(2)}) collective-permute-start(f32[54,8,128]{2,1,0:T(8,128)S(1)} %get-tuple-element.14.own_ref), channel_id=1, source_target_pairs={{0,16},{32,48},{64,80},{96,112},{128,144},{160,176},{192,208},{224... | collective-permute-start | bytes 663560 | tf_op jit(solution)/shard_map/ppermute | solution.py:498
  32.4 8.8 %all_to_all.16.min_ref = f32[8,1,128]{2,1,0:T(1,128)S(1)} all-to-all(f32[8,1,128]{2,1,0:T(1,128)S(1)} %get-tuple-element.17), channel_id=1, replica_groups=mesh['gx_0'=3,'gx_1'=8,'gx_2'=2,'gy'=4,'gz'=4] {'gx_2','gy'}, dimensions={0} | all-to-all | bytes 8192 | tf_op jit(solution)/shard_map/all_to_all | solution.py:531
  41.2 0.0 collective-permute-done.1.xo_ref
  41.2 0.0 collective-permute-done.xa_ref
  41.2 1.3 %pack_y.1 = (f32[168,8,128]{2,1,0:T(8,128)S(1)}, f32[168,8,128]{2,1,0:T(8,128)}, f32[72,8,128]{2,1,0:T(8,128)S(1)}, f32[24,1,128]{2,1,0:T(1,128)S(1)}) custom-call(f32[54,8,128]{2,1,0:T(8,128)S(1)} %get-tuple-element.14.own_ref, f32[36,8,128]{2,1,0:T(8,128)S(1)} %get-tuple-element.15.ownaux_ref, f32[54,8,128]{2,1,0:T(8,128)S(1)} %collective-permute-done.xa_ref, ...), custom_call_target="tpu_custom_call" | custom-call | tf_op jit(solution)/shard_map/pack_y/pallas_call | solution.py:506
  42.5 2.8 %collective-permute-start.3 = (f32[168,8,128]{2,1,0:T(8,128)}, f32[168,8,128]{2,1,0:T(8,128)S(1)}, u32[]{:S(2)}, u32[]{:S(2)}) collective-permute-start(f32[168,8,128]{2,1,0:T(8,128)} %get-tuple-element.20), channel_id=1, source_target_pairs={{4,8},{12,0},{8,4},{0,12},{5,9},{13,1},{9,5},{1,13},{6,10},{14,2},... | collective-permute-start | bytes 2064392 | tf_op jit(solution)/shard_map/ppermute | solution.py:498
  45.2 1.9 %collective-permute-start.2 = (f32[168,8,128]{2,1,0:T(8,128)S(1)}, f32[168,8,128]{2,1,0:T(8,128)S(1)}, u32[]{:S(2)}, u32[]{:S(2)}) collective-permute-start(f32[168,8,128]{2,1,0:T(8,128)S(1)} %get-tuple-element.18.own_ref), channel_id=1, source_target_pairs={{0,4},{8,12},{4,0},{12,8},{1,5},{9,13},{5,1},{13,9},{2,6},{10,14},... | collective-permute-start | bytes 2064392 | tf_op jit(solution)/shard_map/ppermute | solution.py:498
  47.2 20.2 %all_to_all.17.low_ref = f32[24,1,128]{2,1,0:T(1,128)S(1)} all-to-all(f32[24,1,128]{2,1,0:T(1,128)S(1)} %get-tuple-element.21), channel_id=1, replica_groups=mesh['gx_0'=3,'gx_1'=8,'gx_2'=2,'gy'=4,'gz'=4] {'gx_0','gx_1'}, dimensions={0} | all-to-all | bytes 24576 | tf_op jit(solution)/shard_map/all_to_all | solution.py:536
  67.4 0.0 collective-permute-done.3.yo_ref
  67.4 0.0 collective-permute-done.2.ya_ref
  67.4 7.3 %advance.1 = (f32[8,8,128]{2,1,0:T(8,128)}, f32[3,8,8,128]{3,2,1,0:T(8,128)}) custom-call(f32[168,8,128]{2,1,0:T(8,128)S(1)} %get-tuple-element.18.own_ref, f32[72,8,128]{2,1,0:T(8,128)S(1)} %get-tuple-element.19.aux_ref, f32[168,8,128]{2,1,0:T(8,128)S(1)} %collective-permute-done.2.ya_ref, f32[168,8,128]{2,1,0:T(8,128)S(1)} %collective-permute-done.3.yo_ref, ...), custom_call_target="tpu_custom_call" | custom-call | tf_op jit(solution)/shard_map/advance/pallas_call | solution.py:506
Async XLA Ops:
  15.6 25.6 %collective-permute-start.1 = (f32[54,8,128]{2,1,0:T(8,128)S(1)}, f32[54,8,128]{2,1,0:T(8,128)S(1)}, u32[]{:S(2)}, u32[]{:S(2)}) collective-permute-start(f32[54,8,128]{2,1,0:T(8,128)S(1)} %get-tuple-element.16), channel_id=1, source_target_pairs={{16,32},{48,64},{80,96},{112,128},{144,160},{176,192},{208,224},{2... | collective-permute-start | bytes 663560 | tf_op jit(solution)/shard_map/ppermute | solution.py:498
  20.8 20.4 %collective-permute-start = (f32[54,8,128]{2,1,0:T(8,128)S(1)}, f32[54,8,128]{2,1,0:T(8,128)S(1)}, u32[]{:S(2)}, u32[]{:S(2)}) collective-permute-start(f32[54,8,128]{2,1,0:T(8,128)S(1)} %get-tuple-element.14.own_ref), channel_id=1, source_target_pairs={{0,16},{32,48},{64,80},{96,112},{128,144},{160,176},{192,208},{224... | collective-permute-start | bytes 663560 | tf_op jit(solution)/shard_map/ppermute | solution.py:498
  42.5 24.9 %collective-permute-start.3 = (f32[168,8,128]{2,1,0:T(8,128)}, f32[168,8,128]{2,1,0:T(8,128)S(1)}, u32[]{:S(2)}, u32[]{:S(2)}) collective-permute-start(f32[168,8,128]{2,1,0:T(8,128)} %get-tuple-element.20), channel_id=1, source_target_pairs={{4,8},{12,0},{8,4},{0,12},{5,9},{13,1},{9,5},{1,13},{6,10},{14,2},... | collective-permute-start | bytes 2064392 | tf_op jit(solution)/shard_map/ppermute | solution.py:498
  45.2 22.1 %collective-permute-start.2 = (f32[168,8,128]{2,1,0:T(8,128)S(1)}, f32[168,8,128]{2,1,0:T(8,128)S(1)}, u32[]{:S(2)}, u32[]{:S(2)}) collective-permute-start(f32[168,8,128]{2,1,0:T(8,128)S(1)} %get-tuple-element.18.own_ref), channel_id=1, source_target_pairs={{0,4},{8,12},{4,0},{12,8},{1,5},{9,13},{5,1},{13,9},{2,6},{10,14},... | collective-permute-start | bytes 2064392 | tf_op jit(solution)/shard_map/ppermute | solution.py:498

commit v8 on v7

--- a/solution.py
+++ b/solution.py
@@ -33,7 +33,7 @@
 A_TILES = AUX * (XA + XG)
 Y_FULL = FULL * (XE + XG)
 YT = Y_FULL + A_TILES // 4
-SCRATCH = [(PLANES, ROWS, LANES)] * 9 + [
+SCRATCH = [(PLANES, ROWS, LANES)] * 12 + [
     (FULL - 1, PLANES, ROWS, LANES),
     (AUX, A_PLANES, ROWS, LANES),
     (9, PLANES, ROWS, LANES),
@@ -77,10 +77,9 @@
     return divmod(field * W + plane, 16)
 
 
-def pack_z(t_ref, d_ref, b_ref, v_ref, r_ref, kap_ref, out_ref):
+def pack_z(t_ref, d_ref, b_ref, v_ref, r_ref, all_ref, out_ref):
     t = t_ref[...]
     kappa = d_ref[...] * (t * t * jnp.sqrt(t))
-    kap_ref[...] = kappa
     low = lowest(jnp.min(LIMIT / kappa, axis=0))
     lane = lane_ids(W)
     left, right = [], []
@@ -98,6 +97,7 @@
                 u = b_ref[field - 2, plane]
             else:
                 u = v_ref[field - FULL, plane] if field < FULL + 3 else r_ref[plane]
+            all_ref[field * W + plane] = u
             here = (lane >= 8 * k) & (lane < 8 * k + 8)
             below = jnp.where(here, lroll(u, 8 * k), below)
             above = jnp.where(here, lroll(u, 8 * k - (LANES - 8)), above)
@@ -109,7 +109,7 @@
             out_ref[slot, tile] = jnp.where(lo == slot, left[tile], right[tile])
 
 
-def pack_x(t_ref, k_ref, b_ref, v_ref, r_ref, z_ref, a_ref, o_ref, aux_ref, low_ref):
+def pack_x(all_ref, z_ref, a_ref, o_ref, aux_ref, low_ref):
     odd = is_odd(GX)
     lo, hi = neighbours("gz")
     lane = lane_ids(W)
@@ -119,10 +119,7 @@
     for field in range(FULL + AUX):
         ends = jnp.zeros((W, LANES), jnp.float32)
         for plane in range(W):
-            if field < FULL:
-                u = (t_ref, k_ref, b_ref.at[0], b_ref.at[1], b_ref.at[2])[field][plane]
-            else:
-                u = v_ref[field - FULL, plane] if field < FULL + 3 else r_ref[plane]
+            u = all_ref[field * W + plane]
             tile, k = piece(field, plane)
             main = jnp.where(lane < 8, lroll(left[tile], -8 * k), lroll(u, 8))
             to = 16 * plane
@@ -252,7 +249,7 @@
 
 def advance(
     own_ref, aux_ref, ya_ref, yo_ref, low_ref, tout_ref, bout_ref,
-    y00, y01, y02, y10, y11, y12, y20, y21, y22, full, aux, coef, coef_up, ecoef, edge, mid,
+    y00, y01, y02, y03, y10, y11, y12, y13, y20, y21, y22, y23, full, aux, coef, coef_up, ecoef, edge, mid,
 ):
     lane = lane_ids(W)
     dt = lowest(jnp.min(low_ref[...], axis=0))
@@ -310,6 +307,7 @@
         u = y00[x]
         y01[x] = lroll(u, -1)
         y02[x] = lroll(u, 1)
+        y03[x] = lroll(rroll(u, -1) - rroll(u, 1), 1)
         x_p = min(x + 1, PLANES - 1)
         bx, by, bz, sx, sy, sz = sums(x, x_p)
         face(0, x, kap + k_m, bx, sy + sy_m, sz + sz_m)
@@ -323,7 +321,7 @@
         for x in range(first, last):
             carry = faces(x, carry)
 
-    arrays = ((y00, y01, y02), (y10, y11, y12), (y20, y21, y22))
+    arrays = ((y00, y01, y02, y03), (y10, y11, y12, y13), (y20, y21, y22, y23))
     source, older = arrays[0], None
     begun = []
     for j in range(1, SECTIONS + 1):
@@ -346,8 +344,7 @@
             fx_p = flux_x(x + 1, u_p - u, dy_p + dy, dz_p + dz)
             dx = u_p - source[0][x - 1]
             dx_zm = m_p - source[2][x - 1]
-            m_down = rroll(m, 1)
-            dy_zm = rroll(m, -1) - m_down
+            dy_zm = source[3][x]
             fy = (
                 coef[3, x] * (u - down)
                 + coef[4, x] * (dz + rroll(dz, 1))
@@ -365,10 +362,13 @@
             if j == SECTIONS:
                 b = (SECTIONS * SECTIONS + SECTIONS - 2) / (2.0 * SECTIONS * (SECTIONS + 1))
                 new = (1.0 - b) * y00[x] + b * new
-            target[0][x] = new
-            if j < SECTIONS:
+            if j == SECTIONS:
+                target[0][x, W : 2 * W] = new[W : 2 * W]
+            else:
+                target[0][x] = new
                 target[1][x] = lroll(new, -1)
                 target[2][x] = lroll(new, 1)
+                target[3][x] = lroll(rroll(new, -1) - rroll(new, 1), 1)
             return new
 
         def start(x, source=source):
@@ -521,12 +521,12 @@
     zs = lax.axis_size("gz")
     outer = lax.axis_size("gx_2") * lax.axis_size("gy")
     inner = lax.axis_size("gx_0") * lax.axis_size("gx_1")
-    out = [(W, W, LANES), (zs, ZT, W, LANES)]
-    kappa, edges = on_core(pack_z, out, t, diffusivity, b, v, rho)
+    out = [((FULL + AUX) * W, W, LANES), (zs, ZT, W, LANES)]
+    cells, edges = on_core(pack_z, out, t, diffusivity, b, v, rho)
     edges = lax.all_to_all(edges, "gz", 0, 0, tiled=True)
-    kappa, edges = held(kappa, edges)
+    cells, edges = held(cells, edges)
     out = [(SIDE, W, LANES)] * 2 + [((W + 1) * AUX, W, LANES), (outer, 1, LANES)]
-    first, second, aux, low = on_core(pack_x, out, t, kappa, b, v, rho, edges)
+    first, second, aux, low = on_core(pack_x, out, cells, edges)
     x_first, x_second = exchange(first, second, GX)
     low = lax.all_to_all(low, ("gx_2", "gy"), 0, 0, tiled=True)
     args = held(first, aux, x_first, x_second, low)

time: 75 us -> 73.8 us (0.984)
  Pallas kernels: 11.3 us -> 10 us
    pallas_call x4, Pallas kernels: 11.3 us -> 10 us  [on_core(): pl.pallas_call(kernel, out_shape=shape, in_specs=[space] * len(args), out...]
where the time goes in v8:
time: 73.8 us; the launch traced here: 73.4 us
  blocking collectives  41.2 us (56%)
  starting transfers between devices  21.5 us (29%)
  Pallas kernels  10 us (14%)
    all_to_all x1, blocking collectives, on_device(): low = lax.all_to_all(low, ('gx_0', 'gx_1'), 0, 0, tiled=True)  20.2 us
    ppermute x2, starting transfers between devices, exchange(): lax.ppermute(first, axis, swaps)  13.5 us
    all_to_all x1, blocking collectives, on_device(): edges = lax.all_to_all(edges, 'gz', 0, 0, tiled=True)  12.2 us
    pallas_call x4, Pallas kernels, on_core(): pl.pallas_call(kernel, out_shape=shape, in_specs=[space] * len(args), out...  10 us
    all_to_all x1, blocking collectives, on_device(): low = lax.all_to_all(low, ('gx_2', 'gy'), 0, 0, tiled=True)  8.8 us
    ppermute x2, starting transfers between devices, exchange(): lax.ppermute(second, axis, others)  7.98 us
  transfers between devices with their start and end apart: 4, of which 0 were waited for; matrix products, arithmetic and copies ran while one was open for 0% of the time, Pallas kernels for 0%

profile of v8, /device:TPU:1, one launch (start us, length us, event | category | flops | bytes accessed | tf_op | source)
XLA Modules:
  0.0 73.4 jit_solution(9997586750353488147)
XLA Ops:
  0.6 1.2 %pack_z.1 = (f32[72,8,128]{2,1,0:T(8,128)S(1)}, f32[4,5,8,128]{3,2,1,0:T(8,128)S(1)}) custom-call(f32[8,8,128]{2,1,0:T(8,128)} %t_ref.1, f32[8,8,128]{2,1,0:T(8,128)} %d_ref.1, f32[3,8,8,128]{3,2,1,0:T(8,128)} %b_ref.1, f32[3,8,8,128]{3,2,1,0:T(8,128)} %v_ref.1, f32[8,8,128]{2,1,0:T(8,128)} %r_ref.1), custom_call_target="tpu_custom_call" | custom-call | tf_op jit(solution)/shard_map/pack_z/pallas_call | solution.py:506
  1.8 12.2 %all_to_all.15.z_ref = f32[4,5,8,128]{3,2,1,0:T(8,128)S(1)} all-to-all(f32[4,5,8,128]{3,2,1,0:T(8,128)S(1)} %get-tuple-element.13), channel_id=1, replica_groups=mesh['gx_0'=3,'gx_1'=8,'gx_2'=2,'gy'=4,'gz'=4] {'gz'}, dimensions={0} | all-to-all | bytes 163840 | tf_op jit(solution)/shard_map/all_to_all | solution.py:526
  14.1 0.5 pack_x.1
  14.6 5.2 %collective-permute-start.1 = (f32[54,8,128]{2,1,0:T(8,128)S(1)}, f32[54,8,128]{2,1,0:T(8,128)S(1)}, u32[]{:S(2)}, u32[]{:S(2)}) collective-permute-start(f32[54,8,128]{2,1,0:T(8,128)S(1)} %get-tuple-element.16), channel_id=1, source_target_pairs={{16,32},{48,64},{80,96},{112,128},{144,160},{176,192},{208,224},{2... | collective-permute-start | bytes 663560 | tf_op jit(solution)/shard_map/ppermute | solution.py:498
  19.8 11.6 %collective-permute-start = (f32[54,8,128]{2,1,0:T(8,128)S(1)}, f32[54,8,128]{2,1,0:T(8,128)S(1)}, u32[]{:S(2)}, u32[]{:S(2)}) collective-permute-start(f32[54,8,128]{2,1,0:T(8,128)S(1)} %get-tuple-element.14.own_ref), channel_id=1, source_target_pairs={{0,16},{32,48},{64,80},{96,112},{128,144},{160,176},{192,208},{224... | collective-permute-start | bytes 663560 | tf_op jit(solution)/shard_map/ppermute | solution.py:498
  31.4 8.8 %all_to_all.16.min_ref = f32[8,1,128]{2,1,0:T(1,128)S(1)} all-to-all(f32[8,1,128]{2,1,0:T(1,128)S(1)} %get-tuple-element.17), channel_id=1, replica_groups=mesh['gx_0'=3,'gx_1'=8,'gx_2'=2,'gy'=4,'gz'=4] {'gx_2','gy'}, dimensions={0} | all-to-all | bytes 8192 | tf_op jit(solution)/shard_map/all_to_all | solution.py:531
  40.2 0.0 collective-permute-done.1.xo_ref
  40.2 0.0 collective-permute-done.xa_ref
  40.2 1.3 %pack_y.1 = (f32[168,8,128]{2,1,0:T(8,128)S(1)}, f32[168,8,128]{2,1,0:T(8,128)}, f32[72,8,128]{2,1,0:T(8,128)S(1)}, f32[24,1,128]{2,1,0:T(1,128)S(1)}) custom-call(f32[54,8,128]{2,1,0:T(8,128)S(1)} %get-tuple-element.14.own_ref, f32[36,8,128]{2,1,0:T(8,128)S(1)} %get-tuple-element.15.ownaux_ref, f32[54,8,128]{2,1,0:T(8,128)S(1)} %collective-permute-done.xa_ref, ...), custom_call_target="tpu_custom_call" | custom-call | tf_op jit(solution)/shard_map/pack_y/pallas_call | solution.py:506
  41.5 2.8 %collective-permute-start.3 = (f32[168,8,128]{2,1,0:T(8,128)}, f32[168,8,128]{2,1,0:T(8,128)S(1)}, u32[]{:S(2)}, u32[]{:S(2)}) collective-permute-start(f32[168,8,128]{2,1,0:T(8,128)} %get-tuple-element.20), channel_id=1, source_target_pairs={{4,8},{12,0},{8,4},{0,12},{5,9},{13,1},{9,5},{1,13},{6,10},{14,2},... | collective-permute-start | bytes 2064392 | tf_op jit(solution)/shard_map/ppermute | solution.py:498
  44.3 1.9 %collective-permute-start.2 = (f32[168,8,128]{2,1,0:T(8,128)S(1)}, f32[168,8,128]{2,1,0:T(8,128)S(1)}, u32[]{:S(2)}, u32[]{:S(2)}) collective-permute-start(f32[168,8,128]{2,1,0:T(8,128)S(1)} %get-tuple-element.18.own_ref), channel_id=1, source_target_pairs={{0,4},{8,12},{4,0},{12,8},{1,5},{9,13},{5,1},{13,9},{2,6},{10,14},... | collective-permute-start | bytes 2064392 | tf_op jit(solution)/shard_map/ppermute | solution.py:498
  46.2 20.2 %all_to_all.17.low_ref = f32[24,1,128]{2,1,0:T(1,128)S(1)} all-to-all(f32[24,1,128]{2,1,0:T(1,128)S(1)} %get-tuple-element.21), channel_id=1, replica_groups=mesh['gx_0'=3,'gx_1'=8,'gx_2'=2,'gy'=4,'gz'=4] {'gx_0','gx_1'}, dimensions={0} | all-to-all | bytes 24576 | tf_op jit(solution)/shard_map/all_to_all | solution.py:536
  66.4 0.0 collective-permute-done.3.yo_ref
  66.4 0.0 collective-permute-done.2.ya_ref
  66.4 7.0 %advance.1 = (f32[8,8,128]{2,1,0:T(8,128)}, f32[3,8,8,128]{3,2,1,0:T(8,128)}) custom-call(f32[168,8,128]{2,1,0:T(8,128)S(1)} %get-tuple-element.18.own_ref, f32[72,8,128]{2,1,0:T(8,128)S(1)} %get-tuple-element.19.aux_ref, f32[168,8,128]{2,1,0:T(8,128)S(1)} %collective-permute-done.2.ya_ref, f32[168,8,128]{2,1,0:T(8,128)S(1)} %collective-permute-done.3.yo_ref, ...), custom_call_target="tpu_custom_call" | custom-call | tf_op jit(solution)/shard_map/advance/pallas_call | solution.py:506
Async XLA Ops:
  14.6 25.6 %collective-permute-start.1 = (f32[54,8,128]{2,1,0:T(8,128)S(1)}, f32[54,8,128]{2,1,0:T(8,128)S(1)}, u32[]{:S(2)}, u32[]{:S(2)}) collective-permute-start(f32[54,8,128]{2,1,0:T(8,128)S(1)} %get-tuple-element.16), channel_id=1, source_target_pairs={{16,32},{48,64},{80,96},{112,128},{144,160},{176,192},{208,224},{2... | collective-permute-start | bytes 663560 | tf_op jit(solution)/shard_map/ppermute | solution.py:498
  19.8 20.4 %collective-permute-start = (f32[54,8,128]{2,1,0:T(8,128)S(1)}, f32[54,8,128]{2,1,0:T(8,128)S(1)}, u32[]{:S(2)}, u32[]{:S(2)}) collective-permute-start(f32[54,8,128]{2,1,0:T(8,128)S(1)} %get-tuple-element.14.own_ref), channel_id=1, source_target_pairs={{0,16},{32,48},{64,80},{96,112},{128,144},{160,176},{192,208},{224... | collective-permute-start | bytes 663560 | tf_op jit(solution)/shard_map/ppermute | solution.py:498
  41.5 24.9 %collective-permute-start.3 = (f32[168,8,128]{2,1,0:T(8,128)}, f32[168,8,128]{2,1,0:T(8,128)S(1)}, u32[]{:S(2)}, u32[]{:S(2)}) collective-permute-start(f32[168,8,128]{2,1,0:T(8,128)} %get-tuple-element.20), channel_id=1, source_target_pairs={{4,8},{12,0},{8,4},{0,12},{5,9},{13,1},{9,5},{1,13},{6,10},{14,2},... | collective-permute-start | bytes 2064392 | tf_op jit(solution)/shard_map/ppermute | solution.py:498
  44.3 22.1 %collective-permute-start.2 = (f32[168,8,128]{2,1,0:T(8,128)S(1)}, f32[168,8,128]{2,1,0:T(8,128)S(1)}, u32[]{:S(2)}, u32[]{:S(2)}) collective-permute-start(f32[168,8,128]{2,1,0:T(8,128)S(1)} %get-tuple-element.18.own_ref), channel_id=1, source_target_pairs={{0,4},{8,12},{4,0},{12,8},{1,5},{9,13},{5,1},{13,9},{2,6},{10,14},... | collective-permute-start | bytes 2064392 | tf_op jit(solution)/shard_map/ppermute | solution.py:498

commit v9 on v8

--- a/solution.py
+++ b/solution.py
@@ -33,6 +33,7 @@
 A_TILES = AUX * (XA + XG)
 Y_FULL = FULL * (XE + XG)
 YT = Y_FULL + A_TILES // 4
+GRANT = 28 << 20
 SCRATCH = [(PLANES, ROWS, LANES)] * 12 + [
     (FULL - 1, PLANES, ROWS, LANES),
     (AUX, A_PLANES, ROWS, LANES),
@@ -509,6 +510,7 @@
         in_specs=[space] * len(args),
         out_specs=[space] * len(out),
         scratch_shapes=[pltpu.VMEM(shape, jnp.float32) for shape in scratch],
+        compiler_params=pltpu.CompilerParams(vmem_limit_bytes=GRANT),
         name=kernel.__name__,
     )(*args)
 

time: 73.8 us -> 76.3 us (1.034)
  local copies, waits for them, and re-layouts: 0 us -> 4.05 us
  Pallas kernels: 10 us -> 8.2 us
    unnamed x0 -> x10, local copies, waits for them, and re-layouts: none -> 4.05 us
    pallas_call x4, Pallas kernels: 10 us -> 8.2 us  [on_core(): pl.pallas_call(kernel, out_shape=shape, in_specs=[space] * len(args), out...]
where the time goes in v9:
time: 76.3 us; the launch traced here: 75.7 us
  blocking collectives  41.2 us (54%)
  starting transfers between devices  21.5 us (28%)
  Pallas kernels  8.2 us (11%)
  local copies, waits for them, and re-layouts  4.05 us (5%)
    all_to_all x1, blocking collectives, on_device(): low = lax.all_to_all(low, ('gx_0', 'gx_1'), 0, 0, tiled=True)  20.2 us
    ppermute x2, starting transfers between devices, exchange(): lax.ppermute(first, axis, swaps)  13.5 us
    all_to_all x1, blocking collectives, on_device(): edges = lax.all_to_all(edges, 'gz', 0, 0, tiled=True)  12.2 us
    all_to_all x1, blocking collectives, on_device(): low = lax.all_to_all(low, ('gx_2', 'gy'), 0, 0, tiled=True)  8.8 us
    pallas_call x4, Pallas kernels, on_core(): pl.pallas_call(kernel, out_shape=shape, in_specs=[space] * len(args), out...  8.2 us
    ppermute x2, starting transfers between devices, exchange(): lax.ppermute(second, axis, others)  8 us
    unnamed x10, local copies, waits for them, and re-layouts  4.05 us
  transfers between devices with their start and end apart: 4, of which 0 were waited for; matrix products, arithmetic and copies ran while one was open for 0% of the time, Pallas kernels for 0%

profile of v9, /device:TPU:1, one launch (start us, length us, event | category | flops | bytes accessed | tf_op | source)
XLA Modules:
  0.0 75.7 jit_solution(1736413425317545564)
XLA Ops:
  0.6 0.0 copy-start
  0.6 0.9 %copy-done = f32[3,8,8,128]{3,2,1,0:T(8,128)S(1)} copy-done((f32[3,8,8,128]{3,2,1,0:T(8,128)S(1)}, f32[3,8,8,128]{3,2,1,0:T(8,128)}, u32[]{:S(2)}) %copy-start) | copy-done | bytes 98328
  1.5 0.0 copy-start.1
  1.5 0.9 %copy-done.1 = f32[3,8,8,128]{3,2,1,0:T(8,128)S(1)} copy-done((f32[3,8,8,128]{3,2,1,0:T(8,128)S(1)}, f32[3,8,8,128]{3,2,1,0:T(8,128)}, u32[]{:S(2)}) %copy-start.1) | copy-done | bytes 98328
  2.4 0.0 copy-start.2
  2.4 0.8 copy-done.2
  3.2 0.0 copy-start.3
  3.2 0.8 copy-done.3
  3.9 0.0 copy-start.4
  3.9 0.8 copy-done.4
  4.7 0.2 pack_z.1
  4.9 12.2 %all_to_all.15.z_ref = f32[4,5,8,128]{3,2,1,0:T(8,128)S(1)} all-to-all(f32[4,5,8,128]{3,2,1,0:T(8,128)S(1)} %get-tuple-element.13), channel_id=1, replica_groups=mesh['gx_0'=3,'gx_1'=8,'gx_2'=2,'gy'=4,'gz'=4] {'gz'}, dimensions={0} | all-to-all | bytes 163840 | tf_op jit(solution)/shard_map/all_to_all | solution.py:528
  17.2 0.5 pack_x.1
  17.7 5.2 %collective-permute-start.1 = (f32[54,8,128]{2,1,0:T(8,128)S(1)}, f32[54,8,128]{2,1,0:T(8,128)S(1)}, u32[]{:S(2)}, u32[]{:S(2)}) collective-permute-start(f32[54,8,128]{2,1,0:T(8,128)S(1)} %get-tuple-element.16), channel_id=1, source_target_pairs={{16,32},{48,64},{80,96},{112,128},{144,160},{176,192},{208,224},{2... | collective-permute-start | bytes 663560 | tf_op jit(solution)/shard_map/ppermute | solution.py:499
  22.9 11.6 %collective-permute-start = (f32[54,8,128]{2,1,0:T(8,128)S(1)}, f32[54,8,128]{2,1,0:T(8,128)S(1)}, u32[]{:S(2)}, u32[]{:S(2)}) collective-permute-start(f32[54,8,128]{2,1,0:T(8,128)S(1)} %get-tuple-element.14.own_ref), channel_id=1, source_target_pairs={{0,16},{32,48},{64,80},{96,112},{128,144},{160,176},{192,208},{224... | collective-permute-start | bytes 663560 | tf_op jit(solution)/shard_map/ppermute | solution.py:499
  34.5 8.8 %all_to_all.16.min_ref = f32[8,1,128]{2,1,0:T(1,128)S(1)} all-to-all(f32[8,1,128]{2,1,0:T(1,128)S(1)} %get-tuple-element.17), channel_id=1, replica_groups=mesh['gx_0'=3,'gx_1'=8,'gx_2'=2,'gy'=4,'gz'=4] {'gx_2','gy'}, dimensions={0} | all-to-all | bytes 8192 | tf_op jit(solution)/shard_map/all_to_all | solution.py:533
  43.3 0.0 collective-permute-done.1.xo_ref
  43.3 0.0 collective-permute-done.xa_ref
  43.3 0.4 pack_y.1
  43.7 2.8 %collective-permute-start.3 = (f32[168,8,128]{2,1,0:T(8,128)S(1)}, f32[168,8,128]{2,1,0:T(8,128)S(1)}, u32[]{:S(2)}, u32[]{:S(2)}) collective-permute-start(f32[168,8,128]{2,1,0:T(8,128)S(1)} %get-tuple-element.20), channel_id=1, source_target_pairs={{4,8},{12,0},{8,4},{0,12},{5,9},{13,1},{9,5},{1,13},{6,10},{14,2},... | collective-permute-start | bytes 2064392 | tf_op jit(solution)/shard_map/ppermute | solution.py:499
  46.5 1.9 %collective-permute-start.2 = (f32[168,8,128]{2,1,0:T(8,128)S(1)}, f32[168,8,128]{2,1,0:T(8,128)S(1)}, u32[]{:S(2)}, u32[]{:S(2)}) collective-permute-start(f32[168,8,128]{2,1,0:T(8,128)S(1)} %get-tuple-element.18.own_ref), channel_id=1, source_target_pairs={{0,4},{8,12},{4,0},{12,8},{1,5},{9,13},{5,1},{13,9},{2,6},{10,14},... | collective-permute-start | bytes 2064392 | tf_op jit(solution)/shard_map/ppermute | solution.py:499
  48.5 20.2 %all_to_all.17.low_ref = f32[24,1,128]{2,1,0:T(1,128)S(1)} all-to-all(f32[24,1,128]{2,1,0:T(1,128)S(1)} %get-tuple-element.21), channel_id=1, replica_groups=mesh['gx_0'=3,'gx_1'=8,'gx_2'=2,'gy'=4,'gz'=4] {'gx_0','gx_1'}, dimensions={0} | all-to-all | bytes 24576 | tf_op jit(solution)/shard_map/all_to_all | solution.py:538
  68.6 0.0 collective-permute-done.3.yo_ref
  68.6 0.0 collective-permute-done.2.ya_ref
  68.6 7.0 %advance.1 = (f32[8,8,128]{2,1,0:T(8,128)}, f32[3,8,8,128]{3,2,1,0:T(8,128)}) custom-call(f32[168,8,128]{2,1,0:T(8,128)S(1)} %get-tuple-element.18.own_ref, f32[72,8,128]{2,1,0:T(8,128)S(1)} %get-tuple-element.19.aux_ref, f32[168,8,128]{2,1,0:T(8,128)S(1)} %collective-permute-done.2.ya_ref, f32[168,8,128]{2,1,0:T(8,128)S(1)} %collective-permute-done.3.yo_ref, ...), custom_call_target="tpu_custom_call" | custom-call | tf_op jit(solution)/shard_map/advance/pallas_call | solution.py:507
Async XLA Ops:
  0.6 0.9 %copy-start = (f32[3,8,8,128]{3,2,1,0:T(8,128)S(1)}, f32[3,8,8,128]{3,2,1,0:T(8,128)}, u32[]{:S(2)}) copy-start(f32[3,8,8,128]{3,2,1,0:T(8,128)} %b_ref.1) | copy-start | bytes 294916
  1.5 0.9 %copy-start.1 = (f32[3,8,8,128]{3,2,1,0:T(8,128)S(1)}, f32[3,8,8,128]{3,2,1,0:T(8,128)}, u32[]{:S(2)}) copy-start(f32[3,8,8,128]{3,2,1,0:T(8,128)} %v_ref.1) | copy-start | bytes 294916
  2.4 0.8 %copy-start.2 = (f32[8,8,128]{2,1,0:T(8,128)S(1)}, f32[8,8,128]{2,1,0:T(8,128)}, u32[]{:S(2)}) copy-start(f32[8,8,128]{2,1,0:T(8,128)} %t_ref.1) | copy-start | bytes 98308
  3.2 0.8 %copy-start.3 = (f32[8,8,128]{2,1,0:T(8,128)S(1)}, f32[8,8,128]{2,1,0:T(8,128)}, u32[]{:S(2)}) copy-start(f32[8,8,128]{2,1,0:T(8,128)} %d_ref.1) | copy-start | bytes 98308
  3.9 0.8 %copy-start.4 = (f32[8,8,128]{2,1,0:T(8,128)S(1)}, f32[8,8,128]{2,1,0:T(8,128)}, u32[]{:S(2)}) copy-start(f32[8,8,128]{2,1,0:T(8,128)} %r_ref.1) | copy-start | bytes 98308
  17.7 25.6 %collective-permute-start.1 = (f32[54,8,128]{2,1,0:T(8,128)S(1)}, f32[54,8,128]{2,1,0:T(8,128)S(1)}, u32[]{:S(2)}, u32[]{:S(2)}) collective-permute-start(f32[54,8,128]{2,1,0:T(8,128)S(1)} %get-tuple-element.16), channel_id=1, source_target_pairs={{16,32},{48,64},{80,96},{112,128},{144,160},{176,192},{208,224},{2... | collective-permute-start | bytes 663560 | tf_op jit(solution)/shard_map/ppermute | solution.py:499
  22.9 20.4 %collective-permute-start = (f32[54,8,128]{2,1,0:T(8,128)S(1)}, f32[54,8,128]{2,1,0:T(8,128)S(1)}, u32[]{:S(2)}, u32[]{:S(2)}) collective-permute-start(f32[54,8,128]{2,1,0:T(8,128)S(1)} %get-tuple-element.14.own_ref), channel_id=1, source_target_pairs={{0,16},{32,48},{64,80},{96,112},{128,144},{160,176},{192,208},{224... | collective-permute-start | bytes 663560 | tf_op jit(solution)/shard_map/ppermute | solution.py:499
  43.7 24.9 %collective-permute-start.3 = (f32[168,8,128]{2,1,0:T(8,128)S(1)}, f32[168,8,128]{2,1,0:T(8,128)S(1)}, u32[]{:S(2)}, u32[]{:S(2)}) collective-permute-start(f32[168,8,128]{2,1,0:T(8,128)S(1)} %get-tuple-element.20), channel_id=1, source_target_pairs={{4,8},{12,0},{8,4},{0,12},{5,9},{13,1},{9,5},{1,13},{6,10},{14,2},... | collective-permute-start | bytes 2064392 | tf_op jit(solution)/shard_map/ppermute | solution.py:499
  46.5 22.1 %collective-permute-start.2 = (f32[168,8,128]{2,1,0:T(8,128)S(1)}, f32[168,8,128]{2,1,0:T(8,128)S(1)}, u32[]{:S(2)}, u32[]{:S(2)}) collective-permute-start(f32[168,8,128]{2,1,0:T(8,128)S(1)} %get-tuple-element.18.own_ref), channel_id=1, source_target_pairs={{0,4},{8,12},{4,0},{12,8},{1,5},{9,13},{5,1},{13,9},{2,6},{10,14},... | collective-permute-start | bytes 2064392 | tf_op jit(solution)/shard_map/ppermute | solution.py:499

commit v10 on v9

--- a/solution.py
+++ b/solution.py
@@ -499,7 +499,7 @@
     return lax.ppermute(first, axis, swaps), lax.ppermute(second, axis, others)
 
 
-def on_core(kernel, out, *args, scratch=(), last=False):
+def on_core(kernel, out, *args, scratch=(), last=False, grant=GRANT):
     space = pl.BlockSpec(memory_space=pltpu.VMEM)
     shape = [
         jax.ShapeDtypeStruct(o, jnp.float32) if last else pltpu.VMEM(o, jnp.float32) for o in out
@@ -510,7 +510,7 @@
         in_specs=[space] * len(args),
         out_specs=[space] * len(out),
         scratch_shapes=[pltpu.VMEM(shape, jnp.float32) for shape in scratch],
-        compiler_params=pltpu.CompilerParams(vmem_limit_bytes=GRANT),
+        compiler_params=pltpu.CompilerParams(vmem_limit_bytes=grant),
         name=kernel.__name__,
     )(*args)
 
@@ -524,7 +524,7 @@
     outer = lax.axis_size("gx_2") * lax.axis_size("gy")
     inner = lax.axis_size("gx_0") * lax.axis_size("gx_1")
     out = [((FULL + AUX) * W, W, LANES), (zs, ZT, W, LANES)]
-    cells, edges = on_core(pack_z, out, t, diffusivity, b, v, rho)
+    cells, edges = on_core(pack_z, out, t, diffusivity, b, v, rho, grant=None)
     edges = lax.all_to_all(edges, "gz", 0, 0, tiled=True)
     cells, edges = held(cells, edges)
     out = [(SIDE, W, LANES)] * 2 + [((W + 1) * AUX, W, LANES), (outer, 1, LANES)]

time: 76.3 us -> 73 us (0.957)
  local copies, waits for them, and re-layouts: 4.05 us -> 0 us
  Pallas kernels: 8.2 us -> 9.18 us
    unnamed x10 -> x0, local copies, waits for them, and re-layouts: 4.05 us -> none
    pallas_call x4, Pallas kernels: 8.2 us -> 9.18 us  [on_core(): pl.pallas_call(kernel, out_shape=shape, in_specs=[space] * len(args), out...]
where the time goes in v10:
time: 73 us; the launch traced here: 72.6 us
  blocking collectives  41.2 us (56%)
  starting transfers between devices  21.5 us (29%)
  Pallas kernels  9.18 us (13%)
    all_to_all x1, blocking collectives, on_device(): low = lax.all_to_all(low, ('gx_0', 'gx_1'), 0, 0, tiled=True)  20.2 us
    ppermute x2, starting transfers between devices, exchange(): lax.ppermute(first, axis, swaps)  13.5 us
    all_to_all x1, blocking collectives, on_device(): edges = lax.all_to_all(edges, 'gz', 0, 0, tiled=True)  12.2 us
    pallas_call x4, Pallas kernels, on_core(): pl.pallas_call(kernel, out_shape=shape, in_specs=[space] * len(args), out...  9.18 us
    all_to_all x1, blocking collectives, on_device(): low = lax.all_to_all(low, ('gx_2', 'gy'), 0, 0, tiled=True)  8.8 us
    ppermute x2, starting transfers between devices, exchange(): lax.ppermute(second, axis, others)  8 us
  transfers between devices with their start and end apart: 4, of which 0 were waited for; matrix products, arithmetic and copies ran while one was open for 0% of the time, Pallas kernels for 0%

profile of v10, /device:TPU:1, one launch (start us, length us, event | category | flops | bytes accessed | tf_op | source)
XLA Modules:
  0.0 72.6 jit_solution(17115689147956472773)
XLA Ops:
  0.6 1.2 %pack_z.1 = (f32[72,8,128]{2,1,0:T(8,128)S(1)}, f32[4,5,8,128]{3,2,1,0:T(8,128)S(1)}) custom-call(f32[8,8,128]{2,1,0:T(8,128)} %t_ref.1, f32[8,8,128]{2,1,0:T(8,128)} %d_ref.1, f32[3,8,8,128]{3,2,1,0:T(8,128)} %b_ref.1, f32[3,8,8,128]{3,2,1,0:T(8,128)} %v_ref.1, f32[8,8,128]{2,1,0:T(8,128)} %r_ref.1), custom_call_target="tpu_custom_call" | custom-call | tf_op jit(solution)/shard_map/pack_z/pallas_call | solution.py:507
  1.8 12.2 %all_to_all.15.z_ref = f32[4,5,8,128]{3,2,1,0:T(8,128)S(1)} all-to-all(f32[4,5,8,128]{3,2,1,0:T(8,128)S(1)} %get-tuple-element.13), channel_id=1, replica_groups=mesh['gx_0'=3,'gx_1'=8,'gx_2'=2,'gy'=4,'gz'=4] {'gz'}, dimensions={0} | all-to-all | bytes 163840 | tf_op jit(solution)/shard_map/all_to_all | solution.py:528
  14.1 0.5 pack_x.1
  14.6 5.2 %collective-permute-start.1 = (f32[54,8,128]{2,1,0:T(8,128)S(1)}, f32[54,8,128]{2,1,0:T(8,128)S(1)}, u32[]{:S(2)}, u32[]{:S(2)}) collective-permute-start(f32[54,8,128]{2,1,0:T(8,128)S(1)} %get-tuple-element.16), channel_id=1, source_target_pairs={{16,32},{48,64},{80,96},{112,128},{144,160},{176,192},{208,224},{2... | collective-permute-start | bytes 663560 | tf_op jit(solution)/shard_map/ppermute | solution.py:499
  19.8 11.6 %collective-permute-start = (f32[54,8,128]{2,1,0:T(8,128)S(1)}, f32[54,8,128]{2,1,0:T(8,128)S(1)}, u32[]{:S(2)}, u32[]{:S(2)}) collective-permute-start(f32[54,8,128]{2,1,0:T(8,128)S(1)} %get-tuple-element.14.own_ref), channel_id=1, source_target_pairs={{0,16},{32,48},{64,80},{96,112},{128,144},{160,176},{192,208},{224... | collective-permute-start | bytes 663560 | tf_op jit(solution)/shard_map/ppermute | solution.py:499
  31.4 8.8 %all_to_all.16.min_ref = f32[8,1,128]{2,1,0:T(1,128)S(1)} all-to-all(f32[8,1,128]{2,1,0:T(1,128)S(1)} %get-tuple-element.17), channel_id=1, replica_groups=mesh['gx_0'=3,'gx_1'=8,'gx_2'=2,'gy'=4,'gz'=4] {'gx_2','gy'}, dimensions={0} | all-to-all | bytes 8192 | tf_op jit(solution)/shard_map/all_to_all | solution.py:533
  40.2 0.0 collective-permute-done.1.xo_ref
  40.2 0.0 collective-permute-done.xa_ref
  40.2 0.4 pack_y.1
  40.6 2.8 %collective-permute-start.3 = (f32[168,8,128]{2,1,0:T(8,128)S(1)}, f32[168,8,128]{2,1,0:T(8,128)S(1)}, u32[]{:S(2)}, u32[]{:S(2)}) collective-permute-start(f32[168,8,128]{2,1,0:T(8,128)S(1)} %get-tuple-element.20), channel_id=1, source_target_pairs={{4,8},{12,0},{8,4},{0,12},{5,9},{13,1},{9,5},{1,13},{6,10},{14,2},... | collective-permute-start | bytes 2064392 | tf_op jit(solution)/shard_map/ppermute | solution.py:499
  43.5 1.9 %collective-permute-start.2 = (f32[168,8,128]{2,1,0:T(8,128)S(1)}, f32[168,8,128]{2,1,0:T(8,128)S(1)}, u32[]{:S(2)}, u32[]{:S(2)}) collective-permute-start(f32[168,8,128]{2,1,0:T(8,128)S(1)} %get-tuple-element.18.own_ref), channel_id=1, source_target_pairs={{0,4},{8,12},{4,0},{12,8},{1,5},{9,13},{5,1},{13,9},{2,6},{10,14},... | collective-permute-start | bytes 2064392 | tf_op jit(solution)/shard_map/ppermute | solution.py:499
  45.4 20.2 %all_to_all.17.low_ref = f32[24,1,128]{2,1,0:T(1,128)S(1)} all-to-all(f32[24,1,128]{2,1,0:T(1,128)S(1)} %get-tuple-element.21), channel_id=1, replica_groups=mesh['gx_0'=3,'gx_1'=8,'gx_2'=2,'gy'=4,'gz'=4] {'gx_0','gx_1'}, dimensions={0} | all-to-all | bytes 24576 | tf_op jit(solution)/shard_map/all_to_all | solution.py:538
  65.6 0.0 collective-permute-done.3.yo_ref
  65.6 0.0 collective-permute-done.2.ya_ref
  65.6 7.0 %advance.1 = (f32[8,8,128]{2,1,0:T(8,128)}, f32[3,8,8,128]{3,2,1,0:T(8,128)}) custom-call(f32[168,8,128]{2,1,0:T(8,128)S(1)} %get-tuple-element.18.own_ref, f32[72,8,128]{2,1,0:T(8,128)S(1)} %get-tuple-element.19.aux_ref, f32[168,8,128]{2,1,0:T(8,128)S(1)} %collective-permute-done.2.ya_ref, f32[168,8,128]{2,1,0:T(8,128)S(1)} %collective-permute-done.3.yo_ref, ...), custom_call_target="tpu_custom_call" | custom-call | tf_op jit(solution)/shard_map/advance/pallas_call | solution.py:507
Async XLA Ops:
  14.6 25.6 %collective-permute-start.1 = (f32[54,8,128]{2,1,0:T(8,128)S(1)}, f32[54,8,128]{2,1,0:T(8,128)S(1)}, u32[]{:S(2)}, u32[]{:S(2)}) collective-permute-start(f32[54,8,128]{2,1,0:T(8,128)S(1)} %get-tuple-element.16), channel_id=1, source_target_pairs={{16,32},{48,64},{80,96},{112,128},{144,160},{176,192},{208,224},{2... | collective-permute-start | bytes 663560 | tf_op jit(solution)/shard_map/ppermute | solution.py:499
  19.8 20.4 %collective-permute-start = (f32[54,8,128]{2,1,0:T(8,128)S(1)}, f32[54,8,128]{2,1,0:T(8,128)S(1)}, u32[]{:S(2)}, u32[]{:S(2)}) collective-permute-start(f32[54,8,128]{2,1,0:T(8,128)S(1)} %get-tuple-element.14.own_ref), channel_id=1, source_target_pairs={{0,16},{32,48},{64,80},{96,112},{128,144},{160,176},{192,208},{224... | collective-permute-start | bytes 663560 | tf_op jit(solution)/shard_map/ppermute | solution.py:499
  40.6 24.9 %collective-permute-start.3 = (f32[168,8,128]{2,1,0:T(8,128)S(1)}, f32[168,8,128]{2,1,0:T(8,128)S(1)}, u32[]{:S(2)}, u32[]{:S(2)}) collective-permute-start(f32[168,8,128]{2,1,0:T(8,128)S(1)} %get-tuple-element.20), channel_id=1, source_target_pairs={{4,8},{12,0},{8,4},{0,12},{5,9},{13,1},{9,5},{1,13},{6,10},{14,2},... | collective-permute-start | bytes 2064392 | tf_op jit(solution)/shard_map/ppermute | solution.py:499
  43.5 22.1 %collective-permute-start.2 = (f32[168,8,128]{2,1,0:T(8,128)S(1)}, f32[168,8,128]{2,1,0:T(8,128)S(1)}, u32[]{:S(2)}, u32[]{:S(2)}) collective-permute-start(f32[168,8,128]{2,1,0:T(8,128)S(1)} %get-tuple-element.18.own_ref), channel_id=1, source_target_pairs={{0,4},{8,12},{4,0},{12,8},{1,5},{9,13},{5,1},{13,9},{2,6},{10,14},... | collective-permute-start | bytes 2064392 | tf_op jit(solution)/shard_map/ppermute | solution.py:499

commit v11 on v10

--- a/solution.py
+++ b/solution.py
@@ -521,8 +521,8 @@
 
 def on_device(t, diffusivity, b, v, rho):
     zs = lax.axis_size("gz")
-    outer = lax.axis_size("gx_2") * lax.axis_size("gy")
-    inner = lax.axis_size("gx_0") * lax.axis_size("gx_1")
+    outer = lax.axis_size("gx_1") * lax.axis_size("gy")
+    inner = lax.axis_size("gx_0") * lax.axis_size("gx_2")
     out = [((FULL + AUX) * W, W, LANES), (zs, ZT, W, LANES)]
     cells, edges = on_core(pack_z, out, t, diffusivity, b, v, rho, grant=None)
     edges = lax.all_to_all(edges, "gz", 0, 0, tiled=True)
@@ -530,12 +530,12 @@
     out = [(SIDE, W, LANES)] * 2 + [((W + 1) * AUX, W, LANES), (outer, 1, LANES)]
     first, second, aux, low = on_core(pack_x, out, cells, edges)
     x_first, x_second = exchange(first, second, GX)
-    low = lax.all_to_all(low, ("gx_2", "gy"), 0, 0, tiled=True)
+    low = lax.all_to_all(low, ("gx_1", "gy"), 0, 0, tiled=True)
     args = held(first, aux, x_first, x_second, low)
     out = [(YT, W, LANES)] * 2 + [(A_TILES, W, LANES), (inner, 1, LANES)]
     first, second, aux, low = on_core(pack_y, out, *args)
     y_first, y_second = exchange(first, second, "gy")
-    low = lax.all_to_all(low, ("gx_0", "gx_1"), 0, 0, tiled=True)
+    low = lax.all_to_all(low, ("gx_0", "gx_2"), 0, 0, tiled=True)
     out = [(W, W, LANES), (3, W, W, LANES)]
     args = held(first, aux, y_first, y_second, low)
     return tuple(on_core(advance, out, *args, scratch=SCRATCH, last=True))

time: 73 us -> 72.4 us (level)
  blocking collectives: 41.2 us -> 40 us
    all_to_all x2, blocking collectives: 29 us -> 27.7 us  [the longest x1 14.9 us: on_device(): low = lax.all_to_all(low, ('gx_0', 'gx_2'), 0, 0, tiled=True)]
  transfers between devices with their start and end apart: 4 -> 4, of which waited for: 0 -> 1; matrix products, arithmetic and copies ran while one was open for 0% -> 0% of each run, Pallas kernels for 0% -> 0%
where the time goes in v11:
time: 72.4 us; the launch traced here: 71.6 us
  blocking collectives  40 us (55%)
  starting transfers between devices  21.6 us (30%)
  Pallas kernels  9.17 us (13%)
    all_to_all x1, blocking collectives, on_device(): low = lax.all_to_all(low, ('gx_0', 'gx_2'), 0, 0, tiled=True)  14.9 us
    ppermute x2, starting transfers between devices, exchange(): lax.ppermute(first, axis, swaps)  13.5 us
    all_to_all x1, blocking collectives, on_device(): low = lax.all_to_all(low, ('gx_1', 'gy'), 0, 0, tiled=True)  12.8 us
    all_to_all x1, blocking collectives, on_device(): edges = lax.all_to_all(edges, 'gz', 0, 0, tiled=True)  12.2 us
    pallas_call x4, Pallas kernels, on_core(): pl.pallas_call(kernel, out_shape=shape, in_specs=[space] * len(args), out...  9.17 us
    ppermute x2, starting transfers between devices, exchange(): lax.ppermute(second, axis, others)  8.05 us
  transfers between devices with their start and end apart: 4, of which 1 were waited for; matrix products, arithmetic and copies ran while one was open for 0% of the time, Pallas kernels for 0%

profile of v11, /device:TPU:1, one launch (start us, length us, event | category | flops | bytes accessed | tf_op | source)
XLA Modules:
  0.0 71.6 jit_solution(5195775260314887814)
XLA Ops:
  0.6 1.2 %pack_z.1 = (f32[72,8,128]{2,1,0:T(8,128)S(1)}, f32[4,5,8,128]{3,2,1,0:T(8,128)S(1)}) custom-call(f32[8,8,128]{2,1,0:T(8,128)} %t_ref.1, f32[8,8,128]{2,1,0:T(8,128)} %d_ref.1, f32[3,8,8,128]{3,2,1,0:T(8,128)} %b_ref.1, f32[3,8,8,128]{3,2,1,0:T(8,128)} %v_ref.1, f32[8,8,128]{2,1,0:T(8,128)} %r_ref.1), custom_call_target="tpu_custom_call" | custom-call | tf_op jit(solution)/shard_map/pack_z/pallas_call | solution.py:507
  1.8 12.2 %all_to_all.15.z_ref = f32[4,5,8,128]{3,2,1,0:T(8,128)S(1)} all-to-all(f32[4,5,8,128]{3,2,1,0:T(8,128)S(1)} %get-tuple-element.13), channel_id=1, replica_groups=mesh['gx_0'=3,'gx_1'=8,'gx_2'=2,'gy'=4,'gz'=4] {'gz'}, dimensions={0} | all-to-all | bytes 163840 | tf_op jit(solution)/shard_map/all_to_all | solution.py:528
  14.1 0.5 pack_x.1
  14.6 5.2 %collective-permute-start.1 = (f32[54,8,128]{2,1,0:T(8,128)S(1)}, f32[54,8,128]{2,1,0:T(8,128)S(1)}, u32[]{:S(2)}, u32[]{:S(2)}) collective-permute-start(f32[54,8,128]{2,1,0:T(8,128)S(1)} %get-tuple-element.16), channel_id=1, source_target_pairs={{16,32},{48,64},{80,96},{112,128},{144,160},{176,192},{208,224},{2... | collective-permute-start | bytes 663560 | tf_op jit(solution)/shard_map/ppermute | solution.py:499
  19.8 11.6 %collective-permute-start = (f32[54,8,128]{2,1,0:T(8,128)S(1)}, f32[54,8,128]{2,1,0:T(8,128)S(1)}, u32[]{:S(2)}, u32[]{:S(2)}) collective-permute-start(f32[54,8,128]{2,1,0:T(8,128)S(1)} %get-tuple-element.14.own_ref), channel_id=1, source_target_pairs={{0,16},{32,48},{64,80},{96,112},{128,144},{160,176},{192,208},{224... | collective-permute-start | bytes 663560 | tf_op jit(solution)/shard_map/ppermute | solution.py:499
  31.4 12.8 %all_to_all.16.min_ref = f32[32,1,128]{2,1,0:T(1,128)S(1)} all-to-all(f32[32,1,128]{2,1,0:T(1,128)S(1)} %get-tuple-element.17), channel_id=1, replica_groups=mesh['gx_0'=3,'gx_1'=8,'gx_2'=2,'gy'=4,'gz'=4] {'gx_1','gy'}, dimensions={0} | all-to-all | bytes 32768 | tf_op jit(solution)/shard_map/all_to_all | solution.py:533
  44.2 0.0 collective-permute-done.1.xo_ref
  44.2 0.0 collective-permute-done.xa_ref
  44.2 0.4 pack_y.1
  44.7 2.9 %collective-permute-start.3 = (f32[168,8,128]{2,1,0:T(8,128)S(1)}, f32[168,8,128]{2,1,0:T(8,128)S(1)}, u32[]{:S(2)}, u32[]{:S(2)}) collective-permute-start(f32[168,8,128]{2,1,0:T(8,128)S(1)} %get-tuple-element.20), channel_id=1, source_target_pairs={{4,8},{12,0},{8,4},{0,12},{5,9},{13,1},{9,5},{1,13},{6,10},{14,2},... | collective-permute-start | bytes 2064392 | tf_op jit(solution)/shard_map/ppermute | solution.py:499
  47.5 1.9 %collective-permute-start.2 = (f32[168,8,128]{2,1,0:T(8,128)S(1)}, f32[168,8,128]{2,1,0:T(8,128)S(1)}, u32[]{:S(2)}, u32[]{:S(2)}) collective-permute-start(f32[168,8,128]{2,1,0:T(8,128)S(1)} %get-tuple-element.18.own_ref), channel_id=1, source_target_pairs={{0,4},{8,12},{4,0},{12,8},{1,5},{9,13},{5,1},{13,9},{2,6},{10,14},... | collective-permute-start | bytes 2064392 | tf_op jit(solution)/shard_map/ppermute | solution.py:499
  49.5 14.9 %all_to_all.17.low_ref = f32[6,1,128]{2,1,0:T(1,128)S(1)} all-to-all(f32[6,1,128]{2,1,0:T(1,128)S(1)} %get-tuple-element.21), channel_id=1, replica_groups=mesh['gx_0'=3,'gx_1'=8,'gx_2'=2,'gy'=4,'gz'=4] {'gx_0','gx_2'}, dimensions={0} | all-to-all | bytes 6144 | tf_op jit(solution)/shard_map/all_to_all | solution.py:538
  64.4 0.0 collective-permute-done.3.yo_ref
  64.4 0.3 collective-permute-done.2.ya_ref
  64.6 7.0 %advance.1 = (f32[8,8,128]{2,1,0:T(8,128)}, f32[3,8,8,128]{3,2,1,0:T(8,128)}) custom-call(f32[168,8,128]{2,1,0:T(8,128)S(1)} %get-tuple-element.18.own_ref, f32[72,8,128]{2,1,0:T(8,128)S(1)} %get-tuple-element.19.aux_ref, f32[168,8,128]{2,1,0:T(8,128)S(1)} %collective-permute-done.2.ya_ref, f32[168,8,128]{2,1,0:T(8,128)S(1)} %collective-permute-done.3.yo_ref, ...), custom_call_target="tpu_custom_call" | custom-call | tf_op jit(solution)/shard_map/advance/pallas_call | solution.py:507
Async XLA Ops:
  14.6 29.6 %collective-permute-start.1 = (f32[54,8,128]{2,1,0:T(8,128)S(1)}, f32[54,8,128]{2,1,0:T(8,128)S(1)}, u32[]{:S(2)}, u32[]{:S(2)}) collective-permute-start(f32[54,8,128]{2,1,0:T(8,128)S(1)} %get-tuple-element.16), channel_id=1, source_target_pairs={{16,32},{48,64},{80,96},{112,128},{144,160},{176,192},{208,224},{2... | collective-permute-start | bytes 663560 | tf_op jit(solution)/shard_map/ppermute | solution.py:499
  19.8 24.4 %collective-permute-start = (f32[54,8,128]{2,1,0:T(8,128)S(1)}, f32[54,8,128]{2,1,0:T(8,128)S(1)}, u32[]{:S(2)}, u32[]{:S(2)}) collective-permute-start(f32[54,8,128]{2,1,0:T(8,128)S(1)} %get-tuple-element.14.own_ref), channel_id=1, source_target_pairs={{0,16},{32,48},{64,80},{96,112},{128,144},{160,176},{192,208},{224... | collective-permute-start | bytes 663560 | tf_op jit(solution)/shard_map/ppermute | solution.py:499
  44.7 19.7 %collective-permute-start.3 = (f32[168,8,128]{2,1,0:T(8,128)S(1)}, f32[168,8,128]{2,1,0:T(8,128)S(1)}, u32[]{:S(2)}, u32[]{:S(2)}) collective-permute-start(f32[168,8,128]{2,1,0:T(8,128)S(1)} %get-tuple-element.20), channel_id=1, source_target_pairs={{4,8},{12,0},{8,4},{0,12},{5,9},{13,1},{9,5},{1,13},{6,10},{14,2},... | collective-permute-start | bytes 2064392 | tf_op jit(solution)/shard_map/ppermute | solution.py:499
  47.5 17.1 %collective-permute-start.2 = (f32[168,8,128]{2,1,0:T(8,128)S(1)}, f32[168,8,128]{2,1,0:T(8,128)S(1)}, u32[]{:S(2)}, u32[]{:S(2)}) collective-permute-start(f32[168,8,128]{2,1,0:T(8,128)S(1)} %get-tuple-element.18.own_ref), channel_id=1, source_target_pairs={{0,4},{8,12},{4,0},{12,8},{1,5},{9,13},{5,1},{13,9},{2,6},{10,14},... | collective-permute-start | bytes 2064392 | tf_op jit(solution)/shard_map/ppermute | solution.py:499

commit v12 on v11

--- a/solution.py
+++ b/solution.py
@@ -521,8 +521,8 @@
 
 def on_device(t, diffusivity, b, v, rho):
     zs = lax.axis_size("gz")
-    outer = lax.axis_size("gx_1") * lax.axis_size("gy")
-    inner = lax.axis_size("gx_0") * lax.axis_size("gx_2")
+    outer = lax.axis_size("gx_1") * lax.axis_size("gx_2") * lax.axis_size("gy")
+    inner = lax.axis_size("gx_0")
     out = [((FULL + AUX) * W, W, LANES), (zs, ZT, W, LANES)]
     cells, edges = on_core(pack_z, out, t, diffusivity, b, v, rho, grant=None)
     edges = lax.all_to_all(edges, "gz", 0, 0, tiled=True)
@@ -530,12 +530,12 @@
     out = [(SIDE, W, LANES)] * 2 + [((W + 1) * AUX, W, LANES), (outer, 1, LANES)]
     first, second, aux, low = on_core(pack_x, out, cells, edges)
     x_first, x_second = exchange(first, second, GX)
-    low = lax.all_to_all(low, ("gx_1", "gy"), 0, 0, tiled=True)
+    low = lax.all_to_all(low, ("gx_1", "gx_2", "gy"), 0, 0, tiled=True)
     args = held(first, aux, x_first, x_second, low)
     out = [(YT, W, LANES)] * 2 + [(A_TILES, W, LANES), (inner, 1, LANES)]
     first, second, aux, low = on_core(pack_y, out, *args)
     y_first, y_second = exchange(first, second, "gy")
-    low = lax.all_to_all(low, ("gx_0", "gx_2"), 0, 0, tiled=True)
+    low = lax.all_to_all(low, "gx_0", 0, 0, tiled=True)
     out = [(W, W, LANES), (3, W, W, LANES)]
     args = held(first, aux, y_first, y_second, low)
     return tuple(on_core(advance, out, *args, scratch=SCRATCH, last=True))

time: 72.4 us -> 74.2 us (1.025)
  waiting for transfers between devices: 0.26 us -> 3.81 us
  blocking collectives: 40 us -> 38.5 us
    ppermute x2, waiting for transfers between devices: 0.01 us -> 1.93 us  [exchange(): lax.ppermute(second, axis, others)]
    ppermute x2, waiting for transfers between devices: 0.25 us -> 1.88 us  [exchange(): lax.ppermute(first, axis, swaps)]
    all_to_all x2, blocking collectives: 27.7 us -> 26.3 us  [the longest x1 14 us: on_device(): low = lax.all_to_all(low, ('gx_1', 'gx_2', 'gy'), 0, 0, tiled=True)]
  transfers between devices with their start and end apart: 4 -> 4, of which waited for: 1 -> 2; matrix products, arithmetic and copies ran while one was open for 0% -> 0% of each run, Pallas kernels for 0% -> 0%
where the time goes in v12:
time: 74.2 us; the launch traced here: 73.9 us
  blocking collectives  38.5 us (52%)
  starting transfers between devices  21.7 us (29%)
  Pallas kernels  9.19 us (12%)
  waiting for transfers between devices  3.81 us (5%)
    all_to_all x1, blocking collectives, on_device(): low = lax.all_to_all(low, ('gx_1', 'gx_2', 'gy'), 0, 0, tiled=True)  14 us
    ppermute x2, starting transfers between devices, exchange(): lax.ppermute(first, axis, swaps)  13.5 us
    all_to_all x1, blocking collectives, on_device(): low = lax.all_to_all(low, 'gx_0', 0, 0, tiled=True)  12.3 us
    all_to_all x1, blocking collectives, on_device(): edges = lax.all_to_all(edges, 'gz', 0, 0, tiled=True)  12.2 us
    pallas_call x4, Pallas kernels, on_core(): pl.pallas_call(kernel, out_shape=shape, in_specs=[space] * len(args), out...  9.19 us
    ppermute x2, starting transfers between devices, exchange(): lax.ppermute(second, axis, others)  8.14 us
    ppermute x2, waiting for transfers between devices, exchange(): lax.ppermute(second, axis, others)  1.93 us
    ppermute x2, waiting for transfers between devices, exchange(): lax.ppermute(first, axis, swaps)  1.88 us
  transfers between devices with their start and end apart: 4, of which 2 were waited for; matrix products, arithmetic and copies ran while one was open for 0% of the time, Pallas kernels for 0%

profile of v12, /device:TPU:1, one launch (start us, length us, event | category | flops | bytes accessed | tf_op | source)
XLA Modules:
  0.0 73.9 jit_solution(11437612238253933034)
XLA Ops:
  0.6 1.2 %pack_z.1 = (f32[72,8,128]{2,1,0:T(8,128)S(1)}, f32[4,5,8,128]{3,2,1,0:T(8,128)S(1)}) custom-call(f32[8,8,128]{2,1,0:T(8,128)} %t_ref.1, f32[8,8,128]{2,1,0:T(8,128)} %d_ref.1, f32[3,8,8,128]{3,2,1,0:T(8,128)} %b_ref.1, f32[3,8,8,128]{3,2,1,0:T(8,128)} %v_ref.1, f32[8,8,128]{2,1,0:T(8,128)} %r_ref.1), custom_call_target="tpu_custom_call" | custom-call | tf_op jit(solution)/shard_map/pack_z/pallas_call | solution.py:507
  1.8 12.2 %all_to_all.15.z_ref = f32[4,5,8,128]{3,2,1,0:T(8,128)S(1)} all-to-all(f32[4,5,8,128]{3,2,1,0:T(8,128)S(1)} %get-tuple-element.13), channel_id=1, replica_groups=mesh['gx_0'=3,'gx_1'=8,'gx_2'=2,'gy'=4,'gz'=4] {'gz'}, dimensions={0} | all-to-all | bytes 163840 | tf_op jit(solution)/shard_map/all_to_all | solution.py:528
  14.1 0.5 pack_x.1
  14.6 5.2 %collective-permute-start.1 = (f32[54,8,128]{2,1,0:T(8,128)S(1)}, f32[54,8,128]{2,1,0:T(8,128)S(1)}, u32[]{:S(2)}, u32[]{:S(2)}) collective-permute-start(f32[54,8,128]{2,1,0:T(8,128)S(1)} %get-tuple-element.16), channel_id=1, source_target_pairs={{16,32},{48,64},{80,96},{112,128},{144,160},{176,192},{208,224},{2... | collective-permute-start | bytes 663560 | tf_op jit(solution)/shard_map/ppermute | solution.py:499
  19.8 11.6 %collective-permute-start = (f32[54,8,128]{2,1,0:T(8,128)S(1)}, f32[54,8,128]{2,1,0:T(8,128)S(1)}, u32[]{:S(2)}, u32[]{:S(2)}) collective-permute-start(f32[54,8,128]{2,1,0:T(8,128)S(1)} %get-tuple-element.14.own_ref), channel_id=1, source_target_pairs={{0,16},{32,48},{64,80},{96,112},{128,144},{160,176},{192,208},{224... | collective-permute-start | bytes 663560 | tf_op jit(solution)/shard_map/ppermute | solution.py:499
  31.4 14.0 %all_to_all.16.min_ref = f32[64,1,128]{2,1,0:T(1,128)S(1)} all-to-all(f32[64,1,128]{2,1,0:T(1,128)S(1)} %get-tuple-element.17), channel_id=1, replica_groups=mesh['gx_0'=3,'gx_1'=8,'gx_2'=2,'gy'=4,'gz'=4] {'gx_1','gx_2','gy'}, dimensions={0} | all-to-all | bytes 65536 | tf_op jit(solution)/shard_map/all_to_all | solution.py:533
  45.4 0.0 collective-permute-done.1.xo_ref
  45.4 0.0 collective-permute-done.xa_ref
  45.4 0.4 pack_y.1
  45.8 2.9 %collective-permute-start.3 = (f32[168,8,128]{2,1,0:T(8,128)S(1)}, f32[168,8,128]{2,1,0:T(8,128)S(1)}, u32[]{:S(2)}, u32[]{:S(2)}) collective-permute-start(f32[168,8,128]{2,1,0:T(8,128)S(1)} %get-tuple-element.20), channel_id=1, source_target_pairs={{4,8},{12,0},{8,4},{0,12},{5,9},{13,1},{9,5},{1,13},{6,10},{14,2},... | collective-permute-start | bytes 2064392 | tf_op jit(solution)/shard_map/ppermute | solution.py:499
  48.8 1.9 %collective-permute-start.2 = (f32[168,8,128]{2,1,0:T(8,128)S(1)}, f32[168,8,128]{2,1,0:T(8,128)S(1)}, u32[]{:S(2)}, u32[]{:S(2)}) collective-permute-start(f32[168,8,128]{2,1,0:T(8,128)S(1)} %get-tuple-element.18.own_ref), channel_id=1, source_target_pairs={{0,4},{8,12},{4,0},{12,8},{1,5},{9,13},{5,1},{13,9},{2,6},{10,14},... | collective-permute-start | bytes 2064392 | tf_op jit(solution)/shard_map/ppermute | solution.py:499
  50.7 12.3 %all_to_all.17.low_ref = f32[3,1,128]{2,1,0:T(1,128)S(1)} all-to-all(f32[3,1,128]{2,1,0:T(1,128)S(1)} %get-tuple-element.21), channel_id=1, replica_groups=mesh['gx_0'=3,'gx_1'=8,'gx_2'=2,'gy'=4,'gz'=4] {'gx_0'}, dimensions={0} | all-to-all | bytes 3072 | tf_op jit(solution)/shard_map/all_to_all | solution.py:538
  63.0 1.9 %collective-permute-done.3.yo_ref = f32[168,8,128]{2,1,0:T(8,128)S(1)} collective-permute-done((f32[168,8,128]{2,1,0:T(8,128)S(1)}, f32[168,8,128]{2,1,0:T(8,128)S(1)}, u32[]{:S(2)}, u32[]{:S(2)}) %collective-permute-start.3) | collective-permute-done | bytes 688160 | tf_op jit(solution)/shard_map/ppermute | solution.py:499
  65.0 1.9 %collective-permute-done.2.ya_ref = f32[168,8,128]{2,1,0:T(8,128)S(1)} collective-permute-done((f32[168,8,128]{2,1,0:T(8,128)S(1)}, f32[168,8,128]{2,1,0:T(8,128)S(1)}, u32[]{:S(2)}, u32[]{:S(2)}) %collective-permute-start.2) | collective-permute-done | bytes 688160 | tf_op jit(solution)/shard_map/ppermute | solution.py:499
  66.8 7.0 %advance.1 = (f32[8,8,128]{2,1,0:T(8,128)}, f32[3,8,8,128]{3,2,1,0:T(8,128)}) custom-call(f32[168,8,128]{2,1,0:T(8,128)S(1)} %get-tuple-element.18.own_ref, f32[72,8,128]{2,1,0:T(8,128)S(1)} %get-tuple-element.19.aux_ref, f32[168,8,128]{2,1,0:T(8,128)S(1)} %collective-permute-done.2.ya_ref, f32[168,8,128]{2,1,0:T(8,128)S(1)} %collective-permute-done.3.yo_ref, ...), custom_call_target="tpu_custom_call" | custom-call | tf_op jit(solution)/shard_map/advance/pallas_call | solution.py:507
Async XLA Ops:
  14.6 30.8 %collective-permute-start.1 = (f32[54,8,128]{2,1,0:T(8,128)S(1)}, f32[54,8,128]{2,1,0:T(8,128)S(1)}, u32[]{:S(2)}, u32[]{:S(2)}) collective-permute-start(f32[54,8,128]{2,1,0:T(8,128)S(1)} %get-tuple-element.16), channel_id=1, source_target_pairs={{16,32},{48,64},{80,96},{112,128},{144,160},{176,192},{208,224},{2... | collective-permute-start | bytes 663560 | tf_op jit(solution)/shard_map/ppermute | solution.py:499
  19.8 25.6 %collective-permute-start = (f32[54,8,128]{2,1,0:T(8,128)S(1)}, f32[54,8,128]{2,1,0:T(8,128)S(1)}, u32[]{:S(2)}, u32[]{:S(2)}) collective-permute-start(f32[54,8,128]{2,1,0:T(8,128)S(1)} %get-tuple-element.14.own_ref), channel_id=1, source_target_pairs={{0,16},{32,48},{64,80},{96,112},{128,144},{160,176},{192,208},{224... | collective-permute-start | bytes 663560 | tf_op jit(solution)/shard_map/ppermute | solution.py:499
  45.8 19.2 %collective-permute-start.3 = (f32[168,8,128]{2,1,0:T(8,128)S(1)}, f32[168,8,128]{2,1,0:T(8,128)S(1)}, u32[]{:S(2)}, u32[]{:S(2)}) collective-permute-start(f32[168,8,128]{2,1,0:T(8,128)S(1)} %get-tuple-element.20), channel_id=1, source_target_pairs={{4,8},{12,0},{8,4},{0,12},{5,9},{13,1},{9,5},{1,13},{6,10},{14,2},... | collective-permute-start | bytes 2064392 | tf_op jit(solution)/shard_map/ppermute | solution.py:499
  48.8 18.1 %collective-permute-start.2 = (f32[168,8,128]{2,1,0:T(8,128)S(1)}, f32[168,8,128]{2,1,0:T(8,128)S(1)}, u32[]{:S(2)}, u32[]{:S(2)}) collective-permute-start(f32[168,8,128]{2,1,0:T(8,128)S(1)} %get-tuple-element.18.own_ref), channel_id=1, source_target_pairs={{0,4},{8,12},{4,0},{12,8},{1,5},{9,13},{5,1},{13,9},{2,6},{10,14},... | collective-permute-start | bytes 2064392 | tf_op jit(solution)/shard_map/ppermute | solution.py:499
